TPU v7x, 8 devices: a whole 2x2x1 slice. The times are simulated.
8 devices in a mesh: dp: 1 (over z), x: 8 (over y, x, core).
Axes of the slice: x: 2, y: 2, z: 1, core: 2. Of those that a mesh axis runs over, the one named last changes fastest.
Arguments:
- start_pos: int32 [256], P('dp')
- hidden_in: bfloat16 [4, 256, 5120], P(None, ('dp', 'x'))
- k_cache: bfloat16 [256, 256, 8, 128], P('dp', None, 'x')
- v_cache: bfloat16 [256, 256, 8, 128], P('dp', None, 'x')
- attn_norm: bfloat16 [5120], replicated
- w_q: bfloat16 [5120, 5120], replicated
- w_k: bfloat16 [5120, 1024], replicated
- w_v: bfloat16 [5120, 1024], replicated
- q_norm: bfloat16 [128], replicated
- k_norm: bfloat16 [128], replicated
- w_o: bfloat16 [5120, 5120], replicated
- mlp_norm: bfloat16 [5120], replicated
- w_gate: bfloat16 [5120, 17408], replicated
- w_up: bfloat16 [5120, 17408], replicated
- w_down: bfloat16 [17408, 5120], replicated
Outputs:
- output 1: bfloat16 [4, 256, 5120], P(None, ('dp', 'x'))
- output 2: bfloat16 [256, 256, 8, 128], P(('dp', 'x'))
- output 3: bfloat16 [256, 256, 8, 128], P(('dp', 'x'))
All inputs are finite; a program needn't handle non-finite values.
Results may differ from a plain program's by a relative error of at most 0.0104501.
Values are sent between devices in bfloat16 or wider.
A program may use at most 2.75 GiB of HBM per device.

v0:
```python
import functools
import math

import jax
import jax.numpy as jnp
from jax import lax
from jax.experimental import pallas as pl
from jax.experimental.pallas import tpu as pltpu
from jax.sharding import PartitionSpec as P

EPS = 1e-6
THETA = 1000000.0


def rms_norm(values, gain_vec):
    values32 = values.astype(jnp.float32)
    inv_rms = lax.rsqrt(jnp.mean(values32 * values32, axis=-1, keepdims=True) + EPS)
    return values32 * inv_rms * gain_vec.astype(jnp.float32)


def rotary(values, positions):
    head_dim = values.shape[-1]
    half_dim = head_dim // 2
    inv_freq = jnp.power(THETA, -jnp.arange(half_dim, dtype=jnp.float32) * 2.0 / head_dim)
    angles = positions.astype(jnp.float32)[..., None, None] * inv_freq
    cos_part = jnp.cos(angles)
    sin_part = jnp.sin(angles)
    first_half = values[..., :half_dim]
    second_half = values[..., half_dim:]
    return jnp.concatenate([first_half * cos_part - second_half * sin_part, second_half * cos_part + first_half * sin_part], axis=-1)


def project(hidden, positions, attn_norm, w_q, w_k, w_v, q_norm, k_norm):
    n_steps, num_rows = hidden.shape[0], hidden.shape[1]
    head_dim = q_norm.shape[0]
    normed = rms_norm(hidden, attn_norm).astype(jnp.bfloat16)
    queries = jnp.einsum('sbd,de->sbe', normed, w_q, preferred_element_type=jnp.float32).reshape(n_steps, num_rows, -1, head_dim)
    keys_new = jnp.einsum('sbd,de->sbe', normed, w_k, preferred_element_type=jnp.float32).reshape(n_steps, num_rows, -1, head_dim)
    values_new = jnp.einsum('sbd,de->sbe', normed, w_v, preferred_element_type=jnp.float32).reshape(n_steps, num_rows, -1, head_dim)
    queries = rotary(rms_norm(queries, q_norm), positions).astype(jnp.bfloat16)
    keys_new = rotary(rms_norm(keys_new, k_norm), positions).astype(jnp.bfloat16)
    return queries, keys_new, values_new.astype(jnp.bfloat16)


def attend(queries, cache_k, cache_v, keys_new, values_new, start_pos):
    n_steps, num_rows, n_heads, head_dim = queries.shape
    num_slots, kv_local = cache_k.shape[1], cache_k.shape[2]
    grouped = queries.reshape(n_steps, num_rows, kv_local, n_heads // kv_local, head_dim)
    score_scale = head_dim ** -0.5
    old_scores = jnp.einsum('sbkgd,btkd->bkgst', grouped, cache_k, preferred_element_type=jnp.float32) * score_scale
    old_valid = (jnp.arange(num_slots)[None, :] < start_pos[:, None])[:, None, None, None, :]
    old_scores = jnp.where(old_valid, old_scores, -jnp.inf)
    new_scores = jnp.einsum('sbkgd,jbkd->bkgsj', grouped, keys_new, preferred_element_type=jnp.float32) * score_scale
    new_valid = jnp.arange(n_steps)[:, None] >= jnp.arange(n_steps)[None, :]
    new_scores = jnp.where(new_valid, new_scores, -jnp.inf)
    peak_score = jnp.maximum(jnp.max(old_scores, axis=-1, keepdims=True), jnp.max(new_scores, axis=-1, keepdims=True))
    old_weights = jnp.exp(old_scores - peak_score)
    new_weights = jnp.exp(new_scores - peak_score)
    weight_sum = jnp.sum(old_weights, axis=-1) + jnp.sum(new_weights, axis=-1)
    mixed_vals = jnp.einsum('bkgst,btkd->sbkgd', old_weights.astype(jnp.bfloat16), cache_v, preferred_element_type=jnp.float32)
    mixed_vals = mixed_vals + jnp.einsum('bkgsj,jbkd->sbkgd', new_weights.astype(jnp.bfloat16), values_new, preferred_element_type=jnp.float32)
    mixed_vals = mixed_vals / jnp.transpose(weight_sum, (3, 0, 1, 2))[..., None]
    return mixed_vals.astype(jnp.bfloat16).reshape(n_steps, num_rows, n_heads, head_dim)


def finish(hidden, attended, w_o, mlp_norm, w_gate, w_up, w_down):
    n_steps, num_rows = attended.shape[0], attended.shape[1]
    flat_attn = attended.reshape(n_steps, num_rows, -1)
    attn_out = jnp.einsum('sbe,ed->sbd', flat_attn, w_o, preferred_element_type=jnp.float32)
    residual = (hidden.astype(jnp.float32) + attn_out).astype(jnp.bfloat16)
    normed = rms_norm(residual, mlp_norm).astype(jnp.bfloat16)
    gate_val = jnp.einsum('sbd,df->sbf', normed, w_gate, preferred_element_type=jnp.float32)
    up_val = jnp.einsum('sbd,df->sbf', normed, w_up, preferred_element_type=jnp.float32)
    activated = (jax.nn.silu(gate_val) * up_val).astype(jnp.bfloat16)
    down_val = jnp.einsum('sbf,fd->sbd', activated, w_down, preferred_element_type=jnp.float32)
    return (residual.astype(jnp.float32) + down_val).astype(jnp.bfloat16)


ROW_PAD = 9
MERGE_ROWS = 4
K_CUTS = (8, 20, 32)
SWAP_ORDER = (2, 4, 3, 5, 6, 7, 1)


def cuts(num_rows, ends):
    ends = [num_rows * e // 32 for e in ends]
    return [(lo, hi - lo) for lo, hi in zip([0] + ends[:-1], ends)]


def merge_row(row_idx, block_refs, head_ids, fresh_ref, first_slot, out_ref, wide_ref):
    num_slots, n_dev = out_ref.shape[1], len(block_refs)
    for block_ref, head_idx in zip(block_refs, head_ids):
        wide_ref[pl.ds(head_idx, num_slots, stride=ROW_PAD), :] = block_ref[row_idx].astype(jnp.float32)
    for slot_idx in range(num_slots):
        out_ref[row_idx, slot_idx] = wide_ref[slot_idx * ROW_PAD:slot_idx * ROW_PAD + n_dev, :].astype(out_ref.dtype)
    for step_idx in range(fresh_ref.shape[0]):
        out_ref[row_idx, first_slot + step_idx] = fresh_ref[step_idx, row_idx]


def merge_chunk_kernel(row_base, n_dev, meta_ref, *refs):
    block_refs, fresh_ref, out_ref, wide_ref = refs[:n_dev], refs[n_dev], refs[-2], refs[-1]
    step_rows = out_ref.shape[0]
    head_ids = [meta_ref[rel_idx] for rel_idx in range(n_dev)]

    @pl.loop(0, step_rows)
    def _(row_idx):
        first_slot = meta_ref[n_dev + row_base + pl.program_id(0) * step_rows + row_idx]
        merge_row(row_idx, block_refs, head_ids, fresh_ref, first_slot, out_ref, wide_ref)


def merge_chunk(own, blocks, fresh_rows, meta, partial_out, row_base, num_rows):
    n_dev = len(blocks) + 1
    chunk_rows, num_slots, head_dim = blocks[0].shape
    n_steps = fresh_rows.shape[0]
    step_rows = math.gcd(math.gcd(chunk_rows, row_base), MERGE_ROWS)
    base = row_base // step_rows
    grid_spec = pltpu.PrefetchScalarGridSpec(
        num_scalar_prefetch=1,
        grid=(chunk_rows // step_rows,),
        in_specs=[pl.BlockSpec((step_rows, num_slots, head_dim), lambda b, meta: (meta[0] * (num_rows // step_rows) + base + b, 0, 0))]
        + [pl.BlockSpec((step_rows, num_slots, head_dim), lambda b, meta: (b, 0, 0))] * (n_dev - 1)
        + [pl.BlockSpec((n_steps, step_rows, n_dev, head_dim), lambda b, meta: (0, base + b, 0, 0))]
        + ([] if partial_out is None else [pl.BlockSpec(memory_space=pl.ANY)]),
        out_specs=pl.BlockSpec((step_rows, num_slots, n_dev, head_dim), lambda b, meta: (base + b, 0, 0, 0)),
        scratch_shapes=[pltpu.VMEM((num_slots * ROW_PAD, head_dim), jnp.float32)],
    )
    return pl.pallas_call(
        functools.partial(merge_chunk_kernel, row_base, n_dev),
        out_shape=jax.ShapeDtypeStruct((num_rows, num_slots, n_dev, head_dim), own.dtype),
        grid_spec=grid_spec,
        input_output_aliases={} if partial_out is None else {n_dev + 2: 0},
        cost_estimate=pl.CostEstimate(flops=10**8, bytes_accessed=4 * n_dev * blocks[0].size, transcendentals=0),
    )(meta, own, *blocks, fresh_rows, *(() if partial_out is None else (partial_out,)))


def merge_all_kernel(n_dev, meta_ref, blocks_ref, fresh_ref, out_ref, wide_ref):
    step_rows = out_ref.shape[0]

    @pl.loop(0, step_rows)
    def _(row_idx):
        first_slot = meta_ref[n_dev + pl.program_id(0) * step_rows + row_idx]
        merge_row(row_idx, [blocks_ref.at[h] for h in range(n_dev)], range(n_dev), fresh_ref, first_slot, out_ref, wide_ref)


def merge_all(blocks, fresh_rows, meta):
    n_dev, num_rows, num_slots, head_dim = blocks.shape
    n_steps = fresh_rows.shape[0]
    step_rows = math.gcd(num_rows, MERGE_ROWS)
    return pl.pallas_call(
        functools.partial(merge_all_kernel, n_dev),
        out_shape=jax.ShapeDtypeStruct((num_rows, num_slots, n_dev, head_dim), blocks.dtype),
        grid_spec=pltpu.PrefetchScalarGridSpec(
            num_scalar_prefetch=1,
            grid=(num_rows // step_rows,),
            in_specs=[
                pl.BlockSpec((n_dev, step_rows, num_slots, head_dim), lambda b, meta: (0, b, 0, 0)),
                pl.BlockSpec((n_steps, step_rows, n_dev, head_dim), lambda b, meta: (0, b, 0, 0)),
            ],
            out_specs=pl.BlockSpec((step_rows, num_slots, n_dev, head_dim), lambda b, meta: (b, 0, 0, 0)),
            scratch_shapes=[pltpu.VMEM((num_slots * ROW_PAD, head_dim), jnp.float32)],
        ),
        cost_estimate=pl.CostEstimate(flops=10**8, bytes_accessed=4 * blocks.size, transcendentals=0),
    )(meta, blocks, fresh_rows)


def solution(mesh):
    n_dev = mesh.shape['x']
    row_spec = P(None, ('dp', 'x'), None)
    cache_in = P('dp', None, 'x', None)
    cache_out = P(('dp', 'x'), None, None, None)

    def local_run(start_pos, hidden_in, k_heads, v_heads, attn_norm, w_q, w_k, w_v, q_norm, k_norm, w_o, mlp_norm, w_gate, w_up, w_down):
        n_steps, num_rows, _ = hidden_in.shape
        all_rows, num_slots, _, head_dim = k_heads.shape
        me = lax.axis_index('x')
        my_pos = lax.dynamic_slice_in_dim(start_pos, me * num_rows, num_rows)
        k_own, v_own = k_heads[:, :, 0], v_heads[:, :, 0]

        def swap(arr, rel_idx):
            return lax.ppermute(arr, 'x', [(d, d ^ rel_idx) for d in range(n_dev)])

        def swap_cache(own, row_base, chunk_rows):
            return [swap(lax.dynamic_slice_in_dim(own, jnp.bitwise_xor(me, rel_idx) * num_rows + row_base, chunk_rows), rel_idx) for rel_idx in SWAP_ORDER]

        cuts_k = cuts(num_rows, K_CUTS)
        k_got = [swap_cache(k_own, *c) for c in cuts_k]
        positions = my_pos[None, :] + jnp.arange(n_steps)[:, None]
        queries, keys_new, values_new = project(hidden_in, positions, attn_norm, w_q, w_k, w_v, q_norm, k_norm)
        group = queries.shape[2] // n_dev
        q_send = queries.reshape(n_steps, num_rows, n_dev, group, head_dim).transpose(2, 0, 3, 1, 4).reshape(n_dev, n_steps * group, num_rows, head_dim)
        k_send = keys_new.transpose(2, 0, 1, 3)
        v_send = values_new.transpose(2, 0, 1, 3)
        sent = jnp.concatenate([q_send, k_send, v_send], axis=1)
        got = jnp.zeros((n_steps * (group + 2), n_dev, num_rows, head_dim), sent.dtype)
        for rel_idx in range(n_dev):
            peer = jnp.bitwise_xor(me, rel_idx)
            part = lax.dynamic_index_in_dim(sent, peer, 0, keepdims=False)
            part = swap(part, rel_idx) if rel_idx else part
            got = lax.dynamic_update_slice_in_dim(got, part[:, None], peer, 1)
        got = got.reshape(n_steps * (group + 2), all_rows, head_dim)
        q_got = got[:n_steps * group].reshape(n_steps, group, all_rows, head_dim).transpose(0, 2, 1, 3)
        kn_got = got[n_steps * group:n_steps * (group + 1), :, None]
        vn_got = got[n_steps * (group + 1):, :, None]
        mixed = attend(q_got, k_heads, v_heads, kn_got, vn_got, start_pos)
        mixed = mixed.reshape(n_steps, n_dev, num_rows, group, head_dim).transpose(1, 0, 3, 2, 4)
        v_got = lax.all_to_all(v_own, 'x', 0, 0, tiled=True).reshape(n_dev, num_rows, num_slots, head_dim)
        back = jnp.zeros_like(mixed)
        for rel_idx in range(n_dev):
            peer = jnp.bitwise_xor(me, rel_idx)
            part = lax.dynamic_index_in_dim(mixed, peer, 0)
            part = swap(part, rel_idx) if rel_idx else part
            back = lax.dynamic_update_slice_in_dim(back, part, peer, 0)
        attended = back.transpose(1, 3, 0, 2, 4).reshape(n_steps, num_rows, n_dev * group, head_dim)
        out_hidden = finish(hidden_in, attended, w_o, mlp_norm, w_gate, w_up, w_down)
        meta = jnp.concatenate([jnp.bitwise_xor(me, jnp.array((0,) + SWAP_ORDER)), my_pos]).astype(jnp.int32)
        k_out, v_out = None, merge_all(v_got, values_new, meta)
        for chunk_idx, ((row_base, chunk_rows), k_blocks) in enumerate(zip(cuts_k, k_got)):
            if chunk_idx == len(cuts_k) - 1:
                meta, v_out = lax.optimization_barrier((meta, v_out))
            k_out = merge_chunk(k_own, k_blocks, keys_new, meta, k_out, row_base, num_rows)
        return out_hidden, k_out, v_out

    return jax.shard_map(local_run, mesh=mesh, in_specs=(P('dp'), row_spec, cache_in, cache_in) + (P(),) * 11, out_specs=(row_spec, cache_out, cache_out), check_vma=False)
```

profile of v0, /device:TPU:0, one launch (start us, length us, event | category | flops | bytes accessed | tf_op | source)
XLA Modules:
  0.0 586.9 jit_solution(14277897672838668171)
XLA Ops:
  0.7 3.9 dynamic-slice_bitcast_fusion.14
  4.6 3.3 collective-permute-start.28
  7.9 1.5 collective-permute-start.29
  9.4 4.6 all-to-all-start
  14.6 5.6 fusion.24
  20.5 5.5 fusion.82
  27.8 18.2 %fusion.8 = f32[4,32,5120]{2,1,0:T(8,128)S(1)} fusion(bf16[5120,5120]{1,0:T(8,128)(2,1)} %param.21, bf16[4,32,5120]{2,1,0:T(8,128)(2,1)S(1)} %copy-done, f32[5120]{0:T(1024)S(1)} %convert_element_type.61, f32[4,32]{1,0:T(4,128)S(1)} %add_rsqrt_fusion.3), kind=kOutput, calls=%fused_computation.8 | convolution fusion | flops 6713507840 | bytes 56381952 | tf_op jit(solution)/shard_map/sbd,de->sbe/dot_general | solution.py:37
  46.5 1.0 copy-done.1
  48.4 2.3 fusion.66
  50.7 0.9 subtract_convert_fusion
  52.4 1.4 copy.48
  54.5 1.6 pad_maximum_fusion
  56.2 1.2 dynamic-slice_bitcast_fusion.21
  57.9 1.5 collective-permute-start.1
  60.1 8.4 %dynamic-slice_bitcast_fusion = (bf16[12,256,128]{2,1,0:T(8,128)(2,1)}, bf16[12,256,128]{2,1,0:T(8,128)(2,1)}, bf16[12,256,128]{2,1,0:T(8,128)(2,1)}, bf16[12,25...) fusion(bf16[256,256,1,128]{3,1,2,0:T(8,128)(2,1)} %param.18, ...), kind=kLoop, calls=%fused_computation.76 | loop fusion | bytes 22020152 | tf_op jit(solution)/shard_map/dynamic_slice | solution.py:183
  69.3 1.0 bitcast_dynamic-update-slice_fusion.6
  70.3 146.6 %collective-permute-done.1 = bf16[28,32,128]{2,1,0:T(8,128)(2,1)} collective-permute-done((bf16[28,32,128]{2,1,0:T(8,128)(2,1)}, bf16[28,32,128]{2,1,0:T(8,128)(2,1)}, u32[]{:S(2)}, u32[]{:S(2)}) %collective-permute-start.1) | collective-permute-done | bytes 229408 | tf_op jit(solution)/shard_map/ppermute | solution.py:180
  216.9 2.1 collective-permute-start.3
  219.0 1.0 bitcast_dynamic-update-slice_fusion.5
  220.2 2.2 collective-permute-start.4
  223.0 3.5 collective-permute-start.5
  226.5 6.4 %collective-permute-done.4 = bf16[28,32,128]{2,1,0:T(8,128)(2,1)S(1)} collective-permute-done((bf16[28,32,128]{2,1,0:T(8,128)(2,1)S(1)}, bf16[28,32,128]{2,1,0:T(8,128)(2,1)S(1)}, u32[]{:S(2)}, u32[]{:S(2)}) %collective-permute-start.4) | collective-permute-done | bytes 229408 | tf_op jit(solution)/shard_map/ppermute | solution.py:180
  232.9 2.3 collective-permute-start.6
  235.3 5.8 collective-permute-done.6
  242.4 12.1 %fusion.34 = (f32[256,5,4]{1,2,0:T(4,128)S(1)}, f32[256,4,5,256]{3,2,1,0:T(8,128)}) fusion(pred[256,256]{1,0:T(8,128)(4,1)S(1)} %iota_compare_fusion, bf16[256,256,1,128]{3,1,2,0:T(8,128)(2,1)} %param.18, bf16[4,5,256,128]{3,2,1,0:T(8,128)(2,1)S(1)} %bitcast.290), kind=kOutput, calls=%fused_computation.30 | convolution fusion | flops 339471360 | bytes 23416832 | tf_op jit(solution)/shard_map/sbkgd,btkd->bkgst/dot_general | solution.py:50
  254.4 9.7 %fusion.98 = (f32[256,5,4]{1,2,0:T(4,128)S(1)}, f32[256,1,5,4,4]{2,4,3,0,1:T(4,128)S(1)}) fusion(bf16[4,256,128,1]{2,0,3,1:T(4,128)(2,1)S(1)} %bitcast.311, bf16[4,5,256,128]{3,2,1,0:T(8,128)(2,1)S(1)} %bitcast.291, pred[4,4]{1,0:T(4,128)(4,1)S(1)} %iota_compare_fusion.1), kind=kOutput, calls=%fused_computation.161 | convolution fusion | flops 5299200 | bytes 1675280 | tf_op jit(solution)/shard_map/sbkgd,jbkd->bkgsj/dot_general | solution.py:53
  264.3 6.0 %fusion.32 = f32[256,5,4]{1,2,0:T(4,128)S(1)} fusion(f32[256,4,5,256]{3,2,1,0:T(8,128)} %get-tuple-element.52, f32[256,5,4]{1,2,0:T(4,128)S(1)} %max.8, pred[256,256]{1,0:T(8,128)(4,1)S(1)} %iota_compare_fusion), kind=kLoop, calls=%fused_computation.28 | loop fusion | flops 5237760 | bytes 5349376 | tf_op jit(solution)/shard_map/reduce_sum | solution.py:59
  270.4 8.4 %fusion.18 = f32[256,5,4,128]{3,1,2,0:T(8,128)S(1)} fusion(bf16[256,256,1,128]{3,1,2,0:T(8,128)(2,1)} %param.19, f32[256,4,5,256]{3,2,1,0:T(8,128)S(1)} %bitcast.287, f32[256,5,4]{1,2,0:T(4,128)S(1)} %max.8, pred[256,256]{1,0:T(8,128)(4,1)S(1)} %iota_compare_fusion), kind=kOutput, calls=%fused_computation.12 | convolution fusion | flops 340787200 | bytes 24727552 | tf_op jit(solution)/shard_map/bkgst,btkd->sbkgd/dot_general | solution.py:60
  278.7 1.9 fusion.74
  281.0 2.4 fusion.57
  284.4 1.3 collective-permute-start.8
  286.9 6.6 %collective-permute-done.8 = bf16[1,4,5,32,128]{4,2,0,3,1:T(8,128)(2,1)S(1)} collective-permute-done((bf16[1,4,5,32,128]{4,2,0,3,1:T(8,128)(2,1)S(1)}, bf16[1,4,5,32,128]{4,2,0,3,1:T(8,128)(2,1)S(1)}, u32[]{:S(2)}, u32[]{:S(2)}) %collective-permute-start.8) | collective-permute-done | bytes 163872 | tf_op jit(solution)/shard_map/ppermute | solution.py:180
  293.6 1.0 collective-permute-start.10
  294.7 2.9 collective-permute-done.9
  297.5 1.4 collective-permute-start.11
  299.1 1.2 collective-permute-done.10
  300.2 1.7 collective-permute-start.12
  302.1 8.6 %collective-permute-done.11 = bf16[1,4,5,32,128]{4,2,0,3,1:T(8,128)(2,1)S(1)} collective-permute-done((bf16[1,4,5,32,128]{4,2,0,3,1:T(8,128)(2,1)S(1)}, bf16[1,4,5,32,128]{4,2,0,3,1:T(8,128)(2,1)S(1)}, u32[]{:S(2)}, u32[]{:S(2)}) %collective-permute-start.11) | collective-permute-done | bytes 163872 | tf_op jit(solution)/shard_map/ppermute | solution.py:180
  310.6 2.3 collective-permute-start.13
  313.3 5.8 collective-permute-done.13
  319.1 1.5 collective-permute-start.32
  320.7 2.3 reshape_reshape.7
  323.0 1.7 collective-permute-start.33
  324.7 20.8 %multiply_reduce_fusion = (f32[4,32]{1,0:T(4,128)S(1)}, f32[4,32,5120]{2,1,0:T(8,128)}) fusion(bf16[4,32,5120]{2,1,0:T(8,128)(2,1)} %reshape_reshape.7, bf16[5120,5120]{1,0:T(8,128)(2,1)} %param.26, bf16[4,32,5120]{2,1,0:T(8,128)(2,1)S(1)} %copy-done), kind=kOutput, calls=%fused_computation.55 | convolution fusion | flops 6714818560 | bytes 57672192 | tf_op jit(solution)/shard_map/sbe,ed->sbd/dot_general | solution.py:69
  345.5 1.3 collective-permute-start.21
  346.8 7.1 %collective-permute-done.31.refs_4_ = bf16[8,256,128]{2,1,0:T(8,128)(2,1)} collective-permute-done((bf16[8,256,128]{2,1,0:T(8,128)(2,1)}, bf16[8,256,128]{2,1,0:T(8,128)(2,1)}, u32[]{:S(2)}, u32[]{:S(2)}) %collective-permute-start.31) | collective-permute-done | bytes 524320 | tf_op jit(solution)/shard_map/ppermute | solution.py:180
  353.9 0.8 collective-permute-start.22
  355.5 1.4 collective-permute-start.24
  356.9 64.3 %fusion.4 = f32[4,32,17408]{2,1,0:T(8,128)} fusion(bf16[5120,17408]{1,0:T(8,128)(2,1)} %param.28, f32[4,32,5120]{2,1,0:T(8,128)} %get-tuple-element.56, f32[5120]{0:T(1024)S(1)} %convert_element_type.73, f32[4,32]{1,0:T(4,128)S(1)} %add_rsqrt_fusion.2), kind=kOutput, calls=%fused_computation.4 | convolution fusion | flops 22818979840 | bytes 189813248 | tf_op jit(solution)/shard_map/sbd,df->sbf/dot_general | solution.py:72
  421.2 1.0 collective-permute-start.25
  422.3 1.0 collective-permute-start.26
  423.3 1.0 collective-permute-start.27
  424.3 0.8 collective-permute-start.14
  425.1 0.8 collective-permute-start.15
  425.9 60.5 %fusion.13.clone.8 = bf16[4,32,17408]{2,1,0:T(8,128)(2,1)} fusion(bf16[5120,17408]{1,0:T(8,128)(2,1)} %param.29, f32[4,32,17408]{2,1,0:T(8,128)} %fusion.4, f32[4,32,5120]{2,1,0:T(8,128)S(1)} %copy-done.2, f32[5120]{0:T(1024)S(1)} %convert_element_type.73, f32[4,32]{1,0:T(4,128)S(1)} %add_rsqrt_fusion.2), kind=kOutput, calls=%fused_computation.11.clone.clone.clone.clone.clone.clone.clone.1 | convolution fusion | flops 22832349184 | bytes 194269696 | tf_op jit(solution)/shard_map/sbd,df->sbf/dot_general | solution.py:73
  486.7 1.8 collective-permute-start.17
  488.5 1.0 collective-permute-start.18
  490.2 1.3 collective-permute-start.20
  491.6 58.1 %fusion.49 = bf16[4,32,5120]{2,1,0:T(8,128)(2,1)} fusion(f32[4,32,5120]{2,1,0:T(8,128)S(1)} %copy-done.2, bf16[17408,5120]{1,0:T(8,128)(2,1)} %param.30, bf16[4,32,17408]{2,1,0:T(8,128)(2,1)} %fusion.13.clone.8), kind=kOutput, calls=%fused_computation.35 | convolution fusion | flops 22818324480 | bytes 186646528 | tf_op jit(solution)/shard_map/sbf,fd->sbd/dot_general | solution.py:75
  549.7 4.8 shard_map.176.refs_9_
  554.4 7.7 %shard_map.177.refs_9_ = bf16[32,256,8,128]{3,2,1,0:T(8,128)(2,1)} custom-call(s32[40]{0:T(128)} %pad_add_fusion.meta_ref, bf16[256,256,128]{2,1,0:T(8,128)(2,1)} %bitcast.284, bf16[12,256,128]{2,1,0:T(8,128)(2,1)} %collective-permute-done.21.refs_1_, bf16[12,256,128]{2,1,0:T(8,128)(2,1)} %collective-permute-done.22.refs_2_, ...), custom_call_target="tpu_custom_call", output_to_operand_aliasing={{}: (10, {})} | custom-call | flops 100000000 | bytes 12582912 | tf_op jit(solution)/shard_map/pallas_call | solution.py:127
  562.1 15.9 %shard_map.175 = bf16[32,256,8,128]{3,2,1,0:T(8,128)(2,1)} custom-call(s32[40]{0:T(128)} %pad_add_fusion.meta_ref, bf16[8,32,256,128]{3,2,1,0:T(8,128)(2,1)} %bitcast.65.blocks_ref, bf16[4,32,8,128]{3,2,1,0:T(8,128)(2,1)} %bitcast.301), custom_call_target="tpu_custom_call" | custom-call | flops 100000000 | bytes 33554432 | tf_op jit(solution)/shard_map/pallas_call | solution.py:149
  578.1 0.8 copy-done.6
  579.0 7.7 %shard_map.178 = bf16[32,256,8,128]{3,2,1,0:T(8,128)(2,1)} custom-call(s32[40]{0:T(128)} %pad_add_fusion.meta_ref, bf16[256,256,128]{2,1,0:T(8,128)(2,1)} %bitcast.285, bf16[12,256,128]{2,1,0:T(8,128)(2,1)} %collective-permute-done.14.refs_1_, bf16[12,256,128]{2,1,0:T(8,128)(2,1)} %collective-permute-done.15.refs_2_, ...), custom_call_target="tpu_custom_call", output_to_operand_aliasing={{}: (10, {})} | custom-call | flops 100000000 | bytes 12582912 | tf_op jit(solution)/shard_map/pallas_call | solution.py:127
  (136 shorter events, 14.6 us)
Async XLA Ops:
  4.6 318.4 %collective-permute-start.28 = (bf16[8,256,128]{2,1,0:T(8,128)(2,1)}, bf16[8,256,128]{2,1,0:T(8,128)(2,1)}, u32[]{:S(2)}, u32[]{:S(2)}) collective-permute-start(bf16[8,256,128]{2,1,0:T(8,128)(2,1)} %get-tuple-element.12), channel_id=1, source_target_pairs={{0,2},{1,3},{2,0},{3,1},{4,6},{5,7},{6,4},{7,5}} | collective-permute-start | bytes 1572872 | tf_op jit(solution)/shard_map/ppermute | solution.py:180
  7.9 337.6 %collective-permute-start.29 = (bf16[8,256,128]{2,1,0:T(8,128)(2,1)}, bf16[8,256,128]{2,1,0:T(8,128)(2,1)}, u32[]{:S(2)}, u32[]{:S(2)}) collective-permute-start(bf16[8,256,128]{2,1,0:T(8,128)(2,1)} %get-tuple-element.11), channel_id=1, source_target_pairs={{0,4},{1,5},{2,6},{3,7},{4,0},{5,1},{6,2},{7,3}} | collective-permute-start | bytes 1572872 | tf_op jit(solution)/shard_map/ppermute | solution.py:180
  9.4 336.1 %collective-permute-start.30 = (bf16[8,256,128]{2,1,0:T(8,128)(2,1)}, bf16[8,256,128]{2,1,0:T(8,128)(2,1)}, u32[]{:S(2)}, u32[]{:S(2)}) collective-permute-start(bf16[8,256,128]{2,1,0:T(8,128)(2,1)} %get-tuple-element.10), channel_id=1, source_target_pairs={{0,3},{1,2},{2,1},{3,0},{4,7},{5,6},{6,5},{7,4}} | collective-permute-start | bytes 1572872 | tf_op jit(solution)/shard_map/ppermute | solution.py:180
  9.4 4.7 copy-start.14
  9.4 4.8 copy-start.12
  9.4 4.8 copy-start
  9.4 552.7 %all-to-all-start = ((bf16[256,256,128]{2,1,0:T(8,128)(2,1)}), bf16[256,256,128]{2,1,0:T(8,128)(2,1)}, u32[]{:S(2)}, u32[]{:S(2)}) async-start(bf16[256,256,128]{2,1,0:T(8,128)(2,1)} %bitcast.288), calls=%async_computation | async-start | bytes 33554432 | tf_op jit(solution)/shard_map/all_to_all | solution.py:206
  14.6 5.9 %copy-start.15 = (bf16[128]{0:T(256)(128)(2,1)S(1)}, bf16[128]{0:T(256)(128)(2,1)}, u32[]{:S(2)}) copy-start(bf16[128]{0:T(256)(128)(2,1)} %param.25) | copy-start | bytes 772
  26.1 27.6 %copy-start.4 = (bf16[16,8,8,128]{3,2,1,0:T(8,128)(2,1)}, bf16[16,8,8,128]{3,2,1,0:T(8,128)(2,1)S(1)}, u32[]{:S(2)}) copy-start(bf16[16,8,8,128]{3,2,1,0:T(8,128)(2,1)S(1)} %copy.77) | copy-start | bytes 786436
  27.1 0.7 copy-start.3
  46.0 1.5 copy-start.1
  47.5 0.9 copy-start.16
  54.5 4.9 copy-start.17
  57.4 11.9 %collective-permute-start = (bf16[28,32,128]{2,1,0:T(8,128)(2,1)}, bf16[28,32,128]{2,1,0:T(8,128)(2,1)}, u32[]{:S(2)}, u32[]{:S(2)}) collective-permute-start(bf16[28,32,128]{2,1,0:T(8,128)(2,1)} %get-tuple-element.46), channel_id=1, source_target_pairs={{0,1},{1,0},{2,3},{3,2},{4,5},{5,4},{6,7},{7,6}} | collective-permute-start | bytes 688136 | tf_op jit(solution)/shard_map/ppermute | solution.py:180
  57.9 159.0 %collective-permute-start.1 = (bf16[28,32,128]{2,1,0:T(8,128)(2,1)}, bf16[28,32,128]{2,1,0:T(8,128)(2,1)}, u32[]{:S(2)}, u32[]{:S(2)}) collective-permute-start(bf16[28,32,128]{2,1,0:T(8,128)(2,1)} %get-tuple-element.45), channel_id=1, source_target_pairs={{0,2},{1,3},{2,0},{3,1},{4,6},{5,7},{6,4},{7,5}} | collective-permute-start | bytes 688136 | tf_op jit(solution)/shard_map/ppermute | solution.py:180
  60.0 9.1 %copy-start.13 = (bf16[5120]{0:T(1024)(128)(2,1)S(1)}, bf16[5120]{0:T(1024)(128)(2,1)}, u32[]{:S(2)}) copy-start(bf16[5120]{0:T(1024)(128)(2,1)} %param.27) | copy-start | bytes 30724
  60.0 9.2 %copy-start.11 = (bf16[28,32,128]{2,1,0:T(8,128)(2,1)S(1)}, bf16[28,32,128]{2,1,0:T(8,128)(2,1)}, u32[]{:S(2)}) copy-start(bf16[28,32,128]{2,1,0:T(8,128)(2,1)} %get-tuple-element.44) | copy-start | bytes 688132
  60.0 156.9 %copy-start.10 = (bf16[28,32,128]{2,1,0:T(8,128)(2,1)S(1)}, bf16[28,32,128]{2,1,0:T(8,128)(2,1)}, u32[]{:S(2)}) copy-start(bf16[28,32,128]{2,1,0:T(8,128)(2,1)} %get-tuple-element.43) | copy-start | bytes 688132
  60.1 160.1 %copy-start.9 = (bf16[28,32,128]{2,1,0:T(8,128)(2,1)S(1)}, bf16[28,32,128]{2,1,0:T(8,128)(2,1)}, u32[]{:S(2)}) copy-start(bf16[28,32,128]{2,1,0:T(8,128)(2,1)} %get-tuple-element.42) | copy-start | bytes 688132
  60.1 162.9 %copy-start.8 = (bf16[28,32,128]{2,1,0:T(8,128)(2,1)S(1)}, bf16[28,32,128]{2,1,0:T(8,128)(2,1)}, u32[]{:S(2)}) copy-start(bf16[28,32,128]{2,1,0:T(8,128)(2,1)} %get-tuple-element.41) | copy-start | bytes 688132
  69.3 150.9 %collective-permute-start.2 = (bf16[28,32,128]{2,1,0:T(8,128)(2,1)S(1)}, bf16[28,32,128]{2,1,0:T(8,128)(2,1)S(1)}, u32[]{:S(2)}, u32[]{:S(2)}) collective-permute-start(bf16[28,32,128]{2,1,0:T(8,128)(2,1)S(1)} %copy-done.11), channel_id=1, source_target_pairs={{0,3},{1,2},{2,1},{3,0},{4,7},{5,6},{6,5},{7,4}} | collective-permute-start | bytes 688136 | tf_op jit(solution)/shard_map/ppermute | solution.py:180
  216.9 6.1 %collective-permute-start.3 = (bf16[28,32,128]{2,1,0:T(8,128)(2,1)S(1)}, bf16[28,32,128]{2,1,0:T(8,128)(2,1)S(1)}, u32[]{:S(2)}, u32[]{:S(2)}) collective-permute-start(bf16[28,32,128]{2,1,0:T(8,128)(2,1)S(1)} %copy-done.10), channel_id=1, source_target_pairs={{0,4},{1,5},{2,6},{3,7},{4,0},{5,1},{6,2},{7,3}} | collective-permute-start | bytes 688136 | tf_op jit(solution)/shard_map/ppermute | solution.py:180
  220.2 12.7 %collective-permute-start.4 = (bf16[28,32,128]{2,1,0:T(8,128)(2,1)S(1)}, bf16[28,32,128]{2,1,0:T(8,128)(2,1)S(1)}, u32[]{:S(2)}, u32[]{:S(2)}) collective-permute-start(bf16[28,32,128]{2,1,0:T(8,128)(2,1)S(1)} %copy-done.9), channel_id=1, source_target_pairs={{0,5},{1,4},{2,7},{3,6},{4,1},{5,0},{6,3},{7,2}} | collective-permute-start | bytes 688136 | tf_op jit(solution)/shard_map/ppermute | solution.py:180
  223.0 12.3 %collective-permute-start.5 = (bf16[28,32,128]{2,1,0:T(8,128)(2,1)S(1)}, bf16[28,32,128]{2,1,0:T(8,128)(2,1)S(1)}, u32[]{:S(2)}, u32[]{:S(2)}) collective-permute-start(bf16[28,32,128]{2,1,0:T(8,128)(2,1)S(1)} %copy-done.8), channel_id=1, source_target_pairs={{0,6},{1,7},{2,4},{3,5},{4,2},{5,3},{6,0},{7,1}} | collective-permute-start | bytes 688136 | tf_op jit(solution)/shard_map/ppermute | solution.py:180
  232.9 8.3 %collective-permute-start.6 = (bf16[28,32,128]{2,1,0:T(8,128)(2,1)S(1)}, bf16[28,32,128]{2,1,0:T(8,128)(2,1)S(1)}, u32[]{:S(2)}, u32[]{:S(2)}) collective-permute-start(bf16[28,32,128]{2,1,0:T(8,128)(2,1)S(1)} %get-tuple-element.40), channel_id=1, source_target_pairs={{0,7},{1,6},{2,5},{3,4},{4,3},{5,2},{6,1},{7,0}} | collective-permute-start | bytes 688136 | tf_op jit(solution)/shard_map/ppermute | solution.py:180
  254.4 15.9 %slice-start = ((s8[8388608]{0:T(1024)(128)(4,1)}), s8[4194304]{0:T(1024)(128)(4,1)S(1)}, s32[]{:S(2)}) async-start(s8[8388608]{0:T(1024)(128)(4,1)} %bitcast.286), calls=%async_computation.1 | async-start | bytes 8388608
  264.3 6.0 %slice-start.1 = ((s8[8388608]{0:T(1024)(128)(4,1)}), s8[4194304]{0:T(1024)(128)(4,1)S(1)}, s32[]{:S(2)}) async-start(s8[8388608]{0:T(1024)(128)(4,1)} %bitcast.286), calls=%async_computation.2 | async-start | bytes 8388608
  278.7 1.9 copy-start.5
  283.9 2.7 collective-permute-start.7
  284.4 9.2 %collective-permute-start.8 = (bf16[1,4,5,32,128]{4,2,0,3,1:T(8,128)(2,1)S(1)}, bf16[1,4,5,32,128]{4,2,0,3,1:T(8,128)(2,1)S(1)}, u32[]{:S(2)}, u32[]{:S(2)}) collective-permute-start(bf16[1,4,5,32,128]{4,2,0,3,1:T(8,128)(2,1)S(1)} %bitcast.308), channel_id=1, source_target_pairs={{0,2},{1,3},{2,0},{3,1},{4,6},{5,7},{6,4},{7,5}} | collective-permute-start | bytes 491528 | tf_op jit(solution)/shard_map/ppermute | solution.py:180
  286.6 10.9 %collective-permute-start.9 = (bf16[1,4,5,32,128]{4,2,0,3,1:T(8,128)(2,1)S(1)}, bf16[1,4,5,32,128]{4,2,0,3,1:T(8,128)(2,1)S(1)}, u32[]{:S(2)}, u32[]{:S(2)}) collective-permute-start(bf16[1,4,5,32,128]{4,2,0,3,1:T(8,128)(2,1)S(1)} %bitcast.309), channel_id=1, source_target_pairs={{0,3},{1,2},{2,1},{3,0},{4,7},{5,6},{6,5},{7,4}} | collective-permute-start | bytes 491528 | tf_op jit(solution)/shard_map/ppermute | solution.py:180
  293.6 6.7 %collective-permute-start.10 = (bf16[1,4,5,32,128]{4,2,0,3,1:T(8,128)(2,1)S(1)}, bf16[1,4,5,32,128]{4,2,0,3,1:T(8,128)(2,1)S(1)}, u32[]{:S(2)}, u32[]{:S(2)}) collective-permute-start(bf16[1,4,5,32,128]{4,2,0,3,1:T(8,128)(2,1)S(1)} %bitcast.307), channel_id=1, source_target_pairs={{0,4},{1,5},{2,6},{3,7},{4,0},{5,1},{6,2},{7,3}} | collective-permute-start | bytes 491528 | tf_op jit(solution)/shard_map/ppermute | solution.py:180
  297.5 13.1 %collective-permute-start.11 = (bf16[1,4,5,32,128]{4,2,0,3,1:T(8,128)(2,1)S(1)}, bf16[1,4,5,32,128]{4,2,0,3,1:T(8,128)(2,1)S(1)}, u32[]{:S(2)}, u32[]{:S(2)}) collective-permute-start(bf16[1,4,5,32,128]{4,2,0,3,1:T(8,128)(2,1)S(1)} %bitcast.306), channel_id=1, source_target_pairs={{0,5},{1,4},{2,7},{3,6},{4,1},{5,0},{6,3},{7,2}} | collective-permute-start | bytes 491528 | tf_op jit(solution)/shard_map/ppermute | solution.py:180
  300.2 12.8 %collective-permute-start.12 = (bf16[1,4,5,32,128]{4,2,0,3,1:T(8,128)(2,1)S(1)}, bf16[1,4,5,32,128]{4,2,0,3,1:T(8,128)(2,1)S(1)}, u32[]{:S(2)}, u32[]{:S(2)}) collective-permute-start(bf16[1,4,5,32,128]{4,2,0,3,1:T(8,128)(2,1)S(1)} %bitcast.305), channel_id=1, source_target_pairs={{0,6},{1,7},{2,4},{3,5},{4,2},{5,3},{6,0},{7,1}} | collective-permute-start | bytes 491528 | tf_op jit(solution)/shard_map/ppermute | solution.py:180
  310.6 8.5 %collective-permute-start.13 = (bf16[1,4,5,32,128]{4,2,0,3,1:T(8,128)(2,1)S(1)}, bf16[1,4,5,32,128]{4,2,0,3,1:T(8,128)(2,1)S(1)}, u32[]{:S(2)}, u32[]{:S(2)}) collective-permute-start(bf16[1,4,5,32,128]{4,2,0,3,1:T(8,128)(2,1)S(1)} %bitcast.304), channel_id=1, source_target_pairs={{0,7},{1,6},{2,5},{3,4},{4,3},{5,2},{6,1},{7,0}} | collective-permute-start | bytes 491528 | tf_op jit(solution)/shard_map/ppermute | solution.py:180
  313.0 40.9 %collective-permute-start.31 = (bf16[8,256,128]{2,1,0:T(8,128)(2,1)}, bf16[8,256,128]{2,1,0:T(8,128)(2,1)}, u32[]{:S(2)}, u32[]{:S(2)}) collective-permute-start(bf16[8,256,128]{2,1,0:T(8,128)(2,1)} %get-tuple-element.9), channel_id=1, source_target_pairs={{0,5},{1,4},{2,7},{3,6},{4,1},{5,0},{6,3},{7,2}} | collective-permute-start | bytes 1572872 | tf_op jit(solution)/shard_map/ppermute | solution.py:180
  319.1 35.7 %collective-permute-start.32 = (bf16[8,256,128]{2,1,0:T(8,128)(2,1)}, bf16[8,256,128]{2,1,0:T(8,128)(2,1)}, u32[]{:S(2)}, u32[]{:S(2)}) collective-permute-start(bf16[8,256,128]{2,1,0:T(8,128)(2,1)} %get-tuple-element.8), channel_id=1, source_target_pairs={{0,6},{1,7},{2,4},{3,5},{4,2},{5,3},{6,0},{7,1}} | collective-permute-start | bytes 1572872 | tf_op jit(solution)/shard_map/ppermute | solution.py:180
  323.0 32.5 %collective-permute-start.33 = (bf16[8,256,128]{2,1,0:T(8,128)(2,1)}, bf16[8,256,128]{2,1,0:T(8,128)(2,1)S(1)}, u32[]{:S(2)}, u32[]{:S(2)}) collective-permute-start(bf16[8,256,128]{2,1,0:T(8,128)(2,1)} %get-tuple-element.13), channel_id=1, source_target_pairs={{0,7},{1,6},{2,5},{3,4},{4,3},{5,2},{6,1},{7,0}} | collective-permute-start | bytes 1572872 | tf_op jit(solution)/shard_map/ppermute | solution.py:180
  345.5 75.7 %collective-permute-start.34 = (bf16[8,256,128]{2,1,0:T(8,128)(2,1)}, bf16[8,256,128]{2,1,0:T(8,128)(2,1)}, u32[]{:S(2)}, u32[]{:S(2)}) collective-permute-start(bf16[8,256,128]{2,1,0:T(8,128)(2,1)} %get-tuple-element.7), channel_id=1, source_target_pairs={{0,1},{1,0},{2,3},{3,2},{4,5},{5,4},{6,7},{7,6}} | collective-permute-start | bytes 1572872 | tf_op jit(solution)/shard_map/ppermute | solution.py:180
  345.5 76.7 %collective-permute-start.21 = (bf16[12,256,128]{2,1,0:T(8,128)(2,1)}, bf16[12,256,128]{2,1,0:T(8,128)(2,1)}, u32[]{:S(2)}, u32[]{:S(2)}) collective-permute-start(bf16[12,256,128]{2,1,0:T(8,128)(2,1)} %get-tuple-element.20), channel_id=1, source_target_pairs={{0,2},{1,3},{2,0},{3,1},{4,6},{5,7},{6,4},{7,5}} | collective-permute-start | bytes 2359304 | tf_op jit(solution)/shard_map/ppermute | solution.py:180
  353.9 69.4 %collective-permute-start.22 = (bf16[12,256,128]{2,1,0:T(8,128)(2,1)}, bf16[12,256,128]{2,1,0:T(8,128)(2,1)}, u32[]{:S(2)}, u32[]{:S(2)}) collective-permute-start(bf16[12,256,128]{2,1,0:T(8,128)(2,1)} %get-tuple-element.19), channel_id=1, source_target_pairs={{0,4},{1,5},{2,6},{3,7},{4,0},{5,1},{6,2},{7,3}} | collective-permute-start | bytes 2359304 | tf_op jit(solution)/shard_map/ppermute | solution.py:180
  354.8 69.5 %collective-permute-start.23 = (bf16[12,256,128]{2,1,0:T(8,128)(2,1)}, bf16[12,256,128]{2,1,0:T(8,128)(2,1)}, u32[]{:S(2)}, u32[]{:S(2)}) collective-permute-start(bf16[12,256,128]{2,1,0:T(8,128)(2,1)} %get-tuple-element.18), channel_id=1, source_target_pairs={{0,3},{1,2},{2,1},{3,0},{4,7},{5,6},{6,5},{7,4}} | collective-permute-start | bytes 2359304 | tf_op jit(solution)/shard_map/ppermute | solution.py:180
  355.5 65.7 %copy-start.7 = (bf16[8,256,128]{2,1,0:T(8,128)(2,1)}, bf16[8,256,128]{2,1,0:T(8,128)(2,1)S(1)}, u32[]{:S(2)}) copy-start(bf16[8,256,128]{2,1,0:T(8,128)(2,1)S(1)} %collective-permute-done.33.refs_6_) | copy-start | bytes 1572868
  355.5 69.5 %collective-permute-start.24 = (bf16[12,256,128]{2,1,0:T(8,128)(2,1)}, bf16[12,256,128]{2,1,0:T(8,128)(2,1)}, u32[]{:S(2)}, u32[]{:S(2)}) collective-permute-start(bf16[12,256,128]{2,1,0:T(8,128)(2,1)} %get-tuple-element.17), channel_id=1, source_target_pairs={{0,5},{1,4},{2,7},{3,6},{4,1},{5,0},{6,3},{7,2}} | collective-permute-start | bytes 2359304 | tf_op jit(solution)/shard_map/ppermute | solution.py:180
  356.9 68.9 %copy-start.2 = (f32[4,32,5120]{2,1,0:T(8,128)S(1)}, f32[4,32,5120]{2,1,0:T(8,128)}, u32[]{:S(2)}) copy-start(f32[4,32,5120]{2,1,0:T(8,128)} %get-tuple-element.56) | copy-start | bytes 7864324
  421.2 65.1 %collective-permute-start.25 = (bf16[12,256,128]{2,1,0:T(8,128)(2,1)}, bf16[12,256,128]{2,1,0:T(8,128)(2,1)}, u32[]{:S(2)}, u32[]{:S(2)}) collective-permute-start(bf16[12,256,128]{2,1,0:T(8,128)(2,1)} %get-tuple-element.16), channel_id=1, source_target_pairs={{0,6},{1,7},{2,4},{3,5},{4,2},{5,3},{6,0},{7,1}} | collective-permute-start | bytes 2359304 | tf_op jit(solution)/shard_map/ppermute | solution.py:180
  422.3 64.5 %collective-permute-start.26 = (bf16[12,256,128]{2,1,0:T(8,128)(2,1)}, bf16[12,256,128]{2,1,0:T(8,128)(2,1)}, u32[]{:S(2)}, u32[]{:S(2)}) collective-permute-start(bf16[12,256,128]{2,1,0:T(8,128)(2,1)} %get-tuple-element.15), channel_id=1, source_target_pairs={{0,7},{1,6},{2,5},{3,4},{4,3},{5,2},{6,1},{7,0}} | collective-permute-start | bytes 2359304 | tf_op jit(solution)/shard_map/ppermute | solution.py:180
  423.3 65.2 %collective-permute-start.27 = (bf16[12,256,128]{2,1,0:T(8,128)(2,1)}, bf16[12,256,128]{2,1,0:T(8,128)(2,1)}, u32[]{:S(2)}, u32[]{:S(2)}) collective-permute-start(bf16[12,256,128]{2,1,0:T(8,128)(2,1)} %get-tuple-element.14), channel_id=1, source_target_pairs={{0,1},{1,0},{2,3},{3,2},{4,5},{5,4},{6,7},{7,6}} | collective-permute-start | bytes 2359304 | tf_op jit(solution)/shard_map/ppermute | solution.py:180
  424.3 65.3 %collective-permute-start.14 = (bf16[12,256,128]{2,1,0:T(8,128)(2,1)}, bf16[12,256,128]{2,1,0:T(8,128)(2,1)}, u32[]{:S(2)}, u32[]{:S(2)}) collective-permute-start(bf16[12,256,128]{2,1,0:T(8,128)(2,1)} %get-tuple-element.27), channel_id=1, source_target_pairs={{0,2},{1,3},{2,0},{3,1},{4,6},{5,7},{6,4},{7,5}} | collective-permute-start | bytes 2359304 | tf_op jit(solution)/shard_map/ppermute | solution.py:180
  425.1 65.2 %collective-permute-start.15 = (bf16[12,256,128]{2,1,0:T(8,128)(2,1)}, bf16[12,256,128]{2,1,0:T(8,128)(2,1)}, u32[]{:S(2)}, u32[]{:S(2)}) collective-permute-start(bf16[12,256,128]{2,1,0:T(8,128)(2,1)} %get-tuple-element.26), channel_id=1, source_target_pairs={{0,4},{1,5},{2,6},{3,7},{4,0},{5,1},{6,2},{7,3}} | collective-permute-start | bytes 2359304 | tf_op jit(solution)/shard_map/ppermute | solution.py:180
  486.3 91.7 %collective-permute-start.16 = (bf16[12,256,128]{2,1,0:T(8,128)(2,1)}, bf16[12,256,128]{2,1,0:T(8,128)(2,1)S(1)}, u32[]{:S(2)}, u32[]{:S(2)}) collective-permute-start(bf16[12,256,128]{2,1,0:T(8,128)(2,1)} %get-tuple-element.25), channel_id=1, source_target_pairs={{0,3},{1,2},{2,1},{3,0},{4,7},{5,6},{6,5},{7,4}} | collective-permute-start | bytes 2359304 | tf_op jit(solution)/shard_map/ppermute | solution.py:180
  486.7 91.3 %collective-permute-start.17 = (bf16[12,256,128]{2,1,0:T(8,128)(2,1)}, bf16[12,256,128]{2,1,0:T(8,128)(2,1)}, u32[]{:S(2)}, u32[]{:S(2)}) collective-permute-start(bf16[12,256,128]{2,1,0:T(8,128)(2,1)} %get-tuple-element.24), channel_id=1, source_target_pairs={{0,5},{1,4},{2,7},{3,6},{4,1},{5,0},{6,3},{7,2}} | collective-permute-start | bytes 2359304 | tf_op jit(solution)/shard_map/ppermute | solution.py:180
  488.5 89.6 %collective-permute-start.18 = (bf16[12,256,128]{2,1,0:T(8,128)(2,1)}, bf16[12,256,128]{2,1,0:T(8,128)(2,1)}, u32[]{:S(2)}, u32[]{:S(2)}) collective-permute-start(bf16[12,256,128]{2,1,0:T(8,128)(2,1)} %get-tuple-element.23), channel_id=1, source_target_pairs={{0,6},{1,7},{2,4},{3,5},{4,2},{5,3},{6,0},{7,1}} | collective-permute-start | bytes 2359304 | tf_op jit(solution)/shard_map/ppermute | solution.py:180
  489.6 88.5 %collective-permute-start.19 = (bf16[12,256,128]{2,1,0:T(8,128)(2,1)}, bf16[12,256,128]{2,1,0:T(8,128)(2,1)}, u32[]{:S(2)}, u32[]{:S(2)}) collective-permute-start(bf16[12,256,128]{2,1,0:T(8,128)(2,1)} %get-tuple-element.22), channel_id=1, source_target_pairs={{0,7},{1,6},{2,5},{3,4},{4,3},{5,2},{6,1},{7,0}} | collective-permute-start | bytes 2359304 | tf_op jit(solution)/shard_map/ppermute | solution.py:180
  490.2 87.9 %collective-permute-start.20 = (bf16[12,256,128]{2,1,0:T(8,128)(2,1)}, bf16[12,256,128]{2,1,0:T(8,128)(2,1)}, u32[]{:S(2)}, u32[]{:S(2)}) collective-permute-start(bf16[12,256,128]{2,1,0:T(8,128)(2,1)} %get-tuple-element.21), channel_id=1, source_target_pairs={{0,1},{1,0},{2,3},{3,2},{4,5},{5,4},{6,7},{7,6}} | collective-permute-start | bytes 2359304 | tf_op jit(solution)/shard_map/ppermute | solution.py:180
  578.1 0.9 copy-start.6
where the time goes:
time: 594 us; the launch traced here: 587 us
  matrix products  265 us (45%)
  waiting for transfers between devices  192 us (32%)
  starting transfers between devices  47.5 us (8%)
  Pallas kernels  36.1 us (6%)
  local copies, waits for them, and re-layouts  27.4 us (5%)
  other arithmetic  16.9 us (3%)
    ppermute x35, waiting for transfers between devices, swap(): return lax.ppermute(arr, 'x', [(d, d ^ rel_idx) for d in range(n_dev)])  192 us
    dot_general x1, matrix products, finish(): jnp.einsum('sbd,df->sbf', normed, w_gate, preferred_element_type=jnp.floa...  64.3 us
    dot_general x1, matrix products, finish(): jnp.einsum('sbd,df->sbf', normed, w_up, preferred_element_type=jnp.float32)  60.5 us
    dot_general x1, matrix products, finish(): jnp.einsum('sbf,fd->sbd', activated, w_down, preferred_element_type=jnp.f...  58.1 us
    ppermute x35, starting transfers between devices, swap(): return lax.ppermute(arr, 'x', [(d, d ^ rel_idx) for d in range(n_dev)])  42.8 us
    dot_general x1, matrix products, finish(): jnp.einsum('sbe,ed->sbd', flat_attn, w_o, preferred_element_type=jnp.floa...  20.8 us
    pallas_call x3, Pallas kernels, merge_chunk(): pl.pallas_call(functools.partial(merge_chunk_kernel, row_base, n_dev), ou...  20.2 us
    dot_general x1, matrix products, project(): jnp.einsum('sbd,de->sbe', normed, w_q, preferred_element_type=jnp.float32)  18.2 us
  transfers between devices with their start and end apart: 36, of which 11 were waited for; matrix products, arithmetic and copies ran while one was open for 52% of the time, Pallas kernels for 5%

commit v1 on v0

--- a/solution.py
+++ b/solution.py
@@ -40,27 +40,6 @@
     queries = rotary(rms_norm(queries, q_norm), positions).astype(jnp.bfloat16)
     keys_new = rotary(rms_norm(keys_new, k_norm), positions).astype(jnp.bfloat16)
     return queries, keys_new, values_new.astype(jnp.bfloat16)
-
-
-def attend(queries, cache_k, cache_v, keys_new, values_new, start_pos):
-    n_steps, num_rows, n_heads, head_dim = queries.shape
-    num_slots, kv_local = cache_k.shape[1], cache_k.shape[2]
-    grouped = queries.reshape(n_steps, num_rows, kv_local, n_heads // kv_local, head_dim)
-    score_scale = head_dim ** -0.5
-    old_scores = jnp.einsum('sbkgd,btkd->bkgst', grouped, cache_k, preferred_element_type=jnp.float32) * score_scale
-    old_valid = (jnp.arange(num_slots)[None, :] < start_pos[:, None])[:, None, None, None, :]
-    old_scores = jnp.where(old_valid, old_scores, -jnp.inf)
-    new_scores = jnp.einsum('sbkgd,jbkd->bkgsj', grouped, keys_new, preferred_element_type=jnp.float32) * score_scale
-    new_valid = jnp.arange(n_steps)[:, None] >= jnp.arange(n_steps)[None, :]
-    new_scores = jnp.where(new_valid, new_scores, -jnp.inf)
-    peak_score = jnp.maximum(jnp.max(old_scores, axis=-1, keepdims=True), jnp.max(new_scores, axis=-1, keepdims=True))
-    old_weights = jnp.exp(old_scores - peak_score)
-    new_weights = jnp.exp(new_scores - peak_score)
-    weight_sum = jnp.sum(old_weights, axis=-1) + jnp.sum(new_weights, axis=-1)
-    mixed_vals = jnp.einsum('bkgst,btkd->sbkgd', old_weights.astype(jnp.bfloat16), cache_v, preferred_element_type=jnp.float32)
-    mixed_vals = mixed_vals + jnp.einsum('bkgsj,jbkd->sbkgd', new_weights.astype(jnp.bfloat16), values_new, preferred_element_type=jnp.float32)
-    mixed_vals = mixed_vals / jnp.transpose(weight_sum, (3, 0, 1, 2))[..., None]
-    return mixed_vals.astype(jnp.bfloat16).reshape(n_steps, num_rows, n_heads, head_dim)
 
 
 def finish(hidden, attended, w_o, mlp_norm, w_gate, w_up, w_down):
@@ -78,7 +57,7 @@
 
 ROW_PAD = 9
 MERGE_ROWS = 4
-K_CUTS = (8, 20, 32)
+K_CUTS = (8, 18, 26, 32)
 SWAP_ORDER = (2, 4, 3, 5, 6, 7, 1)
 
 
@@ -163,6 +142,70 @@
     )(meta, blocks, fresh_rows)
 
 
+def attend_kernel(n_steps, score_scale, pos_ref, sent_ref, k_ref, v_ref, out_ref, rows_ref, mixed_ref):
+    num_sent, step_rows, head_dim = sent_ref.shape[1:]
+    num_q = out_ref.shape[1]
+    pad_q = num_sent + n_steps
+    stride = num_sent + 1 - num_sent % 2
+    group = num_q // n_steps
+    num_slots = k_ref.shape[1]
+    rows_ref[step_rows * stride:, :] = jnp.zeros((rows_ref.shape[0] - step_rows * stride, head_dim), jnp.float32)
+    for sent_idx in range(num_sent):
+        rows_ref[pl.ds(sent_idx, step_rows, stride=stride), :] = sent_ref[0, sent_idx].astype(jnp.float32)
+    rows_ref[pl.ds(num_sent, step_rows, stride=stride), :] = jnp.zeros((step_rows, head_dim), jnp.float32)
+    row_step = lax.broadcasted_iota(jnp.int32, (pad_q, pad_q), 0) // group
+    col_step = lax.broadcasted_iota(jnp.int32, (pad_q, pad_q), 1) - num_q
+    new_valid = (col_step >= 0) & (col_step < n_steps) & (col_step <= row_step)
+    slot_ids = lax.broadcasted_iota(jnp.int32, (pad_q, num_slots), 1)
+    over_lanes = (((1,), (1,)), ((), ()))
+    base = (pl.program_id(0) * pl.num_programs(1) + pl.program_id(1)) * step_rows
+    for row_idx in range(step_rows):
+        at = row_idx * stride
+        queries = rows_ref[at:at + pad_q, :].astype(jnp.bfloat16)
+        values_new = rows_ref[at + n_steps:at + n_steps + pad_q, :].astype(jnp.bfloat16)
+        old_scores = lax.dot_general(queries, k_ref[row_idx], over_lanes, preferred_element_type=jnp.float32) * score_scale
+        new_scores = lax.dot_general(queries, queries, over_lanes, preferred_element_type=jnp.float32) * score_scale
+        old_scores = jnp.where(slot_ids < pos_ref[base + row_idx], old_scores, -jnp.inf)
+        new_scores = jnp.where(new_valid, new_scores, -jnp.inf)
+        peak = jnp.maximum(jnp.max(old_scores, axis=-1, keepdims=True), jnp.max(new_scores, axis=-1, keepdims=True))
+        old_weights = jnp.exp(old_scores - peak)
+        new_weights = jnp.exp(new_scores - peak)
+        weight_sum = jnp.sum(old_weights, axis=-1, keepdims=True) + jnp.sum(new_weights, axis=-1, keepdims=True)
+        mixed = jnp.dot(old_weights.astype(jnp.bfloat16), v_ref[row_idx], preferred_element_type=jnp.float32)
+        mixed = mixed + jnp.dot(new_weights.astype(jnp.bfloat16), values_new, preferred_element_type=jnp.float32)
+        mixed = mixed / weight_sum
+        mixed_ref[pl.ds(row_idx, pad_q, stride=step_rows + 1), :] = mixed
+    for q_idx in range(num_q):
+        at = q_idx * (step_rows + 1)
+        out_ref[0, q_idx] = mixed_ref[at:at + step_rows, :].astype(out_ref.dtype)
+
+
+def attend_local(got, k_own, v_own, start_pos, n_steps):
+    n_dev, num_sent, num_rows, head_dim = got.shape
+    num_slots = k_own.shape[1]
+    num_q = num_sent - 2 * n_steps
+    step_rows = 8
+    inner = num_rows // step_rows
+    pad_q = num_sent + n_steps
+    stride = num_sent + 1 - num_sent % 2
+    cache_spec = pl.BlockSpec((step_rows, num_slots, head_dim), lambda p, b, pos: (p * inner + b, 0, 0))
+    return pl.pallas_call(
+        functools.partial(attend_kernel, n_steps, head_dim ** -0.5),
+        out_shape=jax.ShapeDtypeStruct((n_dev, num_q, num_rows, head_dim), got.dtype),
+        grid_spec=pltpu.PrefetchScalarGridSpec(
+            num_scalar_prefetch=1,
+            grid=(n_dev, inner),
+            in_specs=[pl.BlockSpec((1, num_sent, step_rows, head_dim), lambda p, b, pos: (p, 0, b, 0)), cache_spec, cache_spec],
+            out_specs=pl.BlockSpec((1, num_q, step_rows, head_dim), lambda p, b, pos: (p, 0, b, 0)),
+            scratch_shapes=[
+                pltpu.VMEM((step_rows * stride + 16, head_dim), jnp.float32),
+                pltpu.VMEM((pad_q * (step_rows + 1) + 8, head_dim), jnp.float32),
+            ],
+        ),
+        cost_estimate=pl.CostEstimate(flops=10**9, bytes_accessed=4 * k_own.size, transcendentals=0),
+    )(start_pos, got, k_own, v_own)
+
+
 def solution(mesh):
     n_dev = mesh.shape['x']
     row_spec = P(None, ('dp', 'x'), None)
@@ -171,7 +214,7 @@
 
     def local_run(start_pos, hidden_in, k_heads, v_heads, attn_norm, w_q, w_k, w_v, q_norm, k_norm, w_o, mlp_norm, w_gate, w_up, w_down):
         n_steps, num_rows, _ = hidden_in.shape
-        all_rows, num_slots, _, head_dim = k_heads.shape
+        _, num_slots, _, head_dim = k_heads.shape
         me = lax.axis_index('x')
         my_pos = lax.dynamic_slice_in_dim(start_pos, me * num_rows, num_rows)
         k_own, v_own = k_heads[:, :, 0], v_heads[:, :, 0]
@@ -191,26 +234,11 @@
         k_send = keys_new.transpose(2, 0, 1, 3)
         v_send = values_new.transpose(2, 0, 1, 3)
         sent = jnp.concatenate([q_send, k_send, v_send], axis=1)
-        got = jnp.zeros((n_steps * (group + 2), n_dev, num_rows, head_dim), sent.dtype)
-        for rel_idx in range(n_dev):
-            peer = jnp.bitwise_xor(me, rel_idx)
-            part = lax.dynamic_index_in_dim(sent, peer, 0, keepdims=False)
-            part = swap(part, rel_idx) if rel_idx else part
-            got = lax.dynamic_update_slice_in_dim(got, part[:, None], peer, 1)
-        got = got.reshape(n_steps * (group + 2), all_rows, head_dim)
-        q_got = got[:n_steps * group].reshape(n_steps, group, all_rows, head_dim).transpose(0, 2, 1, 3)
-        kn_got = got[n_steps * group:n_steps * (group + 1), :, None]
-        vn_got = got[n_steps * (group + 1):, :, None]
-        mixed = attend(q_got, k_heads, v_heads, kn_got, vn_got, start_pos)
-        mixed = mixed.reshape(n_steps, n_dev, num_rows, group, head_dim).transpose(1, 0, 3, 2, 4)
+        got = lax.all_to_all(sent, 'x', 0, 0, tiled=True)
+        mixed = attend_local(got, k_own, v_own, start_pos, n_steps)
         v_got = lax.all_to_all(v_own, 'x', 0, 0, tiled=True).reshape(n_dev, num_rows, num_slots, head_dim)
-        back = jnp.zeros_like(mixed)
-        for rel_idx in range(n_dev):
-            peer = jnp.bitwise_xor(me, rel_idx)
-            part = lax.dynamic_index_in_dim(mixed, peer, 0)
-            part = swap(part, rel_idx) if rel_idx else part
-            back = lax.dynamic_update_slice_in_dim(back, part, peer, 0)
-        attended = back.transpose(1, 3, 0, 2, 4).reshape(n_steps, num_rows, n_dev * group, head_dim)
+        back = lax.all_to_all(mixed, 'x', 0, 0, tiled=True)
+        attended = back.reshape(n_dev, n_steps, group, num_rows, head_dim).transpose(1, 3, 0, 2, 4).reshape(n_steps, num_rows, n_dev * group, head_dim)
         out_hidden = finish(hidden_in, attended, w_o, mlp_norm, w_gate, w_up, w_down)
         meta = jnp.concatenate([jnp.bitwise_xor(me, jnp.array((0,) + SWAP_ORDER)), my_pos]).astype(jnp.int32)
         k_out, v_out = None, merge_all(v_got, values_new, meta)

time: 594 us -> 528 us (0.89)
  waiting for transfers between devices: 192 us -> 108 us
  Pallas kernels: 36.1 us -> 115 us
  matrix products: 265 us -> 225 us
  starting transfers between devices: 47.5 us -> 39.8 us
  other arithmetic: 16.9 us -> 10.2 us
    ppermute x35 -> x28, waiting for transfers between devices: 192 us -> 108 us  [swap(): return lax.ppermute(arr, 'x', [(d, d ^ rel_idx) for d in range(n_dev)])]
    pallas_call x0 -> x1, Pallas kernels: none -> 75.4 us  [attend_local(): pl.pallas_call(functools.partial(attend_kernel, n_steps, head_dim ** (-0....]
    dot_general x4 -> x0, matrix products: 32.6 us -> none  [the longest x1 12.1 us: attend(): jnp.einsum('sbkgd,btkd->bkgst', grouped, cache_k, preferred_element_type=...]
    ppermute x35 -> x28, starting transfers between devices: 42.8 us -> 28.6 us  [swap(): return lax.ppermute(arr, 'x', [(d, d ^ rel_idx) for d in range(n_dev)])]
    reduce_sum x2 -> x0, other arithmetic: 7.95 us -> none  [attend(): weight_sum = jnp.sum(old_weights, axis=-1) + jnp.sum(new_weights, axis=-1)]
    all_to_all x0 -> x2, starting transfers between devices: none -> 6.71 us  [the longest x1 4.27 us: local_run(): got = lax.all_to_all(sent, 'x', 0, 0, tiled=True)]
    pallas_call x3 -> x4, Pallas kernels: 20.2 us -> 24.1 us  [merge_chunk(): pl.pallas_call(functools.partial(merge_chunk_kernel, row_base, n_dev), ou...]
    dynamic_slice x2 -> x3, local copies, waits for them, and re-layouts: 12.3 us -> 13.3 us  [swap_cache(): lax.dynamic_slice_in_dim(own, jnp.bitwise_xor(me, rel_idx) * num_rows + r...]
  transfers between devices with their start and end apart: 36 -> 31, of which waited for: 11 -> 8; matrix products, arithmetic and copies ran while one was open for 52% -> 41% of each run, Pallas kernels for 5% -> 21%
where the time goes in v1:
time: 528 us; the launch traced here: 527 us
  matrix products  225 us (43%)
  Pallas kernels  115 us (22%)
  waiting for transfers between devices  108 us (20%)
  starting transfers between devices  39.8 us (8%)
  local copies, waits for them, and re-layouts  26.4 us (5%)
  other arithmetic  10.2 us (2%)
    ppermute x28, waiting for transfers between devices, swap(): return lax.ppermute(arr, 'x', [(d, d ^ rel_idx) for d in range(n_dev)])  108 us
    pallas_call x1, Pallas kernels, attend_local(): pl.pallas_call(functools.partial(attend_kernel, n_steps, head_dim ** (-0....  75.4 us
    dot_general x1, matrix products, finish(): jnp.einsum('sbd,df->sbf', normed, w_up, preferred_element_type=jnp.float32)  60.5 us
    dot_general x1, matrix products, finish(): jnp.einsum('sbd,df->sbf', normed, w_gate, preferred_element_type=jnp.floa...  60 us
    dot_general x1, matrix products, finish(): jnp.einsum('sbf,fd->sbd', activated, w_down, preferred_element_type=jnp.f...  58.1 us
    ppermute x28, starting transfers between devices, swap(): return lax.ppermute(arr, 'x', [(d, d ^ rel_idx) for d in range(n_dev)])  28.6 us
    pallas_call x4, Pallas kernels, merge_chunk(): pl.pallas_call(functools.partial(merge_chunk_kernel, row_base, n_dev), ou...  24.1 us
    dot_general x1, matrix products, finish(): jnp.einsum('sbe,ed->sbd', flat_attn, w_o, preferred_element_type=jnp.floa...  20.8 us
  transfers between devices with their start and end apart: 31, of which 8 were waited for; matrix products, arithmetic and copies ran while one was open for 41% of the time, Pallas kernels for 21%

profile of v1, /device:TPU:0, one launch (start us, length us, event | category | flops | bytes accessed | tf_op | source)
XLA Modules:
  0.0 526.5 jit_solution(247116637997021795)
XLA Ops:
  0.7 0.8 dynamic_slice.143
  1.4 0.7 convert_element_type.52
  2.1 1.7 fusion.47
  3.8 6.1 %fusion.20 = f32[4,32,1024]{2,1,0:T(8,128)S(1)} fusion(bf16[5120,1024]{1,0:T(8,128)(2,1)} %param.22, bf16[4,32,5120]{2,1,0:T(8,128)(2,1)} %param.17, f32[5120]{0:T(1024)S(1)} %convert_element_type.52, f32[4,32]{1,0:T(4,128)S(1)} %add_rsqrt_fusion.3), kind=kOutput, calls=%fused_computation.14 | convolution fusion | flops 1344798720 | bytes 12341760 | tf_op jit(solution)/shard_map/sbd,de->sbe/dot_general | solution.py:38
  10.3 1.3 copy-done.19
  11.6 1.6 fusion.58
  14.2 18.2 %fusion.8 = f32[4,32,5120]{2,1,0:T(8,128)S(1)} fusion(bf16[5120,5120]{1,0:T(8,128)(2,1)} %param.21, bf16[4,32,5120]{2,1,0:T(8,128)(2,1)S(1)} %copy-done, f32[5120]{0:T(1024)S(1)} %convert_element_type.52, f32[4,32]{1,0:T(4,128)S(1)} %add_rsqrt_fusion.3), kind=kOutput, calls=%fused_computation.8 | convolution fusion | flops 6713507840 | bytes 56381952 | tf_op jit(solution)/shard_map/sbd,de->sbe/dot_general | solution.py:37
  32.9 1.0 copy-done.1
  33.9 0.7 fusion.50
  34.8 2.2 fusion.51
  37.0 0.9 subtract_convert_fusion
  37.9 0.7 maximum_bitcast_fusion
  39.0 1.4 pad_maximum_fusion
  40.5 4.3 all-to-all-start
  44.8 5.9 %dynamic-slice_bitcast_fusion.7 = (bf16[8,256,128]{2,1,0:T(8,128)(2,1)}, bf16[8,256,128]{2,1,0:T(8,128)(2,1)}, bf16[8,256,128]{2,1,0:T(8,128)(2,1)}, bf16[8,256,...) fusion(bf16[256,256,1,128]{3,1,2,0:T(8,128)(2,1)} %param.18, ...), kind=kLoop, calls=%fused_computation.59 | loop fusion | bytes 14680120 | tf_op jit(solution)/shard_map/dynamic_slice | solution.py:226
  50.7 2.0 collective-permute-start.21
  52.7 1.5 collective-permute-start.22
  54.5 2.9 collective-permute-start.25
  57.4 22.2 %collective-permute-done.21.refs_1_ = bf16[8,256,128]{2,1,0:T(8,128)(2,1)} collective-permute-done((bf16[8,256,128]{2,1,0:T(8,128)(2,1)S(1)}, bf16[8,256,128]{2,1,0:T(8,128)(2,1)}, u32[]{:S(2)}, u32[]{:S(2)}) %collective-permute-start.21) | collective-permute-done | bytes 524320 | tf_op jit(solution)/shard_map/ppermute | solution.py:223
  79.7 4.1 dynamic-slice_bitcast_fusion
  83.8 1.5 collective-permute-start.14
  85.3 4.4 collective-permute-done.23.refs_3_
  89.7 1.5 collective-permute-start.15
  91.2 1.0 collective-permute-start.27
  92.2 10.9 %collective-permute-done.25.refs_5_ = bf16[8,256,128]{2,1,0:T(8,128)(2,1)} collective-permute-done((bf16[8,256,128]{2,1,0:T(8,128)(2,1)}, bf16[8,256,128]{2,1,0:T(8,128)(2,1)}, u32[]{:S(2)}, u32[]{:S(2)}) %collective-permute-start.25) | collective-permute-done | bytes 524320 | tf_op jit(solution)/shard_map/ppermute | solution.py:223
  103.1 10.1 %collective-permute-done.26.refs_6_ = bf16[8,256,128]{2,1,0:T(8,128)(2,1)} collective-permute-done((bf16[8,256,128]{2,1,0:T(8,128)(2,1)}, bf16[8,256,128]{2,1,0:T(8,128)(2,1)}, u32[]{:S(2)}, u32[]{:S(2)}) %collective-permute-start.26) | collective-permute-done | bytes 524320 | tf_op jit(solution)/shard_map/ppermute | solution.py:223
  113.2 0.8 collective-permute-start.11
  114.0 1.5 collective-permute-start.16
  115.5 34.6 %collective-permute-done.10.refs_4_ = bf16[8,256,128]{2,1,0:T(8,128)(2,1)S(1)} collective-permute-done((bf16[8,256,128]{2,1,0:T(8,128)(2,1)S(1)}, bf16[8,256,128]{2,1,0:T(8,128)(2,1)S(1)}, u32[]{:S(2)}, u32[]{:S(2)}) %collective-permute-start.10) | collective-permute-done | bytes 524320 | tf_op jit(solution)/shard_map/ppermute | solution.py:223
  150.4 1.5 collective-permute-start.18
  151.9 1.1 collective-permute-start.19
  153.0 0.8 copy-done.8
  153.9 0.5 collective-permute-start.20
  154.3 1.2 copy-done.4
  155.6 75.4 %shard_map.175 = bf16[8,20,32,128]{3,2,1,0:T(8,128)(2,1)} custom-call(s32[256]{0:T(256)} %pos_ref.1, bf16[8,28,32,128]{3,2,1,0:T(8,128)(2,1)} %copy-done.4, bf16[256,256,128]{2,1,0:T(8,128)(2,1)} %bitcast.156, bf16[256,256,128]{2,1,0:T(8,128)(2,1)} %bitcast.161), custom_call_target="tpu_custom_call" | custom-call | flops 1000000000 | bytes 33554432 | tf_op jit(solution)/shard_map/pallas_call | solution.py:192
  230.9 2.4 all-to-all-start.1
  233.5 2.6 collective-permute-start.12
  236.4 0.5 collective-permute-start.7
  237.1 1.0 collective-permute-start.9
  238.2 0.6 pad_add_fusion.meta_ref
  238.8 3.3 dynamic-slice_bitcast_fusion.21
  242.1 4.8 shard_map.177.refs_9_
  246.8 7.8 %shard_map.178.refs_9_ = bf16[32,256,8,128]{3,2,1,0:T(8,128)(2,1)} custom-call(s32[40]{0:T(128)} %pad_add_fusion.meta_ref, bf16[256,256,128]{2,1,0:T(8,128)(2,1)} %bitcast.158, bf16[10,256,128]{2,1,0:T(8,128)(2,1)} %copy-done.7, bf16[10,256,128]{2,1,0:T(8,128)(2,1)} %copy-done.8, ...), custom_call_target="tpu_custom_call", output_to_operand_aliasing={{}: (10, {})} | custom-call | flops 100000000 | bytes 10485760 | tf_op jit(solution)/shard_map/pallas_call | solution.py:106
  254.7 7.6 %collective-permute-done.12.refs_6_ = bf16[8,256,128]{2,1,0:T(8,128)(2,1)S(1)} collective-permute-done((bf16[8,256,128]{2,1,0:T(8,128)(2,1)}, bf16[8,256,128]{2,1,0:T(8,128)(2,1)S(1)}, u32[]{:S(2)}, u32[]{:S(2)}) %collective-permute-start.12) | collective-permute-done | bytes 524320 | tf_op jit(solution)/shard_map/ppermute | solution.py:223
  262.3 0.6 collective-permute-start
  262.9 0.7 collective-permute-start.1
  263.6 10.2 %collective-permute-done.7.refs_1_ = bf16[8,256,128]{2,1,0:T(8,128)(2,1)} collective-permute-done((bf16[8,256,128]{2,1,0:T(8,128)(2,1)}, bf16[8,256,128]{2,1,0:T(8,128)(2,1)}, u32[]{:S(2)}, u32[]{:S(2)}) %collective-permute-start.7) | collective-permute-done | bytes 524320 | tf_op jit(solution)/shard_map/ppermute | solution.py:223
  273.8 1.8 collective-permute-start.3
  275.6 8.3 %collective-permute-done.9.refs_3_ = bf16[8,256,128]{2,1,0:T(8,128)(2,1)} collective-permute-done((bf16[8,256,128]{2,1,0:T(8,128)(2,1)}, bf16[8,256,128]{2,1,0:T(8,128)(2,1)}, u32[]{:S(2)}, u32[]{:S(2)}) %collective-permute-start.9) | collective-permute-done | bytes 524320 | tf_op jit(solution)/shard_map/ppermute | solution.py:223
  283.8 1.6 collective-permute-start.4
  285.5 5.9 %shard_map.179.refs_9_ = bf16[32,256,8,128]{3,2,1,0:T(8,128)(2,1)} custom-call(s32[40]{0:T(128)} %pad_add_fusion.meta_ref, bf16[256,256,128]{2,1,0:T(8,128)(2,1)} %bitcast.159, bf16[8,256,128]{2,1,0:T(8,128)(2,1)} %collective-permute-done.7.refs_1_, bf16[8,256,128]{2,1,0:T(8,128)(2,1)} %collective-permute-done.8.refs_2_, ...), custom_call_target="tpu_custom_call", output_to_operand_aliasing={{}: (10, {})} | custom-call | flops 100000000 | bytes 8388608 | tf_op jit(solution)/shard_map/pallas_call | solution.py:106
  291.4 1.0 copy-done.5
  292.5 4.5 all-to-all-start.2
  296.9 2.0 copy.42
  298.9 2.3 reshape_reshape.3
  301.2 20.8 %multiply_reduce_fusion = (f32[4,32]{1,0:T(4,128)S(1)}, f32[4,32,5120]{2,1,0:T(8,128)}) fusion(bf16[4,32,5120]{2,1,0:T(8,128)(2,1)} %reshape_reshape.3, bf16[5120,5120]{1,0:T(8,128)(2,1)} %param.26, bf16[4,32,5120]{2,1,0:T(8,128)(2,1)S(1)} %copy-done), kind=kOutput, calls=%fused_computation.37 | convolution fusion | flops 6714818560 | bytes 57672192 | tf_op jit(solution)/shard_map/sbe,ed->sbd/dot_general | solution.py:48
  322.1 60.0 %fusion.4 = f32[4,32,17408]{2,1,0:T(8,128)} fusion(bf16[5120,17408]{1,0:T(8,128)(2,1)} %param.28, f32[4,32,5120]{2,1,0:T(8,128)} %get-tuple-element.42, f32[5120]{0:T(1024)S(1)} %convert_element_type.61, f32[4,32]{1,0:T(4,128)S(1)} %add_rsqrt_fusion.2), kind=kOutput, calls=%fused_computation.4 | convolution fusion | flops 22818979840 | bytes 189813248 | tf_op jit(solution)/shard_map/sbd,df->sbf/dot_general | solution.py:51
  382.0 60.5 %fusion.13.clone.8 = bf16[4,32,17408]{2,1,0:T(8,128)(2,1)} fusion(bf16[5120,17408]{1,0:T(8,128)(2,1)} %param.29, f32[4,32,17408]{2,1,0:T(8,128)} %fusion.4, f32[4,32,5120]{2,1,0:T(8,128)S(1)} %copy-done.2, f32[5120]{0:T(1024)S(1)} %convert_element_type.61, f32[4,32]{1,0:T(4,128)S(1)} %add_rsqrt_fusion.2), kind=kOutput, calls=%fused_computation.11.clone.clone.clone.clone.clone.clone.clone.1 | convolution fusion | flops 22832349184 | bytes 194269696 | tf_op jit(solution)/shard_map/sbd,df->sbf/dot_general | solution.py:52
  442.5 2.6 collective-permute-start.5
  445.5 58.1 %fusion.41 = bf16[4,32,5120]{2,1,0:T(8,128)(2,1)} fusion(f32[4,32,5120]{2,1,0:T(8,128)S(1)} %copy-done.2, bf16[17408,5120]{1,0:T(8,128)(2,1)} %param.30, bf16[4,32,17408]{2,1,0:T(8,128)(2,1)} %fusion.13.clone.8), kind=kOutput, calls=%fused_computation.25 | convolution fusion | flops 22818324480 | bytes 186646528 | tf_op jit(solution)/shard_map/sbf,fd->sbd/dot_general | solution.py:54
  503.5 15.9 %shard_map.176 = bf16[32,256,8,128]{3,2,1,0:T(8,128)(2,1)} custom-call(s32[40]{0:T(128)} %pad_add_fusion.meta_ref, bf16[8,32,256,128]{3,2,1,0:T(8,128)(2,1)} %bitcast.17.blocks_ref, bf16[4,32,8,128]{3,2,1,0:T(8,128)(2,1)} %bitcast.174), custom_call_target="tpu_custom_call" | custom-call | flops 100000000 | bytes 33554432 | tf_op jit(solution)/shard_map/pallas_call | solution.py:128
  519.5 0.7 copy-done.16
  520.3 0.7 copy-done.17
  521.0 5.5 %shard_map.180 = bf16[32,256,8,128]{3,2,1,0:T(8,128)(2,1)} custom-call(s32[40]{0:T(128)} %pad_add_fusion.meta_ref, bf16[256,256,128]{2,1,0:T(8,128)(2,1)} %bitcast.160, bf16[6,256,128]{2,1,0:T(8,128)(2,1)} %collective-permute-done.refs_1_, bf16[6,256,128]{2,1,0:T(8,128)(2,1)} %collective-permute-done.1.refs_2_, ...), custom_call_target="tpu_custom_call", output_to_operand_aliasing={{}: (10, {})} | custom-call | flops 100000000 | bytes 6291456 | tf_op jit(solution)/shard_map/pallas_call | solution.py:106
  (94 shorter events, 4.1 us)
Async XLA Ops:
  3.8 6.5 %copy-start.20 = (bf16[128]{0:T(256)(128)(2,1)S(1)}, bf16[128]{0:T(256)(128)(2,1)}, u32[]{:S(2)}) copy-start(bf16[128]{0:T(256)(128)(2,1)} %param.25) | copy-start | bytes 772
  3.8 6.5 %copy-start = (bf16[4,32,5120]{2,1,0:T(8,128)(2,1)S(1)}, bf16[4,32,5120]{2,1,0:T(8,128)(2,1)}, u32[]{:S(2)}) copy-start(bf16[4,32,5120]{2,1,0:T(8,128)(2,1)} %param.17) | copy-start | bytes 3932164
  3.8 7.8 %copy-start.19 = (bf16[5120,1024]{1,0:T(8,128)(2,1)S(1)}, bf16[5120,1024]{1,0:T(8,128)(2,1)}, u32[]{:S(2)}) copy-start(bf16[5120,1024]{1,0:T(8,128)(2,1)} %param.23) | copy-start | bytes 31457284
  13.2 25.8 %copy-start.6 = (bf16[16,8,8,128]{3,2,1,0:T(8,128)(2,1)}, bf16[16,8,8,128]{3,2,1,0:T(8,128)(2,1)S(1)}, u32[]{:S(2)}) copy-start(bf16[16,8,8,128]{3,2,1,0:T(8,128)(2,1)S(1)} %copy.39) | copy-start | bytes 786436
  14.2 18.3 %copy-start.3 = (bf16[4,32,8,128]{3,2,1,0:T(8,128)(2,1)}, bf16[4,32,8,128]{3,2,1,0:T(8,128)(2,1)S(1)}, u32[]{:S(2)}) copy-start(bf16[4,32,8,128]{3,2,1,0:T(8,128)(2,1)S(1)} %pad_maximum_fusion.1.refs_8_) | copy-start | bytes 786436
  32.4 1.5 copy-start.1
  33.9 0.9 copy-start.21
  40.5 113.8 %all-to-all-start = ((bf16[8,28,32,128]{3,2,1,0:T(8,128)(2,1)}), bf16[8,28,32,128]{3,2,1,0:T(8,128)(2,1)S(1)}, u32[]{:S(2)}, u32[]{:S(2)}) async-start(bf16[8,28,32,128]{3,2,1,0:T(8,128)(2,1)} %pad_maximum_fusion), calls=%async_computation | async-start | bytes 3670016 | tf_op jit(solution)/shard_map/all_to_all | solution.py:237
  50.7 28.9 %collective-permute-start.21 = (bf16[8,256,128]{2,1,0:T(8,128)(2,1)S(1)}, bf16[8,256,128]{2,1,0:T(8,128)(2,1)}, u32[]{:S(2)}, u32[]{:S(2)}) collective-permute-start(bf16[8,256,128]{2,1,0:T(8,128)(2,1)S(1)} %get-tuple-element.12), channel_id=1, source_target_pairs={{0,2},{1,3},{2,0},{3,1},{4,6},{5,7},{6,4},{7,5}} | collective-permute-start | bytes 1572872 | tf_op jit(solution)/shard_map/ppermute | solution.py:223
  52.7 31.1 %collective-permute-start.22 = (bf16[8,256,128]{2,1,0:T(8,128)(2,1)}, bf16[8,256,128]{2,1,0:T(8,128)(2,1)}, u32[]{:S(2)}, u32[]{:S(2)}) collective-permute-start(bf16[8,256,128]{2,1,0:T(8,128)(2,1)} %get-tuple-element.11), channel_id=1, source_target_pairs={{0,4},{1,5},{2,6},{3,7},{4,0},{5,1},{6,2},{7,3}} | collective-permute-start | bytes 1572872 | tf_op jit(solution)/shard_map/ppermute | solution.py:223
  54.2 35.5 %collective-permute-start.23 = (bf16[8,256,128]{2,1,0:T(8,128)(2,1)}, bf16[8,256,128]{2,1,0:T(8,128)(2,1)}, u32[]{:S(2)}, u32[]{:S(2)}) collective-permute-start(bf16[8,256,128]{2,1,0:T(8,128)(2,1)} %get-tuple-element.10), channel_id=1, source_target_pairs={{0,3},{1,2},{2,1},{3,0},{4,7},{5,6},{6,5},{7,4}} | collective-permute-start | bytes 1572872 | tf_op jit(solution)/shard_map/ppermute | solution.py:223
  54.2 37.0 %collective-permute-start.24 = (bf16[8,256,128]{2,1,0:T(8,128)(2,1)}, bf16[8,256,128]{2,1,0:T(8,128)(2,1)}, u32[]{:S(2)}, u32[]{:S(2)}) collective-permute-start(bf16[8,256,128]{2,1,0:T(8,128)(2,1)} %get-tuple-element.9), channel_id=1, source_target_pairs={{0,5},{1,4},{2,7},{3,6},{4,1},{5,0},{6,3},{7,2}} | collective-permute-start | bytes 1572872 | tf_op jit(solution)/shard_map/ppermute | solution.py:223
  54.5 48.6 %collective-permute-start.25 = (bf16[8,256,128]{2,1,0:T(8,128)(2,1)}, bf16[8,256,128]{2,1,0:T(8,128)(2,1)}, u32[]{:S(2)}, u32[]{:S(2)}) collective-permute-start(bf16[8,256,128]{2,1,0:T(8,128)(2,1)} %get-tuple-element.8), channel_id=1, source_target_pairs={{0,6},{1,7},{2,4},{3,5},{4,2},{5,3},{6,0},{7,1}} | collective-permute-start | bytes 1572872 | tf_op jit(solution)/shard_map/ppermute | solution.py:223
  79.6 33.6 %collective-permute-start.26 = (bf16[8,256,128]{2,1,0:T(8,128)(2,1)}, bf16[8,256,128]{2,1,0:T(8,128)(2,1)}, u32[]{:S(2)}, u32[]{:S(2)}) collective-permute-start(bf16[8,256,128]{2,1,0:T(8,128)(2,1)} %get-tuple-element.20), channel_id=1, source_target_pairs={{0,7},{1,6},{2,5},{3,4},{4,3},{5,2},{6,1},{7,0}} | collective-permute-start | bytes 1572872 | tf_op jit(solution)/shard_map/ppermute | solution.py:223
  79.7 11.5 %copy-start.15 = (bf16[8,256,128]{2,1,0:T(8,128)(2,1)S(1)}, bf16[8,256,128]{2,1,0:T(8,128)(2,1)}, u32[]{:S(2)}) copy-start(bf16[8,256,128]{2,1,0:T(8,128)(2,1)} %get-tuple-element.7) | copy-start | bytes 1572868
  79.7 23.4 %copy-start.14 = (bf16[8,256,128]{2,1,0:T(8,128)(2,1)S(1)}, bf16[8,256,128]{2,1,0:T(8,128)(2,1)}, u32[]{:S(2)}) copy-start(bf16[8,256,128]{2,1,0:T(8,128)(2,1)} %get-tuple-element.16) | copy-start | bytes 1572868
  79.7 33.5 %copy-start.13 = (bf16[8,256,128]{2,1,0:T(8,128)(2,1)S(1)}, bf16[8,256,128]{2,1,0:T(8,128)(2,1)}, u32[]{:S(2)}) copy-start(bf16[8,256,128]{2,1,0:T(8,128)(2,1)} %get-tuple-element.15) | copy-start | bytes 1572868
  83.8 68.1 %collective-permute-start.14 = (bf16[10,256,128]{2,1,0:T(8,128)(2,1)S(1)}, bf16[10,256,128]{2,1,0:T(8,128)(2,1)S(1)}, u32[]{:S(2)}, u32[]{:S(2)}) collective-permute-start(bf16[10,256,128]{2,1,0:T(8,128)(2,1)S(1)} %get-tuple-element.27), channel_id=1, source_target_pairs={{0,2},{1,3},{2,0},{3,1},{4,6},{5,7},{6,4},{7,5}} | collective-permute-start | bytes 1966088 | tf_op jit(solution)/shard_map/ppermute | solution.py:223
  89.7 63.3 %collective-permute-start.15 = (bf16[10,256,128]{2,1,0:T(8,128)(2,1)S(1)}, bf16[10,256,128]{2,1,0:T(8,128)(2,1)S(1)}, u32[]{:S(2)}, u32[]{:S(2)}) collective-permute-start(bf16[10,256,128]{2,1,0:T(8,128)(2,1)S(1)} %get-tuple-element.26), channel_id=1, source_target_pairs={{0,4},{1,5},{2,6},{3,7},{4,0},{5,1},{6,2},{7,3}} | collective-permute-start | bytes 1966088 | tf_op jit(solution)/shard_map/ppermute | solution.py:223
  91.2 22.8 %collective-permute-start.27 = (bf16[8,256,128]{2,1,0:T(8,128)(2,1)S(1)}, bf16[8,256,128]{2,1,0:T(8,128)(2,1)S(1)}, u32[]{:S(2)}, u32[]{:S(2)}) collective-permute-start(bf16[8,256,128]{2,1,0:T(8,128)(2,1)S(1)} %copy-done.15), channel_id=1, source_target_pairs={{0,1},{1,0},{2,3},{3,2},{4,5},{5,4},{6,7},{7,6}} | collective-permute-start | bytes 1572872 | tf_op jit(solution)/shard_map/ppermute | solution.py:223
  103.1 47.0 %collective-permute-start.10 = (bf16[8,256,128]{2,1,0:T(8,128)(2,1)S(1)}, bf16[8,256,128]{2,1,0:T(8,128)(2,1)S(1)}, u32[]{:S(2)}, u32[]{:S(2)}) collective-permute-start(bf16[8,256,128]{2,1,0:T(8,128)(2,1)S(1)} %copy-done.14), channel_id=1, source_target_pairs={{0,5},{1,4},{2,7},{3,6},{4,1},{5,0},{6,3},{7,2}} | collective-permute-start | bytes 1572872 | tf_op jit(solution)/shard_map/ppermute | solution.py:223
  113.2 37.2 %collective-permute-start.11 = (bf16[8,256,128]{2,1,0:T(8,128)(2,1)S(1)}, bf16[8,256,128]{2,1,0:T(8,128)(2,1)S(1)}, u32[]{:S(2)}, u32[]{:S(2)}) collective-permute-start(bf16[8,256,128]{2,1,0:T(8,128)(2,1)S(1)} %copy-done.13), channel_id=1, source_target_pairs={{0,6},{1,7},{2,4},{3,5},{4,2},{5,3},{6,0},{7,1}} | collective-permute-start | bytes 1572872 | tf_op jit(solution)/shard_map/ppermute | solution.py:223
  114.0 39.0 %copy-start.11 = (bf16[8,256,128]{2,1,0:T(8,128)(2,1)}, bf16[8,256,128]{2,1,0:T(8,128)(2,1)S(1)}, u32[]{:S(2)}) copy-start(bf16[8,256,128]{2,1,0:T(8,128)(2,1)S(1)} %collective-permute-done.27.refs_7_) | copy-start | bytes 1572868
  114.0 119.5 %collective-permute-start.16 = (bf16[10,256,128]{2,1,0:T(8,128)(2,1)}, bf16[10,256,128]{2,1,0:T(8,128)(2,1)}, u32[]{:S(2)}, u32[]{:S(2)}) collective-permute-start(bf16[10,256,128]{2,1,0:T(8,128)(2,1)} %get-tuple-element.25), channel_id=1, source_target_pairs={{0,3},{1,2},{2,1},{3,0},{4,7},{5,6},{6,5},{7,4}} | collective-permute-start | bytes 1966088 | tf_op jit(solution)/shard_map/ppermute | solution.py:223
  150.1 2.9 copy-start.9
  150.1 86.0 %collective-permute-start.17 = (bf16[10,256,128]{2,1,0:T(8,128)(2,1)}, bf16[10,256,128]{2,1,0:T(8,128)(2,1)}, u32[]{:S(2)}, u32[]{:S(2)}) collective-permute-start(bf16[10,256,128]{2,1,0:T(8,128)(2,1)} %get-tuple-element.24), channel_id=1, source_target_pairs={{0,5},{1,4},{2,7},{3,6},{4,1},{5,0},{6,3},{7,2}} | collective-permute-start | bytes 1966088 | tf_op jit(solution)/shard_map/ppermute | solution.py:223
  150.4 2.6 copy-start.10
  150.4 86.0 %collective-permute-start.18 = (bf16[10,256,128]{2,1,0:T(8,128)(2,1)}, bf16[10,256,128]{2,1,0:T(8,128)(2,1)}, u32[]{:S(2)}, u32[]{:S(2)}) collective-permute-start(bf16[10,256,128]{2,1,0:T(8,128)(2,1)} %get-tuple-element.23), channel_id=1, source_target_pairs={{0,6},{1,7},{2,4},{3,5},{4,2},{5,3},{6,0},{7,1}} | collective-permute-start | bytes 1966088 | tf_op jit(solution)/shard_map/ppermute | solution.py:223
  151.9 1.1 copy-start.7
  151.9 85.1 %collective-permute-start.19 = (bf16[10,256,128]{2,1,0:T(8,128)(2,1)}, bf16[10,256,128]{2,1,0:T(8,128)(2,1)}, u32[]{:S(2)}, u32[]{:S(2)}) collective-permute-start(bf16[10,256,128]{2,1,0:T(8,128)(2,1)} %get-tuple-element.22), channel_id=1, source_target_pairs={{0,7},{1,6},{2,5},{3,4},{4,3},{5,2},{6,1},{7,0}} | collective-permute-start | bytes 1966088 | tf_op jit(solution)/shard_map/ppermute | solution.py:223
  153.0 0.8 copy-start.8
  153.9 83.3 %collective-permute-start.20 = (bf16[10,256,128]{2,1,0:T(8,128)(2,1)}, bf16[10,256,128]{2,1,0:T(8,128)(2,1)}, u32[]{:S(2)}, u32[]{:S(2)}) collective-permute-start(bf16[10,256,128]{2,1,0:T(8,128)(2,1)} %get-tuple-element.21), channel_id=1, source_target_pairs={{0,1},{1,0},{2,3},{3,2},{4,5},{5,4},{6,7},{7,6}} | collective-permute-start | bytes 1966088 | tf_op jit(solution)/shard_map/ppermute | solution.py:223
  154.3 1.2 copy-start.4
  230.9 2.5 copy-start.18
  230.9 7.2 %copy-start.22 = (s32[8]{0:T(128)S(1)}, s32[8]{0:T(128)}, u32[]{:S(2)}) copy-start(s32[8]{0:T(128)} %constant.109.clone) | copy-start | bytes 100
  230.9 60.5 %all-to-all-start.1 = ((bf16[8,20,32,128]{3,2,1,0:T(8,128)(2,1)}), bf16[8,20,32,128]{3,2,1,0:T(8,128)(2,1)S(1)}, u32[]{:S(2)}, u32[]{:S(2)}) async-start(bf16[8,20,32,128]{3,2,1,0:T(8,128)(2,1)} %shard_map.175), calls=%async_computation.1 | async-start | bytes 2621440 | tf_op jit(solution)/shard_map/all_to_all | solution.py:240
  233.5 28.8 %collective-permute-start.12 = (bf16[8,256,128]{2,1,0:T(8,128)(2,1)}, bf16[8,256,128]{2,1,0:T(8,128)(2,1)S(1)}, u32[]{:S(2)}, u32[]{:S(2)}) collective-permute-start(bf16[8,256,128]{2,1,0:T(8,128)(2,1)} %get-tuple-element.14), channel_id=1, source_target_pairs={{0,7},{1,6},{2,5},{3,4},{4,3},{5,2},{6,1},{7,0}} | collective-permute-start | bytes 1572872 | tf_op jit(solution)/shard_map/ppermute | solution.py:223
  236.0 26.8 %collective-permute-start.13 = (bf16[8,256,128]{2,1,0:T(8,128)(2,1)}, bf16[8,256,128]{2,1,0:T(8,128)(2,1)}, u32[]{:S(2)}, u32[]{:S(2)}) collective-permute-start(bf16[8,256,128]{2,1,0:T(8,128)(2,1)} %get-tuple-element.13), channel_id=1, source_target_pairs={{0,1},{1,0},{2,3},{3,2},{4,5},{5,4},{6,7},{7,6}} | collective-permute-start | bytes 1572872 | tf_op jit(solution)/shard_map/ppermute | solution.py:223
  236.4 37.3 %collective-permute-start.7 = (bf16[8,256,128]{2,1,0:T(8,128)(2,1)}, bf16[8,256,128]{2,1,0:T(8,128)(2,1)}, u32[]{:S(2)}, u32[]{:S(2)}) collective-permute-start(bf16[8,256,128]{2,1,0:T(8,128)(2,1)} %get-tuple-element.19), channel_id=1, source_target_pairs={{0,2},{1,3},{2,0},{3,1},{4,6},{5,7},{6,4},{7,5}} | collective-permute-start | bytes 1572872 | tf_op jit(solution)/shard_map/ppermute | solution.py:223
  237.0 36.8 %collective-permute-start.8 = (bf16[8,256,128]{2,1,0:T(8,128)(2,1)}, bf16[8,256,128]{2,1,0:T(8,128)(2,1)}, u32[]{:S(2)}, u32[]{:S(2)}) collective-permute-start(bf16[8,256,128]{2,1,0:T(8,128)(2,1)} %get-tuple-element.18), channel_id=1, source_target_pairs={{0,4},{1,5},{2,6},{3,7},{4,0},{5,1},{6,2},{7,3}} | collective-permute-start | bytes 1572872 | tf_op jit(solution)/shard_map/ppermute | solution.py:223
  237.1 46.7 %collective-permute-start.9 = (bf16[8,256,128]{2,1,0:T(8,128)(2,1)}, bf16[8,256,128]{2,1,0:T(8,128)(2,1)}, u32[]{:S(2)}, u32[]{:S(2)}) collective-permute-start(bf16[8,256,128]{2,1,0:T(8,128)(2,1)} %get-tuple-element.17), channel_id=1, source_target_pairs={{0,3},{1,2},{2,1},{3,0},{4,7},{5,6},{6,5},{7,4}} | collective-permute-start | bytes 1572872 | tf_op jit(solution)/shard_map/ppermute | solution.py:223
  262.3 23.2 %copy-start.12 = (bf16[8,256,128]{2,1,0:T(8,128)(2,1)}, bf16[8,256,128]{2,1,0:T(8,128)(2,1)S(1)}, u32[]{:S(2)}) copy-start(bf16[8,256,128]{2,1,0:T(8,128)(2,1)S(1)} %collective-permute-done.12.refs_6_) | copy-start | bytes 1572868
  262.3 180.3 %collective-permute-start = (bf16[6,256,128]{2,1,0:T(8,128)(2,1)}, bf16[6,256,128]{2,1,0:T(8,128)(2,1)}, u32[]{:S(2)}, u32[]{:S(2)}) collective-permute-start(bf16[6,256,128]{2,1,0:T(8,128)(2,1)} %get-tuple-element.34), channel_id=1, source_target_pairs={{0,2},{1,3},{2,0},{3,1},{4,6},{5,7},{6,4},{7,5}} | collective-permute-start | bytes 1179656 | tf_op jit(solution)/shard_map/ppermute | solution.py:223
  262.9 182.2 %collective-permute-start.1 = (bf16[6,256,128]{2,1,0:T(8,128)(2,1)}, bf16[6,256,128]{2,1,0:T(8,128)(2,1)}, u32[]{:S(2)}, u32[]{:S(2)}) collective-permute-start(bf16[6,256,128]{2,1,0:T(8,128)(2,1)} %get-tuple-element.33), channel_id=1, source_target_pairs={{0,4},{1,5},{2,6},{3,7},{4,0},{5,1},{6,2},{7,3}} | collective-permute-start | bytes 1179656 | tf_op jit(solution)/shard_map/ppermute | solution.py:223
  273.7 245.7 %collective-permute-start.2 = (bf16[6,256,128]{2,1,0:T(8,128)(2,1)}, bf16[6,256,128]{2,1,0:T(8,128)(2,1)}, u32[]{:S(2)}, u32[]{:S(2)}) collective-permute-start(bf16[6,256,128]{2,1,0:T(8,128)(2,1)} %get-tuple-element.32), channel_id=1, source_target_pairs={{0,3},{1,2},{2,1},{3,0},{4,7},{5,6},{6,5},{7,4}} | collective-permute-start | bytes 1179656 | tf_op jit(solution)/shard_map/ppermute | solution.py:223
  273.8 245.7 %collective-permute-start.3 = (bf16[6,256,128]{2,1,0:T(8,128)(2,1)}, bf16[6,256,128]{2,1,0:T(8,128)(2,1)}, u32[]{:S(2)}, u32[]{:S(2)}) collective-permute-start(bf16[6,256,128]{2,1,0:T(8,128)(2,1)} %get-tuple-element.31), channel_id=1, source_target_pairs={{0,5},{1,4},{2,7},{3,6},{4,1},{5,0},{6,3},{7,2}} | collective-permute-start | bytes 1179656 | tf_op jit(solution)/shard_map/ppermute | solution.py:223
  283.8 235.6 %collective-permute-start.4 = (bf16[6,256,128]{2,1,0:T(8,128)(2,1)}, bf16[6,256,128]{2,1,0:T(8,128)(2,1)}, u32[]{:S(2)}, u32[]{:S(2)}) collective-permute-start(bf16[6,256,128]{2,1,0:T(8,128)(2,1)} %get-tuple-element.30), channel_id=1, source_target_pairs={{0,6},{1,7},{2,4},{3,5},{4,2},{5,3},{6,0},{7,1}} | collective-permute-start | bytes 1179656 | tf_op jit(solution)/shard_map/ppermute | solution.py:223
  291.4 1.1 copy-start.5
  292.5 211.1 %all-to-all-start.2 = ((bf16[256,256,128]{2,1,0:T(8,128)(2,1)}), bf16[256,256,128]{2,1,0:T(8,128)(2,1)}, u32[]{:S(2)}, u32[]{:S(2)}) async-start(bf16[256,256,128]{2,1,0:T(8,128)(2,1)} %bitcast.162), calls=%async_computation.2 | async-start | bytes 33554432 | tf_op jit(solution)/shard_map/all_to_all | solution.py:239
  322.1 60.0 %copy-start.2 = (f32[4,32,5120]{2,1,0:T(8,128)S(1)}, f32[4,32,5120]{2,1,0:T(8,128)}, u32[]{:S(2)}) copy-start(f32[4,32,5120]{2,1,0:T(8,128)} %get-tuple-element.42) | copy-start | bytes 7864324
  442.5 77.0 %collective-permute-start.5 = (bf16[6,256,128]{2,1,0:T(8,128)(2,1)}, bf16[6,256,128]{2,1,0:T(8,128)(2,1)S(1)}, u32[]{:S(2)}, u32[]{:S(2)}) collective-permute-start(bf16[6,256,128]{2,1,0:T(8,128)(2,1)} %get-tuple-element.29), channel_id=1, source_target_pairs={{0,7},{1,6},{2,5},{3,4},{4,3},{5,2},{6,1},{7,0}} | collective-permute-start | bytes 1179656 | tf_op jit(solution)/shard_map/ppermute | solution.py:223
  445.1 74.4 %collective-permute-start.6 = (bf16[6,256,128]{2,1,0:T(8,128)(2,1)}, bf16[6,256,128]{2,1,0:T(8,128)(2,1)S(1)}, u32[]{:S(2)}, u32[]{:S(2)}) collective-permute-start(bf16[6,256,128]{2,1,0:T(8,128)(2,1)} %get-tuple-element.28), channel_id=1, source_target_pairs={{0,1},{1,0},{2,3},{3,2},{4,5},{5,4},{6,7},{7,6}} | collective-permute-start | bytes 1179656 | tf_op jit(solution)/shard_map/ppermute | solution.py:223
  519.5 0.8 copy-start.16
  520.2 0.7 copy-start.17

commit v2 on v1

--- a/solution.py
+++ b/solution.py
@@ -57,7 +57,7 @@
 
 ROW_PAD = 9
 MERGE_ROWS = 4
-K_CUTS = (8, 18, 26, 32)
+K_CUTS = (8, 16, 28, 32)
 SWAP_ORDER = (2, 4, 3, 5, 6, 7, 1)
 
 
@@ -124,7 +124,7 @@
 def merge_all(blocks, fresh_rows, meta):
     n_dev, num_rows, num_slots, head_dim = blocks.shape
     n_steps = fresh_rows.shape[0]
-    step_rows = math.gcd(num_rows, MERGE_ROWS)
+    step_rows = math.gcd(num_rows, 2 * MERGE_ROWS)
     return pl.pallas_call(
         functools.partial(merge_all_kernel, n_dev),
         out_shape=jax.ShapeDtypeStruct((num_rows, num_slots, n_dev, head_dim), blocks.dtype),
@@ -184,7 +184,7 @@
     n_dev, num_sent, num_rows, head_dim = got.shape
     num_slots = k_own.shape[1]
     num_q = num_sent - 2 * n_steps
-    step_rows = 8
+    step_rows = num_rows
     inner = num_rows // step_rows
     pad_q = num_sent + n_steps
     stride = num_sent + 1 - num_sent % 2
@@ -226,7 +226,6 @@
             return [swap(lax.dynamic_slice_in_dim(own, jnp.bitwise_xor(me, rel_idx) * num_rows + row_base, chunk_rows), rel_idx) for rel_idx in SWAP_ORDER]
 
         cuts_k = cuts(num_rows, K_CUTS)
-        k_got = [swap_cache(k_own, *c) for c in cuts_k]
         positions = my_pos[None, :] + jnp.arange(n_steps)[:, None]
         queries, keys_new, values_new = project(hidden_in, positions, attn_norm, w_q, w_k, w_v, q_norm, k_norm)
         group = queries.shape[2] // n_dev
@@ -234,6 +233,8 @@
         k_send = keys_new.transpose(2, 0, 1, 3)
         v_send = values_new.transpose(2, 0, 1, 3)
         sent = jnp.concatenate([q_send, k_send, v_send], axis=1)
+        k_later, sent = lax.optimization_barrier((k_own, sent))
+        k_got = [swap_cache(k_later if i else k_own, *c) for i, c in enumerate(cuts_k)]
         got = lax.all_to_all(sent, 'x', 0, 0, tiled=True)
         mixed = attend_local(got, k_own, v_own, start_pos, n_steps)
         v_got = lax.all_to_all(v_own, 'x', 0, 0, tiled=True).reshape(n_dev, num_rows, num_slots, head_dim)
@@ -243,6 +244,8 @@
         meta = jnp.concatenate([jnp.bitwise_xor(me, jnp.array((0,) + SWAP_ORDER)), my_pos]).astype(jnp.int32)
         k_out, v_out = None, merge_all(v_got, values_new, meta)
         for chunk_idx, ((row_base, chunk_rows), k_blocks) in enumerate(zip(cuts_k, k_got)):
+            if chunk_idx == 2:
+                meta, out_hidden = lax.optimization_barrier((meta, out_hidden))
             if chunk_idx == len(cuts_k) - 1:
                 meta, v_out = lax.optimization_barrier((meta, v_out))
             k_out = merge_chunk(k_own, k_blocks, keys_new, meta, k_out, row_base, num_rows)

time: 528 us -> 561 us (1.062)
  waiting for transfers between devices: 108 us -> 146 us
  Pallas kernels: 115 us -> 108 us
    ppermute x28, waiting for transfers between devices: 108 us -> 132 us  [swap(): return lax.ppermute(arr, 'x', [(d, d ^ rel_idx) for d in range(n_dev)])]
    all_to_all x1, waiting for transfers between devices: 0.01 us -> 13.9 us  [local_run(): got = lax.all_to_all(sent, 'x', 0, 0, tiled=True)]
    dynamic_slice x3 -> x4, local copies, waits for them, and re-layouts: 13.3 us -> 15.5 us  [swap_cache(): lax.dynamic_slice_in_dim(own, jnp.bitwise_xor(me, rel_idx) * num_rows + r...]
  transfers between devices with their start and end apart: 31 -> 31, of which waited for: 8 -> 7; matrix products, arithmetic and copies ran while one was open for 41% -> 39% of each run, Pallas kernels for 21% -> 18%
where the time goes in v2:
time: 561 us
  matrix products  229 us (41%)
  waiting for transfers between devices  146 us (26%)
  Pallas kernels  108 us (19%)
  starting transfers between devices  40.8 us (7%)
  local copies, waits for them, and re-layouts  26.6 us (5%)
  other arithmetic  10.2 us (2%)
    ppermute x28, waiting for transfers between devices, swap(): return lax.ppermute(arr, 'x', [(d, d ^ rel_idx) for d in range(n_dev)])  132 us
    pallas_call x1, Pallas kernels, attend_local(): pl.pallas_call(functools.partial(attend_kernel, n_steps, head_dim ** (-0....  72.6 us
    dot_general x1, matrix products, finish(): jnp.einsum('sbd,df->sbf', normed, w_up, preferred_element_type=jnp.float32)  60.5 us
    dot_general x1, matrix products, finish(): jnp.einsum('sbd,df->sbf', normed, w_gate, preferred_element_type=jnp.floa...  60 us
    dot_general x1, matrix products, finish(): jnp.einsum('sbf,fd->sbd', activated, w_down, preferred_element_type=jnp.f...  58.1 us
    ppermute x28, starting transfers between devices, swap(): return lax.ppermute(arr, 'x', [(d, d ^ rel_idx) for d in range(n_dev)])  29.8 us
    pallas_call x4, Pallas kernels, merge_chunk(): pl.pallas_call(functools.partial(merge_chunk_kernel, row_base, n_dev), ou...  21.3 us
    dot_general x1, matrix products, finish(): jnp.einsum('sbe,ed->sbd', flat_attn, w_o, preferred_element_type=jnp.floa...  20.8 us
  transfers between devices with their start and end apart: 31, of which 7 were waited for; matrix products, arithmetic and copies ran while one was open for 39% of the time, Pallas kernels for 18%

profile of v2, /device:TPU:0, one launch (start us, length us, event | category | flops | bytes accessed | tf_op | source)
XLA Modules:
  0.0 560.7 jit_solution(15732326441117906950)
XLA Ops:
  0.7 0.8 dynamic_slice.101
  1.4 0.7 convert_element_type.52
  2.1 1.7 fusion.47
  3.8 6.0 %fusion.20 = f32[4,32,1024]{2,1,0:T(8,128)S(1)} fusion(bf16[5120,1024]{1,0:T(8,128)(2,1)} %param.22, bf16[4,32,5120]{2,1,0:T(8,128)(2,1)} %param.17, f32[5120]{0:T(1024)S(1)} %convert_element_type.52, f32[4,32]{1,0:T(4,128)S(1)} %add_rsqrt_fusion.3), kind=kOutput, calls=%fused_computation.14 | convolution fusion | flops 1344798720 | bytes 12341760 | tf_op jit(solution)/shard_map/sbd,de->sbe/dot_general | solution.py:38
  11.2 18.2 %fusion.8 = f32[4,32,5120]{2,1,0:T(8,128)S(1)} fusion(bf16[5120,5120]{1,0:T(8,128)(2,1)} %param.21, bf16[4,32,5120]{2,1,0:T(8,128)(2,1)S(1)} %copy-done, f32[5120]{0:T(1024)S(1)} %convert_element_type.52, f32[4,32]{1,0:T(4,128)S(1)} %add_rsqrt_fusion.3), kind=kOutput, calls=%fused_computation.8 | convolution fusion | flops 6713507840 | bytes 56381952 | tf_op jit(solution)/shard_map/sbd,de->sbe/dot_general | solution.py:37
  29.4 0.5 copy.37
  29.9 1.0 copy-done.1
  30.9 0.7 fusion.50
  31.8 2.2 fusion.51
  33.9 0.9 subtract_convert_fusion
  34.9 0.7 maximum_bitcast_fusion
  35.9 5.5 fusion.58
  41.5 0.7 copy-done.6
  42.3 1.4 pad_maximum_fusion
  43.7 4.3 all-to-all-start
  48.0 3.9 dynamic-slice_bitcast_fusion
  51.9 2.0 collective-permute-start.21
  53.9 1.5 collective-permute-start.22
  55.6 2.9 collective-permute-start.25
  58.6 13.9 %all-to-all-done.sent_ref = bf16[8,28,32,128]{3,2,1,0:T(8,128)(2,1)S(1)} async-done(((bf16[8,28,32,128]{3,2,1,0:T(8,128)(2,1)}), bf16[8,28,32,128]{3,2,1,0:T(8,128)(2,1)S(1)}, u32[]{:S(2)}, u32[]{:S(2)}) %all-to-all-start) | async-done | bytes 1835040 | tf_op jit(solution)/shard_map/all_to_all | solution.py:238
  72.4 1.2 copy-done.4
  73.6 72.6 %shard_map.175 = bf16[8,20,32,128]{3,2,1,0:T(8,128)(2,1)} custom-call(s32[256]{0:T(256)} %pos_ref.1, bf16[8,28,32,128]{3,2,1,0:T(8,128)(2,1)} %copy-done.4, bf16[256,256,128]{2,1,0:T(8,128)(2,1)} %bitcast.114, bf16[256,256,128]{2,1,0:T(8,128)(2,1)} %bitcast.122), custom_call_target="tpu_custom_call" | custom-call | flops 1000000000 | bytes 33554432 | tf_op jit(solution)/shard_map/pallas_call | solution.py:192
  146.2 2.3 all-to-all-start.1
  148.6 3.9 constant_dynamic-slice_fusion
  152.5 2.6 collective-permute-start.26
  155.1 0.4 collective-permute-start.27
  155.5 0.5 collective-permute-start.14
  156.2 1.1 collective-permute-start.16
  157.2 20.3 %collective-permute-done.26.refs_6_ = bf16[8,256,128]{2,1,0:T(8,128)(2,1)} collective-permute-done((bf16[8,256,128]{2,1,0:T(8,128)(2,1)}, bf16[8,256,128]{2,1,0:T(8,128)(2,1)}, u32[]{:S(2)}, u32[]{:S(2)}) %collective-permute-start.26) | collective-permute-done | bytes 524320 | tf_op jit(solution)/shard_map/ppermute | solution.py:223
  177.6 1.0 collective-permute-start.17
  178.6 1.5 collective-permute-start.18
  180.1 8.7 %collective-permute-done.14.refs_1_ = bf16[8,256,128]{2,1,0:T(8,128)(2,1)S(1)} collective-permute-done((bf16[8,256,128]{2,1,0:T(8,128)(2,1)}, bf16[8,256,128]{2,1,0:T(8,128)(2,1)S(1)}, u32[]{:S(2)}, u32[]{:S(2)}) %collective-permute-start.14) | collective-permute-done | bytes 524320 | tf_op jit(solution)/shard_map/ppermute | solution.py:223
  189.0 1.4 collective-permute-start.20
  190.5 0.6 pad_add_fusion.meta_ref
  191.1 2.7 constant_dynamic-slice_fusion.14
  193.8 5.0 constant_dynamic-slice_fusion.7
  198.8 4.8 shard_map.177.refs_9_
  203.6 2.5 collective-permute-start.11
  206.1 6.3 %collective-permute-done.18.refs_5_ = bf16[8,256,128]{2,1,0:T(8,128)(2,1)} collective-permute-done((bf16[8,256,128]{2,1,0:T(8,128)(2,1)}, bf16[8,256,128]{2,1,0:T(8,128)(2,1)}, u32[]{:S(2)}, u32[]{:S(2)}) %collective-permute-start.18) | collective-permute-done | bytes 524320 | tf_op jit(solution)/shard_map/ppermute | solution.py:223
  212.4 10.1 %collective-permute-done.19.refs_6_ = bf16[8,256,128]{2,1,0:T(8,128)(2,1)} collective-permute-done((bf16[8,256,128]{2,1,0:T(8,128)(2,1)}, bf16[8,256,128]{2,1,0:T(8,128)(2,1)}, u32[]{:S(2)}, u32[]{:S(2)}) %collective-permute-start.19) | collective-permute-done | bytes 524320 | tf_op jit(solution)/shard_map/ppermute | solution.py:223
  222.5 0.6 collective-permute-start
  223.1 0.7 collective-permute-start.1
  223.8 4.8 shard_map.178.refs_9_
  228.6 1.0 copy-done.5
  229.7 4.5 all-to-all-start.2
  234.2 2.0 copy.42
  236.2 2.3 reshape_reshape.3
  238.5 20.8 %multiply_reduce_fusion = (f32[4,32]{1,0:T(4,128)S(1)}, f32[4,32,5120]{2,1,0:T(8,128)}) fusion(bf16[4,32,5120]{2,1,0:T(8,128)(2,1)} %reshape_reshape.3, bf16[5120,5120]{1,0:T(8,128)(2,1)} %param.26, bf16[4,32,5120]{2,1,0:T(8,128)(2,1)S(1)} %copy-done), kind=kOutput, calls=%fused_computation.37 | convolution fusion | flops 6714818560 | bytes 57672192 | tf_op jit(solution)/shard_map/sbe,ed->sbd/dot_general | solution.py:48
  259.3 60.0 %fusion.4 = f32[4,32,17408]{2,1,0:T(8,128)} fusion(bf16[5120,17408]{1,0:T(8,128)(2,1)} %param.28, f32[4,32,5120]{2,1,0:T(8,128)} %get-tuple-element.50, f32[5120]{0:T(1024)S(1)} %convert_element_type.61, f32[4,32]{1,0:T(4,128)S(1)} %add_rsqrt_fusion.2), kind=kOutput, calls=%fused_computation.4 | convolution fusion | flops 22818979840 | bytes 189813248 | tf_op jit(solution)/shard_map/sbd,df->sbf/dot_general | solution.py:51
  319.2 0.4 collective-permute-start.13
  319.6 5.1 collective-permute-start.7
  324.7 0.4 collective-permute-start.8
  325.1 60.5 %fusion.13.clone.8 = bf16[4,32,17408]{2,1,0:T(8,128)(2,1)} fusion(bf16[5120,17408]{1,0:T(8,128)(2,1)} %param.29, f32[4,32,17408]{2,1,0:T(8,128)} %fusion.4, f32[4,32,5120]{2,1,0:T(8,128)S(1)} %copy-done.2, f32[5120]{0:T(1024)S(1)} %convert_element_type.61, f32[4,32]{1,0:T(4,128)S(1)} %add_rsqrt_fusion.2), kind=kOutput, calls=%fused_computation.11.clone.clone.clone.clone.clone.clone.clone.1 | convolution fusion | flops 22832349184 | bytes 194269696 | tf_op jit(solution)/shard_map/sbd,df->sbf/dot_general | solution.py:52
  385.6 1.7 collective-permute-start.2
  387.3 0.8 collective-permute-start.3
  388.1 70.6 %collective-permute-done.7.refs_1_ = bf16[12,256,128]{2,1,0:T(8,128)(2,1)} collective-permute-done((bf16[12,256,128]{2,1,0:T(8,128)(2,1)}, bf16[12,256,128]{2,1,0:T(8,128)(2,1)}, u32[]{:S(2)}, u32[]{:S(2)}) %collective-permute-start.7) | collective-permute-done | bytes 786464 | tf_op jit(solution)/shard_map/ppermute | solution.py:223
  458.7 1.5 collective-permute-start.4
  460.2 15.6 %collective-permute-done.8.refs_2_ = bf16[12,256,128]{2,1,0:T(8,128)(2,1)} collective-permute-done((bf16[12,256,128]{2,1,0:T(8,128)(2,1)}, bf16[12,256,128]{2,1,0:T(8,128)(2,1)}, u32[]{:S(2)}, u32[]{:S(2)}) %collective-permute-start.8) | collective-permute-done | bytes 786464 | tf_op jit(solution)/shard_map/ppermute | solution.py:223
  475.9 0.4 collective-permute-start.6
  476.3 58.1 %fusion.41 = bf16[4,32,5120]{2,1,0:T(8,128)(2,1)} fusion(f32[4,32,5120]{2,1,0:T(8,128)S(1)} %copy-done.2, bf16[17408,5120]{1,0:T(8,128)(2,1)} %param.30, bf16[4,32,17408]{2,1,0:T(8,128)(2,1)} %fusion.13.clone.8), kind=kOutput, calls=%fused_computation.25 | convolution fusion | flops 22818324480 | bytes 186646528 | tf_op jit(solution)/shard_map/sbf,fd->sbd/dot_general | solution.py:54
  534.4 7.7 %shard_map.179.refs_9_ = bf16[32,256,8,128]{3,2,1,0:T(8,128)(2,1)} custom-call(s32[40]{0:T(128)} %pad_add_fusion.meta_ref, bf16[256,256,128]{2,1,0:T(8,128)(2,1)} %bitcast.120, bf16[12,256,128]{2,1,0:T(8,128)(2,1)} %collective-permute-done.7.refs_1_, bf16[12,256,128]{2,1,0:T(8,128)(2,1)} %collective-permute-done.8.refs_2_, ...), custom_call_target="tpu_custom_call", output_to_operand_aliasing={{}: (10, {})} | custom-call | flops 100000000 | bytes 12582912 | tf_op jit(solution)/shard_map/pallas_call | solution.py:106
  542.1 13.6 %shard_map.176 = bf16[32,256,8,128]{3,2,1,0:T(8,128)(2,1)} custom-call(s32[40]{0:T(128)} %pad_add_fusion.meta_ref, bf16[8,32,256,128]{3,2,1,0:T(8,128)(2,1)} %bitcast.17.blocks_ref, bf16[4,32,8,128]{3,2,1,0:T(8,128)(2,1)} %bitcast.135), custom_call_target="tpu_custom_call" | custom-call | flops 100000000 | bytes 33554432 | tf_op jit(solution)/shard_map/pallas_call | solution.py:128
  555.8 0.6 copy-done.8
  556.7 4.0 shard_map.180
  (79 shorter events, 2.9 us)
Async XLA Ops:
  3.8 6.3 %copy-start.12 = (bf16[128]{0:T(256)(128)(2,1)S(1)}, bf16[128]{0:T(256)(128)(2,1)}, u32[]{:S(2)}) copy-start(bf16[128]{0:T(256)(128)(2,1)} %param.25) | copy-start | bytes 772
  9.9 1.3 copy-start
  11.1 18.3 %copy-start.3 = (bf16[4,32,8,128]{3,2,1,0:T(8,128)(2,1)}, bf16[4,32,8,128]{3,2,1,0:T(8,128)(2,1)S(1)}, u32[]{:S(2)}) copy-start(bf16[4,32,8,128]{3,2,1,0:T(8,128)(2,1)S(1)} %pad_maximum_fusion.1.refs_8_) | copy-start | bytes 786436
  29.4 1.5 copy-start.1
  30.9 0.9 copy-start.13
  41.5 0.7 copy-start.6
  43.7 28.7 %all-to-all-start = ((bf16[8,28,32,128]{3,2,1,0:T(8,128)(2,1)}), bf16[8,28,32,128]{3,2,1,0:T(8,128)(2,1)S(1)}, u32[]{:S(2)}, u32[]{:S(2)}) async-start(bf16[8,28,32,128]{3,2,1,0:T(8,128)(2,1)} %pad_maximum_fusion), calls=%async_computation | async-start | bytes 3670016 | tf_op jit(solution)/shard_map/all_to_all | solution.py:238
  51.9 100.6 %collective-permute-start.21 = (bf16[8,256,128]{2,1,0:T(8,128)(2,1)}, bf16[8,256,128]{2,1,0:T(8,128)(2,1)}, u32[]{:S(2)}, u32[]{:S(2)}) collective-permute-start(bf16[8,256,128]{2,1,0:T(8,128)(2,1)} %get-tuple-element.20), channel_id=1, source_target_pairs={{0,2},{1,3},{2,0},{3,1},{4,6},{5,7},{6,4},{7,5}} | collective-permute-start | bytes 1572872 | tf_op jit(solution)/shard_map/ppermute | solution.py:223
  53.9 101.2 %collective-permute-start.22 = (bf16[8,256,128]{2,1,0:T(8,128)(2,1)}, bf16[8,256,128]{2,1,0:T(8,128)(2,1)}, u32[]{:S(2)}, u32[]{:S(2)}) collective-permute-start(bf16[8,256,128]{2,1,0:T(8,128)(2,1)} %get-tuple-element.19), channel_id=1, source_target_pairs={{0,4},{1,5},{2,6},{3,7},{4,0},{5,1},{6,2},{7,3}} | collective-permute-start | bytes 1572872 | tf_op jit(solution)/shard_map/ppermute | solution.py:223
  55.4 100.1 %collective-permute-start.23 = (bf16[8,256,128]{2,1,0:T(8,128)(2,1)}, bf16[8,256,128]{2,1,0:T(8,128)(2,1)}, u32[]{:S(2)}, u32[]{:S(2)}) collective-permute-start(bf16[8,256,128]{2,1,0:T(8,128)(2,1)} %get-tuple-element.18), channel_id=1, source_target_pairs={{0,3},{1,2},{2,1},{3,0},{4,7},{5,6},{6,5},{7,4}} | collective-permute-start | bytes 1572872 | tf_op jit(solution)/shard_map/ppermute | solution.py:223
  55.4 100.7 %collective-permute-start.24 = (bf16[8,256,128]{2,1,0:T(8,128)(2,1)}, bf16[8,256,128]{2,1,0:T(8,128)(2,1)}, u32[]{:S(2)}, u32[]{:S(2)}) collective-permute-start(bf16[8,256,128]{2,1,0:T(8,128)(2,1)} %get-tuple-element.17), channel_id=1, source_target_pairs={{0,5},{1,4},{2,7},{3,6},{4,1},{5,0},{6,3},{7,2}} | collective-permute-start | bytes 1572872 | tf_op jit(solution)/shard_map/ppermute | solution.py:223
  55.6 100.5 %collective-permute-start.25 = (bf16[8,256,128]{2,1,0:T(8,128)(2,1)}, bf16[8,256,128]{2,1,0:T(8,128)(2,1)}, u32[]{:S(2)}, u32[]{:S(2)}) collective-permute-start(bf16[8,256,128]{2,1,0:T(8,128)(2,1)} %get-tuple-element.16), channel_id=1, source_target_pairs={{0,6},{1,7},{2,4},{3,5},{4,2},{5,3},{6,0},{7,1}} | collective-permute-start | bytes 1572872 | tf_op jit(solution)/shard_map/ppermute | solution.py:223
  72.4 1.2 copy-start.4
  146.2 82.3 %all-to-all-start.1 = ((bf16[8,20,32,128]{3,2,1,0:T(8,128)(2,1)}), bf16[8,20,32,128]{3,2,1,0:T(8,128)(2,1)S(1)}, u32[]{:S(2)}, u32[]{:S(2)}) async-start(bf16[8,20,32,128]{3,2,1,0:T(8,128)(2,1)} %shard_map.175), calls=%async_computation.1 | async-start | bytes 2621440 | tf_op jit(solution)/shard_map/all_to_all | solution.py:241
  148.6 7.6 %copy-start.11 = (bf16[5120]{0:T(1024)(128)(2,1)S(1)}, bf16[5120]{0:T(1024)(128)(2,1)}, u32[]{:S(2)}) copy-start(bf16[5120]{0:T(1024)(128)(2,1)} %param.27) | copy-start | bytes 30724
  148.6 7.6 %copy-start.14 = (s32[8]{0:T(128)S(1)}, s32[8]{0:T(128)}, u32[]{:S(2)}) copy-start(s32[8]{0:T(128)} %constant.88.clone) | copy-start | bytes 100
  152.5 25.1 %collective-permute-start.26 = (bf16[8,256,128]{2,1,0:T(8,128)(2,1)}, bf16[8,256,128]{2,1,0:T(8,128)(2,1)}, u32[]{:S(2)}, u32[]{:S(2)}) collective-permute-start(bf16[8,256,128]{2,1,0:T(8,128)(2,1)} %get-tuple-element.21), channel_id=1, source_target_pairs={{0,7},{1,6},{2,5},{3,4},{4,3},{5,2},{6,1},{7,0}} | collective-permute-start | bytes 1572872 | tf_op jit(solution)/shard_map/ppermute | solution.py:223
  155.1 23.5 %collective-permute-start.27 = (bf16[8,256,128]{2,1,0:T(8,128)(2,1)}, bf16[8,256,128]{2,1,0:T(8,128)(2,1)}, u32[]{:S(2)}, u32[]{:S(2)}) collective-permute-start(bf16[8,256,128]{2,1,0:T(8,128)(2,1)} %get-tuple-element.15), channel_id=1, source_target_pairs={{0,1},{1,0},{2,3},{3,2},{4,5},{5,4},{6,7},{7,6}} | collective-permute-start | bytes 1572872 | tf_op jit(solution)/shard_map/ppermute | solution.py:223
  155.5 33.4 %collective-permute-start.14 = (bf16[8,256,128]{2,1,0:T(8,128)(2,1)}, bf16[8,256,128]{2,1,0:T(8,128)(2,1)S(1)}, u32[]{:S(2)}, u32[]{:S(2)}) collective-permute-start(bf16[8,256,128]{2,1,0:T(8,128)(2,1)} %get-tuple-element.28), channel_id=1, source_target_pairs={{0,2},{1,3},{2,0},{3,1},{4,6},{5,7},{6,4},{7,5}} | collective-permute-start | bytes 1572872 | tf_op jit(solution)/shard_map/ppermute | solution.py:223
  156.0 33.0 %collective-permute-start.15 = (bf16[8,256,128]{2,1,0:T(8,128)(2,1)}, bf16[8,256,128]{2,1,0:T(8,128)(2,1)}, u32[]{:S(2)}, u32[]{:S(2)}) collective-permute-start(bf16[8,256,128]{2,1,0:T(8,128)(2,1)} %get-tuple-element.27), channel_id=1, source_target_pairs={{0,4},{1,5},{2,6},{3,7},{4,0},{5,1},{6,2},{7,3}} | collective-permute-start | bytes 1572872 | tf_op jit(solution)/shard_map/ppermute | solution.py:223
  156.2 47.4 %collective-permute-start.16 = (bf16[8,256,128]{2,1,0:T(8,128)(2,1)}, bf16[8,256,128]{2,1,0:T(8,128)(2,1)}, u32[]{:S(2)}, u32[]{:S(2)}) collective-permute-start(bf16[8,256,128]{2,1,0:T(8,128)(2,1)} %get-tuple-element.26), channel_id=1, source_target_pairs={{0,3},{1,2},{2,1},{3,0},{4,7},{5,6},{6,5},{7,4}} | collective-permute-start | bytes 1572872 | tf_op jit(solution)/shard_map/ppermute | solution.py:223
  177.6 26.1 %collective-permute-start.17 = (bf16[8,256,128]{2,1,0:T(8,128)(2,1)}, bf16[8,256,128]{2,1,0:T(8,128)(2,1)}, u32[]{:S(2)}, u32[]{:S(2)}) collective-permute-start(bf16[8,256,128]{2,1,0:T(8,128)(2,1)} %get-tuple-element.25), channel_id=1, source_target_pairs={{0,5},{1,4},{2,7},{3,6},{4,1},{5,0},{6,3},{7,2}} | collective-permute-start | bytes 1572872 | tf_op jit(solution)/shard_map/ppermute | solution.py:223
  178.6 33.8 %collective-permute-start.18 = (bf16[8,256,128]{2,1,0:T(8,128)(2,1)}, bf16[8,256,128]{2,1,0:T(8,128)(2,1)}, u32[]{:S(2)}, u32[]{:S(2)}) collective-permute-start(bf16[8,256,128]{2,1,0:T(8,128)(2,1)} %get-tuple-element.24), channel_id=1, source_target_pairs={{0,6},{1,7},{2,4},{3,5},{4,2},{5,3},{6,0},{7,1}} | collective-permute-start | bytes 1572872 | tf_op jit(solution)/shard_map/ppermute | solution.py:223
  188.8 10.0 %copy-start.7 = (bf16[8,256,128]{2,1,0:T(8,128)(2,1)}, bf16[8,256,128]{2,1,0:T(8,128)(2,1)S(1)}, u32[]{:S(2)}) copy-start(bf16[8,256,128]{2,1,0:T(8,128)(2,1)S(1)} %collective-permute-done.14.refs_1_) | copy-start | bytes 1572868
  188.8 33.7 %collective-permute-start.19 = (bf16[8,256,128]{2,1,0:T(8,128)(2,1)}, bf16[8,256,128]{2,1,0:T(8,128)(2,1)}, u32[]{:S(2)}, u32[]{:S(2)}) collective-permute-start(bf16[8,256,128]{2,1,0:T(8,128)(2,1)} %get-tuple-element.23), channel_id=1, source_target_pairs={{0,7},{1,6},{2,5},{3,4},{4,3},{5,2},{6,1},{7,0}} | collective-permute-start | bytes 1572872 | tf_op jit(solution)/shard_map/ppermute | solution.py:223
  189.0 34.1 %collective-permute-start.20 = (bf16[8,256,128]{2,1,0:T(8,128)(2,1)}, bf16[8,256,128]{2,1,0:T(8,128)(2,1)}, u32[]{:S(2)}, u32[]{:S(2)}) collective-permute-start(bf16[8,256,128]{2,1,0:T(8,128)(2,1)} %get-tuple-element.22), channel_id=1, source_target_pairs={{0,1},{1,0},{2,3},{3,2},{4,5},{5,4},{6,7},{7,6}} | collective-permute-start | bytes 1572872 | tf_op jit(solution)/shard_map/ppermute | solution.py:223
  203.6 121.2 %collective-permute-start.10 = (bf16[12,256,128]{2,1,0:T(8,128)(2,1)}, bf16[12,256,128]{2,1,0:T(8,128)(2,1)}, u32[]{:S(2)}, u32[]{:S(2)}) collective-permute-start(bf16[12,256,128]{2,1,0:T(8,128)(2,1)} %get-tuple-element.32), channel_id=1, source_target_pairs={{0,5},{1,4},{2,7},{3,6},{4,1},{5,0},{6,3},{7,2}} | collective-permute-start | bytes 2359304 | tf_op jit(solution)/shard_map/ppermute | solution.py:223
  203.6 121.5 %collective-permute-start.11 = (bf16[12,256,128]{2,1,0:T(8,128)(2,1)}, bf16[12,256,128]{2,1,0:T(8,128)(2,1)}, u32[]{:S(2)}, u32[]{:S(2)}) collective-permute-start(bf16[12,256,128]{2,1,0:T(8,128)(2,1)} %get-tuple-element.31), channel_id=1, source_target_pairs={{0,6},{1,7},{2,4},{3,5},{4,2},{5,3},{6,0},{7,1}} | collective-permute-start | bytes 2359304 | tf_op jit(solution)/shard_map/ppermute | solution.py:223
  212.4 173.2 %collective-permute-start.12 = (bf16[12,256,128]{2,1,0:T(8,128)(2,1)}, bf16[12,256,128]{2,1,0:T(8,128)(2,1)}, u32[]{:S(2)}, u32[]{:S(2)}) collective-permute-start(bf16[12,256,128]{2,1,0:T(8,128)(2,1)} %get-tuple-element.30), channel_id=1, source_target_pairs={{0,7},{1,6},{2,5},{3,4},{4,3},{5,2},{6,1},{7,0}} | collective-permute-start | bytes 2359304 | tf_op jit(solution)/shard_map/ppermute | solution.py:223
  222.5 96.7 %collective-permute-start = (bf16[4,256,128]{2,1,0:T(8,128)(2,1)}, bf16[4,256,128]{2,1,0:T(8,128)(2,1)}, u32[]{:S(2)}, u32[]{:S(2)}) collective-permute-start(bf16[4,256,128]{2,1,0:T(8,128)(2,1)} %get-tuple-element.42), channel_id=1, source_target_pairs={{0,2},{1,3},{2,0},{3,1},{4,6},{5,7},{6,4},{7,5}} | collective-permute-start | bytes 786440 | tf_op jit(solution)/shard_map/ppermute | solution.py:223
  223.1 96.5 %collective-permute-start.1 = (bf16[4,256,128]{2,1,0:T(8,128)(2,1)}, bf16[4,256,128]{2,1,0:T(8,128)(2,1)}, u32[]{:S(2)}, u32[]{:S(2)}) collective-permute-start(bf16[4,256,128]{2,1,0:T(8,128)(2,1)} %get-tuple-element.41), channel_id=1, source_target_pairs={{0,4},{1,5},{2,6},{3,7},{4,0},{5,1},{6,2},{7,3}} | collective-permute-start | bytes 786440 | tf_op jit(solution)/shard_map/ppermute | solution.py:223
  228.6 1.1 copy-start.5
  229.7 312.4 %all-to-all-start.2 = ((bf16[256,256,128]{2,1,0:T(8,128)(2,1)}), bf16[256,256,128]{2,1,0:T(8,128)(2,1)}, u32[]{:S(2)}, u32[]{:S(2)}) async-start(bf16[256,256,128]{2,1,0:T(8,128)(2,1)} %bitcast.123), calls=%async_computation.2 | async-start | bytes 33554432 | tf_op jit(solution)/shard_map/all_to_all | solution.py:240
  259.3 65.8 %copy-start.2 = (f32[4,32,5120]{2,1,0:T(8,128)S(1)}, f32[4,32,5120]{2,1,0:T(8,128)}, u32[]{:S(2)}) copy-start(f32[4,32,5120]{2,1,0:T(8,128)} %get-tuple-element.50) | copy-start | bytes 7864324
  319.2 68.1 %collective-permute-start.13 = (bf16[12,256,128]{2,1,0:T(8,128)(2,1)}, bf16[12,256,128]{2,1,0:T(8,128)(2,1)}, u32[]{:S(2)}, u32[]{:S(2)}) collective-permute-start(bf16[12,256,128]{2,1,0:T(8,128)(2,1)} %get-tuple-element.29), channel_id=1, source_target_pairs={{0,1},{1,0},{2,3},{3,2},{4,5},{5,4},{6,7},{7,6}} | collective-permute-start | bytes 2359304 | tf_op jit(solution)/shard_map/ppermute | solution.py:223
  319.6 139.1 %collective-permute-start.7 = (bf16[12,256,128]{2,1,0:T(8,128)(2,1)}, bf16[12,256,128]{2,1,0:T(8,128)(2,1)}, u32[]{:S(2)}, u32[]{:S(2)}) collective-permute-start(bf16[12,256,128]{2,1,0:T(8,128)(2,1)} %get-tuple-element.35), channel_id=1, source_target_pairs={{0,2},{1,3},{2,0},{3,1},{4,6},{5,7},{6,4},{7,5}} | collective-permute-start | bytes 2359304 | tf_op jit(solution)/shard_map/ppermute | solution.py:223
  324.7 151.1 %collective-permute-start.8 = (bf16[12,256,128]{2,1,0:T(8,128)(2,1)}, bf16[12,256,128]{2,1,0:T(8,128)(2,1)}, u32[]{:S(2)}, u32[]{:S(2)}) collective-permute-start(bf16[12,256,128]{2,1,0:T(8,128)(2,1)} %get-tuple-element.34), channel_id=1, source_target_pairs={{0,4},{1,5},{2,6},{3,7},{4,0},{5,1},{6,2},{7,3}} | collective-permute-start | bytes 2359304 | tf_op jit(solution)/shard_map/ppermute | solution.py:223
  325.1 150.8 %collective-permute-start.9 = (bf16[12,256,128]{2,1,0:T(8,128)(2,1)}, bf16[12,256,128]{2,1,0:T(8,128)(2,1)}, u32[]{:S(2)}, u32[]{:S(2)}) collective-permute-start(bf16[12,256,128]{2,1,0:T(8,128)(2,1)} %get-tuple-element.33), channel_id=1, source_target_pairs={{0,3},{1,2},{2,1},{3,0},{4,7},{5,6},{6,5},{7,4}} | collective-permute-start | bytes 2359304 | tf_op jit(solution)/shard_map/ppermute | solution.py:223
  385.6 170.1 %collective-permute-start.2 = (bf16[4,256,128]{2,1,0:T(8,128)(2,1)}, bf16[4,256,128]{2,1,0:T(8,128)(2,1)S(1)}, u32[]{:S(2)}, u32[]{:S(2)}) collective-permute-start(bf16[4,256,128]{2,1,0:T(8,128)(2,1)} %get-tuple-element.40), channel_id=1, source_target_pairs={{0,3},{1,2},{2,1},{3,0},{4,7},{5,6},{6,5},{7,4}} | collective-permute-start | bytes 786440 | tf_op jit(solution)/shard_map/ppermute | solution.py:223
  387.3 168.4 %collective-permute-start.3 = (bf16[4,256,128]{2,1,0:T(8,128)(2,1)}, bf16[4,256,128]{2,1,0:T(8,128)(2,1)S(1)}, u32[]{:S(2)}, u32[]{:S(2)}) collective-permute-start(bf16[4,256,128]{2,1,0:T(8,128)(2,1)} %get-tuple-element.39), channel_id=1, source_target_pairs={{0,5},{1,4},{2,7},{3,6},{4,1},{5,0},{6,3},{7,2}} | collective-permute-start | bytes 786440 | tf_op jit(solution)/shard_map/ppermute | solution.py:223
  458.7 97.1 %collective-permute-start.4 = (bf16[4,256,128]{2,1,0:T(8,128)(2,1)}, bf16[4,256,128]{2,1,0:T(8,128)(2,1)S(1)}, u32[]{:S(2)}, u32[]{:S(2)}) collective-permute-start(bf16[4,256,128]{2,1,0:T(8,128)(2,1)} %get-tuple-element.38), channel_id=1, source_target_pairs={{0,6},{1,7},{2,4},{3,5},{4,2},{5,3},{6,0},{7,1}} | collective-permute-start | bytes 786440 | tf_op jit(solution)/shard_map/ppermute | solution.py:223
  475.8 80.0 %collective-permute-start.5 = (bf16[4,256,128]{2,1,0:T(8,128)(2,1)}, bf16[4,256,128]{2,1,0:T(8,128)(2,1)}, u32[]{:S(2)}, u32[]{:S(2)}) collective-permute-start(bf16[4,256,128]{2,1,0:T(8,128)(2,1)} %get-tuple-element.37), channel_id=1, source_target_pairs={{0,7},{1,6},{2,5},{3,4},{4,3},{5,2},{6,1},{7,0}} | collective-permute-start | bytes 786440 | tf_op jit(solution)/shard_map/ppermute | solution.py:223
  475.9 79.9 %collective-permute-start.6 = (bf16[4,256,128]{2,1,0:T(8,128)(2,1)}, bf16[4,256,128]{2,1,0:T(8,128)(2,1)}, u32[]{:S(2)}, u32[]{:S(2)}) collective-permute-start(bf16[4,256,128]{2,1,0:T(8,128)(2,1)} %get-tuple-element.36), channel_id=1, source_target_pairs={{0,1},{1,0},{2,3},{3,2},{4,5},{5,4},{6,7},{7,6}} | collective-permute-start | bytes 786440 | tf_op jit(solution)/shard_map/ppermute | solution.py:223
  555.7 0.7 copy-start.8
  555.7 0.8 copy-start.9
  555.8 0.9 copy-start.10

commit v3 on v2

--- a/solution.py
+++ b/solution.py
@@ -57,6 +57,7 @@
 
 ROW_PAD = 9
 MERGE_ROWS = 4
+ATTEND_ROWS = 8
 K_CUTS = (8, 16, 28, 32)
 SWAP_ORDER = (2, 4, 3, 5, 6, 7, 1)
 
@@ -159,22 +160,23 @@
     slot_ids = lax.broadcasted_iota(jnp.int32, (pad_q, num_slots), 1)
     over_lanes = (((1,), (1,)), ((), ()))
     base = (pl.program_id(0) * pl.num_programs(1) + pl.program_id(1)) * step_rows
-    for row_idx in range(step_rows):
-        at = row_idx * stride
-        queries = rows_ref[at:at + pad_q, :].astype(jnp.bfloat16)
-        values_new = rows_ref[at + n_steps:at + n_steps + pad_q, :].astype(jnp.bfloat16)
-        old_scores = lax.dot_general(queries, k_ref[row_idx], over_lanes, preferred_element_type=jnp.float32) * score_scale
-        new_scores = lax.dot_general(queries, queries, over_lanes, preferred_element_type=jnp.float32) * score_scale
-        old_scores = jnp.where(slot_ids < pos_ref[base + row_idx], old_scores, -jnp.inf)
-        new_scores = jnp.where(new_valid, new_scores, -jnp.inf)
-        peak = jnp.maximum(jnp.max(old_scores, axis=-1, keepdims=True), jnp.max(new_scores, axis=-1, keepdims=True))
-        old_weights = jnp.exp(old_scores - peak)
-        new_weights = jnp.exp(new_scores - peak)
-        weight_sum = jnp.sum(old_weights, axis=-1, keepdims=True) + jnp.sum(new_weights, axis=-1, keepdims=True)
-        mixed = jnp.dot(old_weights.astype(jnp.bfloat16), v_ref[row_idx], preferred_element_type=jnp.float32)
-        mixed = mixed + jnp.dot(new_weights.astype(jnp.bfloat16), values_new, preferred_element_type=jnp.float32)
-        mixed = mixed / weight_sum
-        mixed_ref[pl.ds(row_idx, pad_q, stride=step_rows + 1), :] = mixed
+    for first_row in range(0, step_rows, ATTEND_ROWS):
+        rows = range(first_row, min(first_row + ATTEND_ROWS, step_rows))
+        queries = [rows_ref[r * stride:r * stride + pad_q, :].astype(jnp.bfloat16) for r in rows]
+        old = [lax.dot_general(q, k_ref[r], over_lanes, preferred_element_type=jnp.float32) for r, q in zip(rows, queries)]
+        new = [lax.dot_general(q, q, over_lanes, preferred_element_type=jnp.float32) for q in queries]
+        old = [jnp.where(slot_ids < pos_ref[base + r], s * score_scale, -jnp.inf) for r, s in zip(rows, old)]
+        new = [jnp.where(new_valid, s * score_scale, -jnp.inf) for s in new]
+        peak = [jnp.maximum(jnp.max(a, axis=-1, keepdims=True), jnp.max(c, axis=-1, keepdims=True)) for a, c in zip(old, new)]
+        old = [jnp.exp(s - m) for s, m in zip(old, peak)]
+        new = [jnp.exp(s - m) for s, m in zip(new, peak)]
+        weight_sum = [jnp.sum(a, axis=-1, keepdims=True) + jnp.sum(c, axis=-1, keepdims=True) for a, c in zip(old, new)]
+        mixed = [jnp.dot(w.astype(jnp.bfloat16), v_ref[r], preferred_element_type=jnp.float32) for r, w in zip(rows, old)]
+        values_new = [rows_ref[r * stride + n_steps:r * stride + n_steps + pad_q, :].astype(jnp.bfloat16) for r in rows]
+        fresh = [jnp.dot(w.astype(jnp.bfloat16), v, preferred_element_type=jnp.float32) for w, v in zip(new, values_new)]
+        mixed = [(a + c) / s for a, c, s in zip(mixed, fresh, weight_sum)]
+        for r, o in zip(rows, mixed):
+            mixed_ref[pl.ds(r, pad_q, stride=step_rows + 1), :] = o
     for q_idx in range(num_q):
         at = q_idx * (step_rows + 1)
         out_ref[0, q_idx] = mixed_ref[at:at + step_rows, :].astype(out_ref.dtype)

time: 561 us -> 514 us (0.916)
  Pallas kernels: 108 us -> 56.6 us
    pallas_call x1, Pallas kernels: 72.6 us -> 21.6 us  [attend_local(): pl.pallas_call(functools.partial(attend_kernel, n_steps, head_dim ** (-0....]
  transfers between devices with their start and end apart: 31 -> 31, of which waited for: 7 -> 9; matrix products, arithmetic and copies ran while one was open for 39% -> 43% of each run, Pallas kernels for 18% -> 10%
where the time goes in v3:
time: 514 us
  matrix products  229 us (45%)
  waiting for transfers between devices  151 us (29%)
  Pallas kernels  56.6 us (11%)
  starting transfers between devices  39.4 us (8%)
  local copies, waits for them, and re-layouts  26.6 us (5%)
  other arithmetic  10.2 us (2%)
    ppermute x28, waiting for transfers between devices, swap(): return lax.ppermute(arr, 'x', [(d, d ^ rel_idx) for d in range(n_dev)])  137 us
    dot_general x1, matrix products, finish(): jnp.einsum('sbd,df->sbf', normed, w_up, preferred_element_type=jnp.float32)  60.5 us
    dot_general x1, matrix products, finish(): jnp.einsum('sbd,df->sbf', normed, w_gate, preferred_element_type=jnp.floa...  60 us
    dot_general x1, matrix products, finish(): jnp.einsum('sbf,fd->sbd', activated, w_down, preferred_element_type=jnp.f...  58.1 us
    ppermute x28, starting transfers between devices, swap(): return lax.ppermute(arr, 'x', [(d, d ^ rel_idx) for d in range(n_dev)])  28.4 us
    pallas_call x1, Pallas kernels, attend_local(): pl.pallas_call(functools.partial(attend_kernel, n_steps, head_dim ** (-0....  21.6 us
    pallas_call x4, Pallas kernels, merge_chunk(): pl.pallas_call(functools.partial(merge_chunk_kernel, row_base, n_dev), ou...  21.3 us
    dot_general x1, matrix products, finish(): jnp.einsum('sbe,ed->sbd', flat_attn, w_o, preferred_element_type=jnp.floa...  20.8 us
  transfers between devices with their start and end apart: 31, of which 9 were waited for; matrix products, arithmetic and copies ran while one was open for 43% of the time, Pallas kernels for 10%

profile of v3, /device:TPU:0, one launch (start us, length us, event | category | flops | bytes accessed | tf_op | source)
XLA Modules:
  0.0 513.7 jit_solution(3446069698854134008)
XLA Ops:
  0.7 0.8 dynamic_slice.101
  1.4 0.7 convert_element_type.52
  2.1 1.7 fusion.47
  3.8 6.0 %fusion.20 = f32[4,32,1024]{2,1,0:T(8,128)S(1)} fusion(bf16[5120,1024]{1,0:T(8,128)(2,1)} %param.22, bf16[4,32,5120]{2,1,0:T(8,128)(2,1)} %param.17, f32[5120]{0:T(1024)S(1)} %convert_element_type.52, f32[4,32]{1,0:T(4,128)S(1)} %add_rsqrt_fusion.3), kind=kOutput, calls=%fused_computation.14 | convolution fusion | flops 1344798720 | bytes 12341760 | tf_op jit(solution)/shard_map/sbd,de->sbe/dot_general | solution.py:38
  11.2 18.2 %fusion.8 = f32[4,32,5120]{2,1,0:T(8,128)S(1)} fusion(bf16[5120,5120]{1,0:T(8,128)(2,1)} %param.21, bf16[4,32,5120]{2,1,0:T(8,128)(2,1)S(1)} %copy-done, f32[5120]{0:T(1024)S(1)} %convert_element_type.52, f32[4,32]{1,0:T(4,128)S(1)} %add_rsqrt_fusion.3), kind=kOutput, calls=%fused_computation.8 | convolution fusion | flops 6713507840 | bytes 56381952 | tf_op jit(solution)/shard_map/sbd,de->sbe/dot_general | solution.py:37
  29.4 0.5 copy.37
  29.9 1.0 copy-done.1
  30.9 0.7 fusion.50
  31.8 2.2 fusion.51
  33.9 0.9 subtract_convert_fusion
  34.9 0.7 maximum_bitcast_fusion
  35.9 5.5 %fusion.58 = bf16[4,32,1024]{2,1,0:T(8,128)(2,1)S(1)} fusion(bf16[5120,1024]{1,0:T(8,128)(2,1)} %param.23, bf16[4,32,5120]{2,1,0:T(8,128)(2,1)S(1)} %copy-done, f32[5120]{0:T(1024)S(1)} %convert_element_type.52, f32[4,32]{1,0:T(4,128)S(1)} %add_rsqrt_fusion.3), kind=kOutput, calls=%fused_computation.47 | convolution fusion | flops 1344929792 | bytes 12079616 | tf_op jit(solution)/shard_map/sbd,de->sbe/dot_general | solution.py:39
  41.5 0.7 copy-done.6
  42.3 1.4 pad_maximum_fusion
  43.7 4.3 all-to-all-start
  48.0 3.9 dynamic-slice_bitcast_fusion
  51.9 2.0 collective-permute-start.21
  53.9 1.5 collective-permute-start.22
  55.6 2.9 collective-permute-start.25
  58.6 13.9 %all-to-all-done.sent_ref = bf16[8,28,32,128]{3,2,1,0:T(8,128)(2,1)S(1)} async-done(((bf16[8,28,32,128]{3,2,1,0:T(8,128)(2,1)}), bf16[8,28,32,128]{3,2,1,0:T(8,128)(2,1)S(1)}, u32[]{:S(2)}, u32[]{:S(2)}) %all-to-all-start) | async-done | bytes 1835040 | tf_op jit(solution)/shard_map/all_to_all | solution.py:240
  72.4 1.2 copy-done.4
  73.6 21.6 %shard_map.175 = bf16[8,20,32,128]{3,2,1,0:T(8,128)(2,1)} custom-call(s32[256]{0:T(256)} %pos_ref.1, bf16[8,28,32,128]{3,2,1,0:T(8,128)(2,1)} %copy-done.4, bf16[256,256,128]{2,1,0:T(8,128)(2,1)} %bitcast.114, bf16[256,256,128]{2,1,0:T(8,128)(2,1)} %bitcast.122), custom_call_target="tpu_custom_call" | custom-call | flops 1000000000 | bytes 33554432 | tf_op jit(solution)/shard_map/pallas_call | solution.py:194
  95.3 2.3 all-to-all-start.1
  97.6 3.9 constant_dynamic-slice_fusion
  101.5 2.6 collective-permute-start.26
  104.1 0.4 collective-permute-start.27
  104.5 0.5 collective-permute-start.14
  105.2 1.1 collective-permute-done.25.refs_5_
  106.3 24.3 %collective-permute-done.26.refs_6_ = bf16[8,256,128]{2,1,0:T(8,128)(2,1)} collective-permute-done((bf16[8,256,128]{2,1,0:T(8,128)(2,1)}, bf16[8,256,128]{2,1,0:T(8,128)(2,1)}, u32[]{:S(2)}, u32[]{:S(2)}) %collective-permute-start.26) | collective-permute-done | bytes 524320 | tf_op jit(solution)/shard_map/ppermute | solution.py:225
  130.5 1.1 collective-permute-start.17
  131.6 1.5 collective-permute-start.18
  133.1 8.8 %collective-permute-done.14.refs_1_ = bf16[8,256,128]{2,1,0:T(8,128)(2,1)S(1)} collective-permute-done((bf16[8,256,128]{2,1,0:T(8,128)(2,1)}, bf16[8,256,128]{2,1,0:T(8,128)(2,1)S(1)}, u32[]{:S(2)}, u32[]{:S(2)}) %collective-permute-start.14) | collective-permute-done | bytes 524320 | tf_op jit(solution)/shard_map/ppermute | solution.py:225
  142.2 1.2 collective-permute-start.20
  143.4 0.6 pad_add_fusion.meta_ref
  144.0 2.7 constant_dynamic-slice_fusion.14
  146.7 5.0 constant_dynamic-slice_fusion.7
  151.8 4.8 shard_map.177.refs_9_
  156.6 2.5 collective-permute-start.11
  159.1 6.3 %collective-permute-done.18.refs_5_ = bf16[8,256,128]{2,1,0:T(8,128)(2,1)} collective-permute-done((bf16[8,256,128]{2,1,0:T(8,128)(2,1)}, bf16[8,256,128]{2,1,0:T(8,128)(2,1)}, u32[]{:S(2)}, u32[]{:S(2)}) %collective-permute-start.18) | collective-permute-done | bytes 524320 | tf_op jit(solution)/shard_map/ppermute | solution.py:225
  165.4 10.1 %collective-permute-done.19.refs_6_ = bf16[8,256,128]{2,1,0:T(8,128)(2,1)} collective-permute-done((bf16[8,256,128]{2,1,0:T(8,128)(2,1)}, bf16[8,256,128]{2,1,0:T(8,128)(2,1)}, u32[]{:S(2)}, u32[]{:S(2)}) %collective-permute-start.19) | collective-permute-done | bytes 524320 | tf_op jit(solution)/shard_map/ppermute | solution.py:225
  175.5 0.6 collective-permute-start
  176.1 0.8 collective-permute-start.1
  176.9 4.8 shard_map.178.refs_9_
  181.7 1.0 copy-done.5
  182.7 4.5 all-to-all-start.2
  187.2 2.0 copy.42
  189.2 2.3 reshape_reshape.3
  191.5 20.8 %multiply_reduce_fusion = (f32[4,32]{1,0:T(4,128)S(1)}, f32[4,32,5120]{2,1,0:T(8,128)}) fusion(bf16[4,32,5120]{2,1,0:T(8,128)(2,1)} %reshape_reshape.3, bf16[5120,5120]{1,0:T(8,128)(2,1)} %param.26, bf16[4,32,5120]{2,1,0:T(8,128)(2,1)S(1)} %copy-done), kind=kOutput, calls=%fused_computation.37 | convolution fusion | flops 6714818560 | bytes 57672192 | tf_op jit(solution)/shard_map/sbe,ed->sbd/dot_general | solution.py:48
  212.3 60.0 %fusion.4 = f32[4,32,17408]{2,1,0:T(8,128)} fusion(bf16[5120,17408]{1,0:T(8,128)(2,1)} %param.28, f32[4,32,5120]{2,1,0:T(8,128)} %get-tuple-element.50, f32[5120]{0:T(1024)S(1)} %convert_element_type.61, f32[4,32]{1,0:T(4,128)S(1)} %add_rsqrt_fusion.2), kind=kOutput, calls=%fused_computation.4 | convolution fusion | flops 22818979840 | bytes 189813248 | tf_op jit(solution)/shard_map/sbd,df->sbf/dot_general | solution.py:51
  272.3 0.4 collective-permute-start.13
  272.7 5.0 collective-permute-start.7
  277.7 0.4 collective-permute-start.8
  278.1 60.5 %fusion.13.clone.8 = bf16[4,32,17408]{2,1,0:T(8,128)(2,1)} fusion(bf16[5120,17408]{1,0:T(8,128)(2,1)} %param.29, f32[4,32,17408]{2,1,0:T(8,128)} %fusion.4, f32[4,32,5120]{2,1,0:T(8,128)S(1)} %copy-done.2, f32[5120]{0:T(1024)S(1)} %convert_element_type.61, f32[4,32]{1,0:T(4,128)S(1)} %add_rsqrt_fusion.2), kind=kOutput, calls=%fused_computation.11.clone.clone.clone.clone.clone.clone.clone.1 | convolution fusion | flops 22832349184 | bytes 194269696 | tf_op jit(solution)/shard_map/sbd,df->sbf/dot_general | solution.py:52
  338.6 1.7 collective-permute-start.2
  340.3 0.8 collective-permute-start.3
  341.1 70.6 %collective-permute-done.7.refs_1_ = bf16[12,256,128]{2,1,0:T(8,128)(2,1)} collective-permute-done((bf16[12,256,128]{2,1,0:T(8,128)(2,1)}, bf16[12,256,128]{2,1,0:T(8,128)(2,1)}, u32[]{:S(2)}, u32[]{:S(2)}) %collective-permute-start.7) | collective-permute-done | bytes 786464 | tf_op jit(solution)/shard_map/ppermute | solution.py:225
  411.8 1.5 collective-permute-start.4
  413.2 15.6 %collective-permute-done.8.refs_2_ = bf16[12,256,128]{2,1,0:T(8,128)(2,1)} collective-permute-done((bf16[12,256,128]{2,1,0:T(8,128)(2,1)}, bf16[12,256,128]{2,1,0:T(8,128)(2,1)}, u32[]{:S(2)}, u32[]{:S(2)}) %collective-permute-start.8) | collective-permute-done | bytes 786464 | tf_op jit(solution)/shard_map/ppermute | solution.py:225
  428.9 0.4 collective-permute-start.6
  429.3 58.1 %fusion.41 = bf16[4,32,5120]{2,1,0:T(8,128)(2,1)} fusion(f32[4,32,5120]{2,1,0:T(8,128)S(1)} %copy-done.2, bf16[17408,5120]{1,0:T(8,128)(2,1)} %param.30, bf16[4,32,17408]{2,1,0:T(8,128)(2,1)} %fusion.13.clone.8), kind=kOutput, calls=%fused_computation.25 | convolution fusion | flops 22818324480 | bytes 186646528 | tf_op jit(solution)/shard_map/sbf,fd->sbd/dot_general | solution.py:54
  487.4 7.7 %shard_map.179.refs_9_ = bf16[32,256,8,128]{3,2,1,0:T(8,128)(2,1)} custom-call(s32[40]{0:T(128)} %pad_add_fusion.meta_ref, bf16[256,256,128]{2,1,0:T(8,128)(2,1)} %bitcast.120, bf16[12,256,128]{2,1,0:T(8,128)(2,1)} %collective-permute-done.7.refs_1_, bf16[12,256,128]{2,1,0:T(8,128)(2,1)} %collective-permute-done.8.refs_2_, ...), custom_call_target="tpu_custom_call", output_to_operand_aliasing={{}: (10, {})} | custom-call | flops 100000000 | bytes 12582912 | tf_op jit(solution)/shard_map/pallas_call | solution.py:107
  495.1 13.6 %shard_map.176 = bf16[32,256,8,128]{3,2,1,0:T(8,128)(2,1)} custom-call(s32[40]{0:T(128)} %pad_add_fusion.meta_ref, bf16[8,32,256,128]{3,2,1,0:T(8,128)(2,1)} %bitcast.17.blocks_ref, bf16[4,32,8,128]{3,2,1,0:T(8,128)(2,1)} %bitcast.135), custom_call_target="tpu_custom_call" | custom-call | flops 100000000 | bytes 33554432 | tf_op jit(solution)/shard_map/pallas_call | solution.py:129
  508.8 0.6 copy-done.8
  509.7 4.0 shard_map.180
  (79 shorter events, 3.1 us)
Async XLA Ops:
  3.8 6.3 %copy-start.12 = (bf16[128]{0:T(256)(128)(2,1)S(1)}, bf16[128]{0:T(256)(128)(2,1)}, u32[]{:S(2)}) copy-start(bf16[128]{0:T(256)(128)(2,1)} %param.25) | copy-start | bytes 772
  9.9 1.3 copy-start
  11.1 18.3 %copy-start.3 = (bf16[4,32,8,128]{3,2,1,0:T(8,128)(2,1)}, bf16[4,32,8,128]{3,2,1,0:T(8,128)(2,1)S(1)}, u32[]{:S(2)}) copy-start(bf16[4,32,8,128]{3,2,1,0:T(8,128)(2,1)S(1)} %pad_maximum_fusion.1.refs_8_) | copy-start | bytes 786436
  29.4 1.5 copy-start.1
  30.9 0.9 copy-start.13
  41.5 0.7 copy-start.6
  43.7 28.7 %all-to-all-start = ((bf16[8,28,32,128]{3,2,1,0:T(8,128)(2,1)}), bf16[8,28,32,128]{3,2,1,0:T(8,128)(2,1)S(1)}, u32[]{:S(2)}, u32[]{:S(2)}) async-start(bf16[8,28,32,128]{3,2,1,0:T(8,128)(2,1)} %pad_maximum_fusion), calls=%async_computation | async-start | bytes 3670016 | tf_op jit(solution)/shard_map/all_to_all | solution.py:240
  51.9 49.6 %collective-permute-start.21 = (bf16[8,256,128]{2,1,0:T(8,128)(2,1)}, bf16[8,256,128]{2,1,0:T(8,128)(2,1)}, u32[]{:S(2)}, u32[]{:S(2)}) collective-permute-start(bf16[8,256,128]{2,1,0:T(8,128)(2,1)} %get-tuple-element.20), channel_id=1, source_target_pairs={{0,2},{1,3},{2,0},{3,1},{4,6},{5,7},{6,4},{7,5}} | collective-permute-start | bytes 1572872 | tf_op jit(solution)/shard_map/ppermute | solution.py:225
  53.9 50.2 %collective-permute-start.22 = (bf16[8,256,128]{2,1,0:T(8,128)(2,1)}, bf16[8,256,128]{2,1,0:T(8,128)(2,1)}, u32[]{:S(2)}, u32[]{:S(2)}) collective-permute-start(bf16[8,256,128]{2,1,0:T(8,128)(2,1)} %get-tuple-element.19), channel_id=1, source_target_pairs={{0,4},{1,5},{2,6},{3,7},{4,0},{5,1},{6,2},{7,3}} | collective-permute-start | bytes 1572872 | tf_op jit(solution)/shard_map/ppermute | solution.py:225
  55.4 49.1 %collective-permute-start.23 = (bf16[8,256,128]{2,1,0:T(8,128)(2,1)}, bf16[8,256,128]{2,1,0:T(8,128)(2,1)}, u32[]{:S(2)}, u32[]{:S(2)}) collective-permute-start(bf16[8,256,128]{2,1,0:T(8,128)(2,1)} %get-tuple-element.18), channel_id=1, source_target_pairs={{0,3},{1,2},{2,1},{3,0},{4,7},{5,6},{6,5},{7,4}} | collective-permute-start | bytes 1572872 | tf_op jit(solution)/shard_map/ppermute | solution.py:225
  55.4 49.7 %collective-permute-start.24 = (bf16[8,256,128]{2,1,0:T(8,128)(2,1)}, bf16[8,256,128]{2,1,0:T(8,128)(2,1)}, u32[]{:S(2)}, u32[]{:S(2)}) collective-permute-start(bf16[8,256,128]{2,1,0:T(8,128)(2,1)} %get-tuple-element.17), channel_id=1, source_target_pairs={{0,5},{1,4},{2,7},{3,6},{4,1},{5,0},{6,3},{7,2}} | collective-permute-start | bytes 1572872 | tf_op jit(solution)/shard_map/ppermute | solution.py:225
  55.6 50.6 %collective-permute-start.25 = (bf16[8,256,128]{2,1,0:T(8,128)(2,1)}, bf16[8,256,128]{2,1,0:T(8,128)(2,1)}, u32[]{:S(2)}, u32[]{:S(2)}) collective-permute-start(bf16[8,256,128]{2,1,0:T(8,128)(2,1)} %get-tuple-element.16), channel_id=1, source_target_pairs={{0,6},{1,7},{2,4},{3,5},{4,2},{5,3},{6,0},{7,1}} | collective-permute-start | bytes 1572872 | tf_op jit(solution)/shard_map/ppermute | solution.py:225
  72.4 1.2 copy-start.4
  95.3 86.4 %all-to-all-start.1 = ((bf16[8,20,32,128]{3,2,1,0:T(8,128)(2,1)}), bf16[8,20,32,128]{3,2,1,0:T(8,128)(2,1)S(1)}, u32[]{:S(2)}, u32[]{:S(2)}) async-start(bf16[8,20,32,128]{3,2,1,0:T(8,128)(2,1)} %shard_map.175), calls=%async_computation.1 | async-start | bytes 2621440 | tf_op jit(solution)/shard_map/all_to_all | solution.py:243
  97.6 7.6 %copy-start.11 = (bf16[5120]{0:T(1024)(128)(2,1)S(1)}, bf16[5120]{0:T(1024)(128)(2,1)}, u32[]{:S(2)}) copy-start(bf16[5120]{0:T(1024)(128)(2,1)} %param.27) | copy-start | bytes 30724
  97.6 7.6 %copy-start.14 = (s32[8]{0:T(128)S(1)}, s32[8]{0:T(128)}, u32[]{:S(2)}) copy-start(s32[8]{0:T(128)} %constant.88.clone) | copy-start | bytes 100
  101.5 29.0 %collective-permute-start.26 = (bf16[8,256,128]{2,1,0:T(8,128)(2,1)}, bf16[8,256,128]{2,1,0:T(8,128)(2,1)}, u32[]{:S(2)}, u32[]{:S(2)}) collective-permute-start(bf16[8,256,128]{2,1,0:T(8,128)(2,1)} %get-tuple-element.21), channel_id=1, source_target_pairs={{0,7},{1,6},{2,5},{3,4},{4,3},{5,2},{6,1},{7,0}} | collective-permute-start | bytes 1572872 | tf_op jit(solution)/shard_map/ppermute | solution.py:225
  104.1 27.6 %collective-permute-start.27 = (bf16[8,256,128]{2,1,0:T(8,128)(2,1)}, bf16[8,256,128]{2,1,0:T(8,128)(2,1)}, u32[]{:S(2)}, u32[]{:S(2)}) collective-permute-start(bf16[8,256,128]{2,1,0:T(8,128)(2,1)} %get-tuple-element.15), channel_id=1, source_target_pairs={{0,1},{1,0},{2,3},{3,2},{4,5},{5,4},{6,7},{7,6}} | collective-permute-start | bytes 1572872 | tf_op jit(solution)/shard_map/ppermute | solution.py:225
  104.5 37.4 %collective-permute-start.14 = (bf16[8,256,128]{2,1,0:T(8,128)(2,1)}, bf16[8,256,128]{2,1,0:T(8,128)(2,1)S(1)}, u32[]{:S(2)}, u32[]{:S(2)}) collective-permute-start(bf16[8,256,128]{2,1,0:T(8,128)(2,1)} %get-tuple-element.28), channel_id=1, source_target_pairs={{0,2},{1,3},{2,0},{3,1},{4,6},{5,7},{6,4},{7,5}} | collective-permute-start | bytes 1572872 | tf_op jit(solution)/shard_map/ppermute | solution.py:225
  105.0 37.2 %collective-permute-start.15 = (bf16[8,256,128]{2,1,0:T(8,128)(2,1)}, bf16[8,256,128]{2,1,0:T(8,128)(2,1)}, u32[]{:S(2)}, u32[]{:S(2)}) collective-permute-start(bf16[8,256,128]{2,1,0:T(8,128)(2,1)} %get-tuple-element.27), channel_id=1, source_target_pairs={{0,4},{1,5},{2,6},{3,7},{4,0},{5,1},{6,2},{7,3}} | collective-permute-start | bytes 1572872 | tf_op jit(solution)/shard_map/ppermute | solution.py:225
  106.3 50.3 %collective-permute-start.16 = (bf16[8,256,128]{2,1,0:T(8,128)(2,1)}, bf16[8,256,128]{2,1,0:T(8,128)(2,1)}, u32[]{:S(2)}, u32[]{:S(2)}) collective-permute-start(bf16[8,256,128]{2,1,0:T(8,128)(2,1)} %get-tuple-element.26), channel_id=1, source_target_pairs={{0,3},{1,2},{2,1},{3,0},{4,7},{5,6},{6,5},{7,4}} | collective-permute-start | bytes 1572872 | tf_op jit(solution)/shard_map/ppermute | solution.py:225
  130.5 26.1 %collective-permute-start.17 = (bf16[8,256,128]{2,1,0:T(8,128)(2,1)}, bf16[8,256,128]{2,1,0:T(8,128)(2,1)}, u32[]{:S(2)}, u32[]{:S(2)}) collective-permute-start(bf16[8,256,128]{2,1,0:T(8,128)(2,1)} %get-tuple-element.25), channel_id=1, source_target_pairs={{0,5},{1,4},{2,7},{3,6},{4,1},{5,0},{6,3},{7,2}} | collective-permute-start | bytes 1572872 | tf_op jit(solution)/shard_map/ppermute | solution.py:225
  131.6 33.8 %collective-permute-start.18 = (bf16[8,256,128]{2,1,0:T(8,128)(2,1)}, bf16[8,256,128]{2,1,0:T(8,128)(2,1)}, u32[]{:S(2)}, u32[]{:S(2)}) collective-permute-start(bf16[8,256,128]{2,1,0:T(8,128)(2,1)} %get-tuple-element.24), channel_id=1, source_target_pairs={{0,6},{1,7},{2,4},{3,5},{4,2},{5,3},{6,0},{7,1}} | collective-permute-start | bytes 1572872 | tf_op jit(solution)/shard_map/ppermute | solution.py:225
  141.9 9.9 %copy-start.7 = (bf16[8,256,128]{2,1,0:T(8,128)(2,1)}, bf16[8,256,128]{2,1,0:T(8,128)(2,1)S(1)}, u32[]{:S(2)}) copy-start(bf16[8,256,128]{2,1,0:T(8,128)(2,1)S(1)} %collective-permute-done.14.refs_1_) | copy-start | bytes 1572868
  141.9 33.7 %collective-permute-start.19 = (bf16[8,256,128]{2,1,0:T(8,128)(2,1)}, bf16[8,256,128]{2,1,0:T(8,128)(2,1)}, u32[]{:S(2)}, u32[]{:S(2)}) collective-permute-start(bf16[8,256,128]{2,1,0:T(8,128)(2,1)} %get-tuple-element.23), channel_id=1, source_target_pairs={{0,7},{1,6},{2,5},{3,4},{4,3},{5,2},{6,1},{7,0}} | collective-permute-start | bytes 1572872 | tf_op jit(solution)/shard_map/ppermute | solution.py:225
  142.2 33.9 %collective-permute-start.20 = (bf16[8,256,128]{2,1,0:T(8,128)(2,1)}, bf16[8,256,128]{2,1,0:T(8,128)(2,1)}, u32[]{:S(2)}, u32[]{:S(2)}) collective-permute-start(bf16[8,256,128]{2,1,0:T(8,128)(2,1)} %get-tuple-element.22), channel_id=1, source_target_pairs={{0,1},{1,0},{2,3},{3,2},{4,5},{5,4},{6,7},{7,6}} | collective-permute-start | bytes 1572872 | tf_op jit(solution)/shard_map/ppermute | solution.py:225
  156.6 121.2 %collective-permute-start.10 = (bf16[12,256,128]{2,1,0:T(8,128)(2,1)}, bf16[12,256,128]{2,1,0:T(8,128)(2,1)}, u32[]{:S(2)}, u32[]{:S(2)}) collective-permute-start(bf16[12,256,128]{2,1,0:T(8,128)(2,1)} %get-tuple-element.32), channel_id=1, source_target_pairs={{0,5},{1,4},{2,7},{3,6},{4,1},{5,0},{6,3},{7,2}} | collective-permute-start | bytes 2359304 | tf_op jit(solution)/shard_map/ppermute | solution.py:225
  156.6 121.5 %collective-permute-start.11 = (bf16[12,256,128]{2,1,0:T(8,128)(2,1)}, bf16[12,256,128]{2,1,0:T(8,128)(2,1)}, u32[]{:S(2)}, u32[]{:S(2)}) collective-permute-start(bf16[12,256,128]{2,1,0:T(8,128)(2,1)} %get-tuple-element.31), channel_id=1, source_target_pairs={{0,6},{1,7},{2,4},{3,5},{4,2},{5,3},{6,0},{7,1}} | collective-permute-start | bytes 2359304 | tf_op jit(solution)/shard_map/ppermute | solution.py:225
  165.4 173.2 %collective-permute-start.12 = (bf16[12,256,128]{2,1,0:T(8,128)(2,1)}, bf16[12,256,128]{2,1,0:T(8,128)(2,1)}, u32[]{:S(2)}, u32[]{:S(2)}) collective-permute-start(bf16[12,256,128]{2,1,0:T(8,128)(2,1)} %get-tuple-element.30), channel_id=1, source_target_pairs={{0,7},{1,6},{2,5},{3,4},{4,3},{5,2},{6,1},{7,0}} | collective-permute-start | bytes 2359304 | tf_op jit(solution)/shard_map/ppermute | solution.py:225
  175.5 96.8 %collective-permute-start = (bf16[4,256,128]{2,1,0:T(8,128)(2,1)}, bf16[4,256,128]{2,1,0:T(8,128)(2,1)}, u32[]{:S(2)}, u32[]{:S(2)}) collective-permute-start(bf16[4,256,128]{2,1,0:T(8,128)(2,1)} %get-tuple-element.42), channel_id=1, source_target_pairs={{0,2},{1,3},{2,0},{3,1},{4,6},{5,7},{6,4},{7,5}} | collective-permute-start | bytes 786440 | tf_op jit(solution)/shard_map/ppermute | solution.py:225
  176.1 96.6 %collective-permute-start.1 = (bf16[4,256,128]{2,1,0:T(8,128)(2,1)}, bf16[4,256,128]{2,1,0:T(8,128)(2,1)}, u32[]{:S(2)}, u32[]{:S(2)}) collective-permute-start(bf16[4,256,128]{2,1,0:T(8,128)(2,1)} %get-tuple-element.41), channel_id=1, source_target_pairs={{0,4},{1,5},{2,6},{3,7},{4,0},{5,1},{6,2},{7,3}} | collective-permute-start | bytes 786440 | tf_op jit(solution)/shard_map/ppermute | solution.py:225
  181.7 1.1 copy-start.5
  182.7 312.4 %all-to-all-start.2 = ((bf16[256,256,128]{2,1,0:T(8,128)(2,1)}), bf16[256,256,128]{2,1,0:T(8,128)(2,1)}, u32[]{:S(2)}, u32[]{:S(2)}) async-start(bf16[256,256,128]{2,1,0:T(8,128)(2,1)} %bitcast.123), calls=%async_computation.2 | async-start | bytes 33554432 | tf_op jit(solution)/shard_map/all_to_all | solution.py:242
  212.3 65.8 %copy-start.2 = (f32[4,32,5120]{2,1,0:T(8,128)S(1)}, f32[4,32,5120]{2,1,0:T(8,128)}, u32[]{:S(2)}) copy-start(f32[4,32,5120]{2,1,0:T(8,128)} %get-tuple-element.50) | copy-start | bytes 7864324
  272.3 68.0 %collective-permute-start.13 = (bf16[12,256,128]{2,1,0:T(8,128)(2,1)}, bf16[12,256,128]{2,1,0:T(8,128)(2,1)}, u32[]{:S(2)}, u32[]{:S(2)}) collective-permute-start(bf16[12,256,128]{2,1,0:T(8,128)(2,1)} %get-tuple-element.29), channel_id=1, source_target_pairs={{0,1},{1,0},{2,3},{3,2},{4,5},{5,4},{6,7},{7,6}} | collective-permute-start | bytes 2359304 | tf_op jit(solution)/shard_map/ppermute | solution.py:225
  272.7 139.1 %collective-permute-start.7 = (bf16[12,256,128]{2,1,0:T(8,128)(2,1)}, bf16[12,256,128]{2,1,0:T(8,128)(2,1)}, u32[]{:S(2)}, u32[]{:S(2)}) collective-permute-start(bf16[12,256,128]{2,1,0:T(8,128)(2,1)} %get-tuple-element.35), channel_id=1, source_target_pairs={{0,2},{1,3},{2,0},{3,1},{4,6},{5,7},{6,4},{7,5}} | collective-permute-start | bytes 2359304 | tf_op jit(solution)/shard_map/ppermute | solution.py:225
  277.7 151.1 %collective-permute-start.8 = (bf16[12,256,128]{2,1,0:T(8,128)(2,1)}, bf16[12,256,128]{2,1,0:T(8,128)(2,1)}, u32[]{:S(2)}, u32[]{:S(2)}) collective-permute-start(bf16[12,256,128]{2,1,0:T(8,128)(2,1)} %get-tuple-element.34), channel_id=1, source_target_pairs={{0,4},{1,5},{2,6},{3,7},{4,0},{5,1},{6,2},{7,3}} | collective-permute-start | bytes 2359304 | tf_op jit(solution)/shard_map/ppermute | solution.py:225
  278.1 150.8 %collective-permute-start.9 = (bf16[12,256,128]{2,1,0:T(8,128)(2,1)}, bf16[12,256,128]{2,1,0:T(8,128)(2,1)}, u32[]{:S(2)}, u32[]{:S(2)}) collective-permute-start(bf16[12,256,128]{2,1,0:T(8,128)(2,1)} %get-tuple-element.33), channel_id=1, source_target_pairs={{0,3},{1,2},{2,1},{3,0},{4,7},{5,6},{6,5},{7,4}} | collective-permute-start | bytes 2359304 | tf_op jit(solution)/shard_map/ppermute | solution.py:225
  338.6 170.1 %collective-permute-start.2 = (bf16[4,256,128]{2,1,0:T(8,128)(2,1)}, bf16[4,256,128]{2,1,0:T(8,128)(2,1)S(1)}, u32[]{:S(2)}, u32[]{:S(2)}) collective-permute-start(bf16[4,256,128]{2,1,0:T(8,128)(2,1)} %get-tuple-element.40), channel_id=1, source_target_pairs={{0,3},{1,2},{2,1},{3,0},{4,7},{5,6},{6,5},{7,4}} | collective-permute-start | bytes 786440 | tf_op jit(solution)/shard_map/ppermute | solution.py:225
  340.3 168.4 %collective-permute-start.3 = (bf16[4,256,128]{2,1,0:T(8,128)(2,1)}, bf16[4,256,128]{2,1,0:T(8,128)(2,1)S(1)}, u32[]{:S(2)}, u32[]{:S(2)}) collective-permute-start(bf16[4,256,128]{2,1,0:T(8,128)(2,1)} %get-tuple-element.39), channel_id=1, source_target_pairs={{0,5},{1,4},{2,7},{3,6},{4,1},{5,0},{6,3},{7,2}} | collective-permute-start | bytes 786440 | tf_op jit(solution)/shard_map/ppermute | solution.py:225
  411.8 97.0 %collective-permute-start.4 = (bf16[4,256,128]{2,1,0:T(8,128)(2,1)}, bf16[4,256,128]{2,1,0:T(8,128)(2,1)S(1)}, u32[]{:S(2)}, u32[]{:S(2)}) collective-permute-start(bf16[4,256,128]{2,1,0:T(8,128)(2,1)} %get-tuple-element.38), channel_id=1, source_target_pairs={{0,6},{1,7},{2,4},{3,5},{4,2},{5,3},{6,0},{7,1}} | collective-permute-start | bytes 786440 | tf_op jit(solution)/shard_map/ppermute | solution.py:225
  428.8 80.0 %collective-permute-start.5 = (bf16[4,256,128]{2,1,0:T(8,128)(2,1)}, bf16[4,256,128]{2,1,0:T(8,128)(2,1)}, u32[]{:S(2)}, u32[]{:S(2)}) collective-permute-start(bf16[4,256,128]{2,1,0:T(8,128)(2,1)} %get-tuple-element.37), channel_id=1, source_target_pairs={{0,7},{1,6},{2,5},{3,4},{4,3},{5,2},{6,1},{7,0}} | collective-permute-start | bytes 786440 | tf_op jit(solution)/shard_map/ppermute | solution.py:225
  428.9 79.9 %collective-permute-start.6 = (bf16[4,256,128]{2,1,0:T(8,128)(2,1)}, bf16[4,256,128]{2,1,0:T(8,128)(2,1)}, u32[]{:S(2)}, u32[]{:S(2)}) collective-permute-start(bf16[4,256,128]{2,1,0:T(8,128)(2,1)} %get-tuple-element.36), channel_id=1, source_target_pairs={{0,1},{1,0},{2,3},{3,2},{4,5},{5,4},{6,7},{7,6}} | collective-permute-start | bytes 786440 | tf_op jit(solution)/shard_map/ppermute | solution.py:225
  508.8 0.7 copy-start.8
  508.8 0.8 copy-start.9
  508.8 0.9 copy-start.10

commit v4 on v3

--- a/solution.py
+++ b/solution.py
@@ -58,13 +58,8 @@
 ROW_PAD = 9
 MERGE_ROWS = 4
 ATTEND_ROWS = 8
-K_CUTS = (8, 16, 28, 32)
+K_CHUNKS = ((24, 8), (0, 20), (20, 4))
 SWAP_ORDER = (2, 4, 3, 5, 6, 7, 1)
-
-
-def cuts(num_rows, ends):
-    ends = [num_rows * e // 32 for e in ends]
-    return [(lo, hi - lo) for lo, hi in zip([0] + ends[:-1], ends)]
 
 
 def merge_row(row_idx, block_refs, head_ids, fresh_ref, first_slot, out_ref, wide_ref):
@@ -113,7 +108,7 @@
     )(meta, own, *blocks, fresh_rows, *(() if partial_out is None else (partial_out,)))
 
 
-def merge_all_kernel(n_dev, meta_ref, blocks_ref, fresh_ref, out_ref, wide_ref):
+def merge_first_kernel(n_dev, meta_ref, blocks_ref, fresh_ref, partial_ref, out_ref, wide_ref):
     step_rows = out_ref.shape[0]
 
     @pl.loop(0, step_rows)
@@ -122,34 +117,36 @@
         merge_row(row_idx, [blocks_ref.at[h] for h in range(n_dev)], range(n_dev), fresh_ref, first_slot, out_ref, wide_ref)
 
 
-def merge_all(blocks, fresh_rows, meta):
-    n_dev, num_rows, num_slots, head_dim = blocks.shape
+def merge_first(blocks, fresh_rows, meta, partial_out):
+    n_dev, chunk_rows, num_slots, head_dim = blocks.shape
     n_steps = fresh_rows.shape[0]
-    step_rows = math.gcd(num_rows, 2 * MERGE_ROWS)
+    step_rows = math.gcd(chunk_rows, 2 * MERGE_ROWS)
     return pl.pallas_call(
-        functools.partial(merge_all_kernel, n_dev),
-        out_shape=jax.ShapeDtypeStruct((num_rows, num_slots, n_dev, head_dim), blocks.dtype),
+        functools.partial(merge_first_kernel, n_dev),
+        out_shape=jax.ShapeDtypeStruct(partial_out.shape, blocks.dtype),
         grid_spec=pltpu.PrefetchScalarGridSpec(
             num_scalar_prefetch=1,
-            grid=(num_rows // step_rows,),
+            grid=(chunk_rows // step_rows,),
             in_specs=[
                 pl.BlockSpec((n_dev, step_rows, num_slots, head_dim), lambda b, meta: (0, b, 0, 0)),
                 pl.BlockSpec((n_steps, step_rows, n_dev, head_dim), lambda b, meta: (0, b, 0, 0)),
+                pl.BlockSpec(memory_space=pl.ANY),
             ],
             out_specs=pl.BlockSpec((step_rows, num_slots, n_dev, head_dim), lambda b, meta: (b, 0, 0, 0)),
             scratch_shapes=[pltpu.VMEM((num_slots * ROW_PAD, head_dim), jnp.float32)],
         ),
+        input_output_aliases={3: 0},
         cost_estimate=pl.CostEstimate(flops=10**8, bytes_accessed=4 * blocks.size, transcendentals=0),
-    )(meta, blocks, fresh_rows)
-
-
-def attend_kernel(n_steps, score_scale, pos_ref, sent_ref, k_ref, v_ref, out_ref, rows_ref, mixed_ref):
+    )(meta, blocks, fresh_rows, partial_out)
+
+
+def attend_kernel(n_steps, score_scale, meta_ref, sent_ref, k_ref, v_ref, out_ref, rows_ref, mixed_ref):
     num_sent, step_rows, head_dim = sent_ref.shape[1:]
     num_q = out_ref.shape[1]
     pad_q = num_sent + n_steps
     stride = num_sent + 1 - num_sent % 2
     group = num_q // n_steps
-    num_slots = k_ref.shape[1]
+    num_slots = k_ref.shape[2]
     rows_ref[step_rows * stride:, :] = jnp.zeros((rows_ref.shape[0] - step_rows * stride, head_dim), jnp.float32)
     for sent_idx in range(num_sent):
         rows_ref[pl.ds(sent_idx, step_rows, stride=stride), :] = sent_ref[0, sent_idx].astype(jnp.float32)
@@ -159,19 +156,19 @@
     new_valid = (col_step >= 0) & (col_step < n_steps) & (col_step <= row_step)
     slot_ids = lax.broadcasted_iota(jnp.int32, (pad_q, num_slots), 1)
     over_lanes = (((1,), (1,)), ((), ()))
-    base = (pl.program_id(0) * pl.num_programs(1) + pl.program_id(1)) * step_rows
+    base = pl.num_programs(0) + pl.program_id(0) * step_rows
     for first_row in range(0, step_rows, ATTEND_ROWS):
         rows = range(first_row, min(first_row + ATTEND_ROWS, step_rows))
         queries = [rows_ref[r * stride:r * stride + pad_q, :].astype(jnp.bfloat16) for r in rows]
-        old = [lax.dot_general(q, k_ref[r], over_lanes, preferred_element_type=jnp.float32) for r, q in zip(rows, queries)]
+        old = [lax.dot_general(q, k_ref[0, r], over_lanes, preferred_element_type=jnp.float32) for r, q in zip(rows, queries)]
         new = [lax.dot_general(q, q, over_lanes, preferred_element_type=jnp.float32) for q in queries]
-        old = [jnp.where(slot_ids < pos_ref[base + r], s * score_scale, -jnp.inf) for r, s in zip(rows, old)]
+        old = [jnp.where(slot_ids < meta_ref[base + r], s * score_scale, -jnp.inf) for r, s in zip(rows, old)]
         new = [jnp.where(new_valid, s * score_scale, -jnp.inf) for s in new]
         peak = [jnp.maximum(jnp.max(a, axis=-1, keepdims=True), jnp.max(c, axis=-1, keepdims=True)) for a, c in zip(old, new)]
         old = [jnp.exp(s - m) for s, m in zip(old, peak)]
         new = [jnp.exp(s - m) for s, m in zip(new, peak)]
         weight_sum = [jnp.sum(a, axis=-1, keepdims=True) + jnp.sum(c, axis=-1, keepdims=True) for a, c in zip(old, new)]
-        mixed = [jnp.dot(w.astype(jnp.bfloat16), v_ref[r], preferred_element_type=jnp.float32) for r, w in zip(rows, old)]
+        mixed = [jnp.dot(w.astype(jnp.bfloat16), v_ref[0, r], preferred_element_type=jnp.float32) for r, w in zip(rows, old)]
         values_new = [rows_ref[r * stride + n_steps:r * stride + n_steps + pad_q, :].astype(jnp.bfloat16) for r in rows]
         fresh = [jnp.dot(w.astype(jnp.bfloat16), v, preferred_element_type=jnp.float32) for w, v in zip(new, values_new)]
         mixed = [(a + c) / s for a, c, s in zip(mixed, fresh, weight_sum)]
@@ -182,30 +179,29 @@
         out_ref[0, q_idx] = mixed_ref[at:at + step_rows, :].astype(out_ref.dtype)
 
 
-def attend_local(got, k_own, v_own, start_pos, n_steps):
-    n_dev, num_sent, num_rows, head_dim = got.shape
-    num_slots = k_own.shape[1]
+def attend_local(sent, k_blocks, v_blocks, block_ids, first_slots, row_block, n_steps):
+    n_dev, num_sent, _, head_dim = sent.shape
+    step_rows = first_slots.shape[1]
+    num_slots = k_blocks.shape[2]
     num_q = num_sent - 2 * n_steps
-    step_rows = num_rows
-    inner = num_rows // step_rows
     pad_q = num_sent + n_steps
     stride = num_sent + 1 - num_sent % 2
-    cache_spec = pl.BlockSpec((step_rows, num_slots, head_dim), lambda p, b, pos: (p * inner + b, 0, 0))
+    cache_spec = pl.BlockSpec((1, step_rows, num_slots, head_dim), lambda p, meta: (p, 0, 0, 0))
     return pl.pallas_call(
         functools.partial(attend_kernel, n_steps, head_dim ** -0.5),
-        out_shape=jax.ShapeDtypeStruct((n_dev, num_q, num_rows, head_dim), got.dtype),
+        out_shape=jax.ShapeDtypeStruct((n_dev, num_q, step_rows, head_dim), sent.dtype),
         grid_spec=pltpu.PrefetchScalarGridSpec(
             num_scalar_prefetch=1,
-            grid=(n_dev, inner),
-            in_specs=[pl.BlockSpec((1, num_sent, step_rows, head_dim), lambda p, b, pos: (p, 0, b, 0)), cache_spec, cache_spec],
-            out_specs=pl.BlockSpec((1, num_q, step_rows, head_dim), lambda p, b, pos: (p, 0, b, 0)),
+            grid=(n_dev,),
+            in_specs=[pl.BlockSpec((1, num_sent, step_rows, head_dim), lambda p, meta: (meta[p], 0, row_block, 0)), cache_spec, cache_spec],
+            out_specs=pl.BlockSpec((1, num_q, step_rows, head_dim), lambda p, meta: (meta[p], 0, 0, 0)),
             scratch_shapes=[
                 pltpu.VMEM((step_rows * stride + 16, head_dim), jnp.float32),
                 pltpu.VMEM((pad_q * (step_rows + 1) + 8, head_dim), jnp.float32),
             ],
         ),
-        cost_estimate=pl.CostEstimate(flops=10**9, bytes_accessed=4 * k_own.size, transcendentals=0),
-    )(start_pos, got, k_own, v_own)
+        cost_estimate=pl.CostEstimate(flops=10**9, bytes_accessed=4 * n_dev * step_rows * num_slots * head_dim, transcendentals=0),
+    )(jnp.concatenate([block_ids, first_slots.reshape(-1)]).astype(jnp.int32), sent, k_blocks, v_blocks)
 
 
 def solution(mesh):
@@ -227,7 +223,8 @@
         def swap_cache(own, row_base, chunk_rows):
             return [swap(lax.dynamic_slice_in_dim(own, jnp.bitwise_xor(me, rel_idx) * num_rows + row_base, chunk_rows), rel_idx) for rel_idx in SWAP_ORDER]
 
-        cuts_k = cuts(num_rows, K_CUTS)
+        cuts_k = [(lo * num_rows // 32, n * num_rows // 32) for lo, n in K_CHUNKS]
+        far_rows, near_rows = cuts_k[0]
         positions = my_pos[None, :] + jnp.arange(n_steps)[:, None]
         queries, keys_new, values_new = project(hidden_in, positions, attn_norm, w_q, w_k, w_v, q_norm, k_norm)
         group = queries.shape[2] // n_dev
@@ -235,22 +232,30 @@
         k_send = keys_new.transpose(2, 0, 1, 3)
         v_send = values_new.transpose(2, 0, 1, 3)
         sent = jnp.concatenate([q_send, k_send, v_send], axis=1)
-        k_later, sent = lax.optimization_barrier((k_own, sent))
+        k_later, v_later, sent = lax.optimization_barrier((k_own, v_own, sent))
         k_got = [swap_cache(k_later if i else k_own, *c) for i, c in enumerate(cuts_k)]
-        got = lax.all_to_all(sent, 'x', 0, 0, tiled=True)
-        mixed = attend_local(got, k_own, v_own, start_pos, n_steps)
-        v_got = lax.all_to_all(v_own, 'x', 0, 0, tiled=True).reshape(n_dev, num_rows, num_slots, head_dim)
+        v_near = swap_cache(v_later, far_rows, near_rows)
+        got = lax.all_to_all(sent[:, :, :far_rows], 'x', 0, 0, tiled=True)
+        peers = jnp.arange(n_dev, dtype=jnp.int32)
+        by_peer = (n_dev, num_rows, num_slots, head_dim)
+        mixed = attend_local(got, k_own.reshape(by_peer), v_own.reshape(by_peer), peers, start_pos.reshape(n_dev, num_rows)[:, :far_rows], 0, n_steps)
+        v_got = lax.all_to_all(v_later.reshape(by_peer)[:, :far_rows], 'x', 0, 0, tiled=True)
         back = lax.all_to_all(mixed, 'x', 0, 0, tiled=True)
-        attended = back.reshape(n_dev, n_steps, group, num_rows, head_dim).transpose(1, 3, 0, 2, 4).reshape(n_steps, num_rows, n_dev * group, head_dim)
+        head_ids = jnp.bitwise_xor(me, jnp.array((0,) + SWAP_ORDER, dtype=jnp.int32))
+        k_near, v_near_late, _ = lax.optimization_barrier((k_got[0], v_near, mixed))
+        near = [jnp.stack([lax.dynamic_slice_in_dim(own, me * num_rows + far_rows, near_rows)] + blocks) for own, blocks in ((k_later, k_near), (v_later, v_near_late))]
+        mixed_near = attend_local(sent, *near, head_ids, jnp.broadcast_to(my_pos[far_rows:], (n_dev, near_rows)), far_rows // near_rows, n_steps)
+        attended = jnp.concatenate([back, mixed_near], axis=2)
+        attended = attended.reshape(n_dev, n_steps, group, num_rows, head_dim).transpose(1, 3, 0, 2, 4).reshape(n_steps, num_rows, n_dev * group, head_dim)
         out_hidden = finish(hidden_in, attended, w_o, mlp_norm, w_gate, w_up, w_down)
-        meta = jnp.concatenate([jnp.bitwise_xor(me, jnp.array((0,) + SWAP_ORDER)), my_pos]).astype(jnp.int32)
-        k_out, v_out = None, merge_all(v_got, values_new, meta)
-        for chunk_idx, ((row_base, chunk_rows), k_blocks) in enumerate(zip(cuts_k, k_got)):
-            if chunk_idx == 2:
-                meta, out_hidden = lax.optimization_barrier((meta, out_hidden))
-            if chunk_idx == len(cuts_k) - 1:
-                meta, v_out = lax.optimization_barrier((meta, v_out))
-            k_out = merge_chunk(k_own, k_blocks, keys_new, meta, k_out, row_base, num_rows)
+        meta = jnp.concatenate([head_ids, my_pos]).astype(jnp.int32)
+        k_out = merge_chunk(k_own, k_got[0], keys_new, meta, None, *cuts_k[0][:1], num_rows)
+        v_out = merge_chunk(v_own, v_near, values_new, meta, None, *cuts_k[0][:1], num_rows)
+        meta, out_hidden = lax.optimization_barrier((meta, out_hidden))
+        k_out = merge_chunk(k_own, k_got[1], keys_new, meta, k_out, cuts_k[1][0], num_rows)
+        v_out = merge_first(v_got, values_new, meta, v_out)
+        meta, v_out = lax.optimization_barrier((meta, v_out))
+        k_out = merge_chunk(k_own, k_got[2], keys_new, meta, k_out, cuts_k[2][0], num_rows)
         return out_hidden, k_out, v_out
 
     return jax.shard_map(local_run, mesh=mesh, in_specs=(P('dp'), row_spec, cache_in, cache_in) + (P(),) * 11, out_specs=(row_spec, cache_out, cache_out), check_vma=False)

time: 514 us -> 517 us (level)
  local copies, waits for them, and re-layouts: 26.6 us -> 64.2 us
  waiting for transfers between devices: 151 us -> 114 us
  Pallas kernels: 56.6 us -> 64.4 us
    ppermute x28, waiting for transfers between devices: 137 us -> 100 us  [swap(): return lax.ppermute(arr, 'x', [(d, d ^ rel_idx) for d in range(n_dev)])]
    unnamed x33 -> x66, local copies, waits for them, and re-layouts: 5.56 us -> 26.8 us
    all_to_all x2, waiting for transfers between devices: 13.9 us -> 0.01 us  [the longest x1 0.01 us: local_run(): got = lax.all_to_all(sent[:, :, :far_rows], 'x', 0, 0, tiled=True)]
    all_to_all x1, waiting for transfers between devices: 0.01 us -> 13.7 us  [local_run(): back = lax.all_to_all(mixed, 'x', 0, 0, tiled=True)]
    slice x0 -> x3, local copies, waits for them, and re-layouts: none -> 13.3 us  [the longest x1 11.6 us: local_run(): v_later.reshape(by_peer)[:, :far_rows]]
    pallas_call x1 -> x2, Pallas kernels: 21.6 us -> 27.2 us  [attend_local(): pl.pallas_call(functools.partial(attend_kernel, n_steps, head_dim ** (-0....]
  transfers between devices with their start and end apart: 31 -> 31, of which waited for: 9 -> 5; matrix products, arithmetic and copies ran while one was open for 43% -> 56% of each run, Pallas kernels for 10% -> 12%
where the time goes in v4:
time: 517 us; the launch traced here: 516 us
  matrix products  225 us (44%)
  waiting for transfers between devices  114 us (22%)
  Pallas kernels  64.4 us (12%)
  local copies, waits for them, and re-layouts  64.2 us (12%)
  starting transfers between devices  39.2 us (8%)
  other arithmetic  8.47 us (2%)
    ppermute x28, waiting for transfers between devices, swap(): return lax.ppermute(arr, 'x', [(d, d ^ rel_idx) for d in range(n_dev)])  100 us
    dot_general x1, matrix products, finish(): jnp.einsum('sbd,df->sbf', normed, w_up, preferred_element_type=jnp.float32)  60.5 us
    dot_general x1, matrix products, finish(): jnp.einsum('sbd,df->sbf', normed, w_gate, preferred_element_type=jnp.floa...  60 us
    dot_general x1, matrix products, finish(): jnp.einsum('sbf,fd->sbd', activated, w_down, preferred_element_type=jnp.f...  58.1 us
    ppermute x28, starting transfers between devices, swap(): return lax.ppermute(arr, 'x', [(d, d ^ rel_idx) for d in range(n_dev)])  29.3 us
    pallas_call x2, Pallas kernels, attend_local(): pl.pallas_call(functools.partial(attend_kernel, n_steps, head_dim ** (-0....  27.2 us
    unnamed x66, local copies, waits for them, and re-layouts  26.8 us
    pallas_call x4, Pallas kernels, merge_chunk(): pl.pallas_call(functools.partial(merge_chunk_kernel, row_base, n_dev), ou...  24.9 us
  transfers between devices with their start and end apart: 31, of which 5 were waited for; matrix products, arithmetic and copies ran while one was open for 56% of the time, Pallas kernels for 12%

profile of v4, /device:TPU:0, one launch (start us, length us, event | category | flops | bytes accessed | tf_op | source)
XLA Modules:
  0.0 516.1 jit_solution(15384431550606713147)
XLA Ops:
  0.7 4.0 dynamic-slice_bitcast_fusion
  4.7 3.3 collective-permute-start
  8.0 1.5 collective-permute-start.1
  9.8 3.0 collective-permute-start.4
  13.1 5.7 %fusion.58 = bf16[4,32,1024]{2,1,0:T(8,128)(2,1)S(1)} fusion(bf16[5120,1024]{1,0:T(8,128)(2,1)} %param.23, bf16[4,32,5120]{2,1,0:T(8,128)(2,1)S(1)} %copy-done, f32[5120]{0:T(1024)S(1)} %convert_element_type.52, f32[4,32]{1,0:T(4,128)S(1)} %add_rsqrt_fusion.3), kind=kOutput, calls=%fused_computation.48 | convolution fusion | flops 1344929792 | bytes 12079616 | tf_op jit(solution)/shard_map/sbd,de->sbe/dot_general | solution.py:39
  18.9 0.7 copy-done.6
  20.2 1.6 fusion.20
  22.2 18.1 %fusion.8 = f32[4,32,5120]{2,1,0:T(8,128)S(1)} fusion(bf16[5120,5120]{1,0:T(8,128)(2,1)} %param.21, bf16[4,32,5120]{2,1,0:T(8,128)(2,1)S(1)} %copy-done, f32[5120]{0:T(1024)S(1)} %convert_element_type.52, f32[4,32]{1,0:T(4,128)S(1)} %add_rsqrt_fusion.3), kind=kOutput, calls=%fused_computation.8 | convolution fusion | flops 6713507840 | bytes 56381952 | tf_op jit(solution)/shard_map/sbd,de->sbe/dot_general | solution.py:37
  40.9 1.0 copy-done.1
  41.9 0.7 fusion.50
  43.0 2.2 fusion.51
  45.7 0.9 subtract_convert_fusion
  46.9 0.7 maximum_bitcast_fusion
  48.2 1.6 slice.29
  49.9 3.2 all-to-all-start
  53.5 3.6 constant_dynamic-slice_fusion.14
  57.1 2.4 collective-permute-start.5
  62.0 2.3 bitcast_dynamic-update-slice_fusion.7
  64.3 0.9 collective-permute-start.9
  65.1 17.4 %collective-permute-done.5.refs_6_ = bf16[8,256,128]{2,1,0:T(8,128)(2,1)S(1)} collective-permute-done((bf16[8,256,128]{2,1,0:T(8,128)(2,1)S(1)}, bf16[8,256,128]{2,1,0:T(8,128)(2,1)S(1)}, u32[]{:S(2)}, u32[]{:S(2)}) %collective-permute-start.5) | collective-permute-done | bytes 524320 | tf_op jit(solution)/shard_map/ppermute | solution.py:221
  82.5 1.0 collective-permute-start.10
  83.5 1.5 collective-permute-start.11
  85.0 8.8 %collective-permute-done.7.refs_1_ = bf16[8,256,128]{2,1,0:T(8,128)(2,1)S(1)} collective-permute-done((bf16[8,256,128]{2,1,0:T(8,128)(2,1)S(1)}, bf16[8,256,128]{2,1,0:T(8,128)(2,1)S(1)}, u32[]{:S(2)}, u32[]{:S(2)}) %collective-permute-start.7) | collective-permute-done | bytes 524320 | tf_op jit(solution)/shard_map/ppermute | solution.py:221
  94.1 1.4 collective-permute-start.13
  96.2 11.6 %slice.36 = bf16[8,24,256,128]{3,2,1,0:T(8,128)(2,1)} slice(bf16[8,32,256,128]{3,2,1,0:T(8,128)(2,1)} %bitcast.158), slice={[0:8], [0:24], [0:256], [0:128]} | slice | bytes 25165824 | tf_op jit(solution)/shard_map/slice | solution.py:242
  107.9 2.7 constant_dynamic-slice_fusion.7
  110.6 7.2 %constant_dynamic-slice_fusion = (bf16[20,256,128]{2,1,0:T(8,128)(2,1)}, bf16[20,256,128]{2,1,0:T(8,128)(2,1)}, bf16[20,256,128]{2,1,0:T(8,128)(2,1)}, bf16[20,2...) fusion(bf16[256,256,128]{2,1,0:T(8,128)(2,1)} %bitcast.151, ...), kind=kLoop, calls=%fused_computation.83 | loop fusion | bytes 18350108 | tf_op jit(solution)/shard_map/dynamic_slice | solution.py:224
  117.9 4.8 shard_map.179.refs_9_
  122.6 1.5 collective-permute-start.14
  124.9 2.6 collective-permute-done.12.refs_6_
  128.6 4.8 shard_map.177.partial_ref
  133.4 17.5 %shard_map.175 = bf16[8,20,24,128]{3,2,1,0:T(8,128)(2,1)} custom-call(s32[200]{0:T(256)} %pad_add_fusion.meta_ref, bf16[8,28,24,128]{3,2,1,0:T(8,128)(2,1)} %all-to-all-done.sent_ref, bf16[8,32,256,128]{3,2,1,0:T(8,128)(2,1)} %bitcast.153, bf16[8,32,256,128]{3,2,1,0:T(8,128)(2,1)} %bitcast.160), custom_call_target="tpu_custom_call" | custom-call | flops 1000000000 | bytes 25165824 | tf_op jit(solution)/shard_map/pallas_call | solution.py:190
  150.9 2.6 all-to-all-start.1
  153.5 1.9 bitcast_dynamic-update-slice_fusion.14
  155.5 1.9 bitcast_dynamic-update-slice_fusion.13
  157.4 1.9 bitcast_dynamic-update-slice_fusion.12
  159.3 1.9 bitcast_dynamic-update-slice_fusion.11
  161.2 1.9 bitcast_dynamic-update-slice_fusion.10
  163.1 0.8 bitcast_dynamic-update-slice_fusion.9
  163.9 0.8 bitcast_dynamic-update-slice_fusion.8.k_ref
  164.8 0.8 bitcast_dynamic-update-slice_fusion.6
  165.6 1.9 bitcast_dynamic-update-slice_fusion.5
  167.5 1.9 bitcast_dynamic-update-slice_fusion.4
  169.4 1.9 bitcast_dynamic-update-slice_fusion.3
  171.3 1.9 bitcast_dynamic-update-slice_fusion.2
  173.2 1.9 bitcast_dynamic-update-slice_fusion.1
  175.0 1.9 bitcast_dynamic-update-slice_fusion.v_ref
  176.9 9.7 %shard_map.176 = bf16[8,20,8,128]{3,2,1,0:T(8,128)(2,1)} custom-call(s32[72]{0:T(128)} %pad_add_fusion.2.meta_ref, bf16[8,28,32,128]{3,2,1,0:T(8,128)(2,1)} %copy-done.4, bf16[8,8,256,128]{3,2,1,0:T(8,128)(2,1)} %bitcast_dynamic-update-slice_fusion.8.k_ref, bf16[8,8,256,128]{3,2,1,0:T(8,128)(2,1)} %bitcast_dynamic-update-slice_fusion.v_ref), custom_call_target="tpu_custom_call" | custom-call | flops 1000000000 | bytes 8388608 | tf_op jit(solution)/shard_map/pallas_call | solution.py:190
  186.6 13.7 %all-to-all-done.1 = bf16[8,20,24,128]{3,2,1,0:T(8,128)(2,1)S(1)} async-done(((bf16[8,20,24,128]{3,2,1,0:T(8,128)(2,1)}), bf16[8,20,24,128]{3,2,1,0:T(8,128)(2,1)S(1)}, u32[]{:S(2)}, u32[]{:S(2)}) %all-to-all-start.1) | async-done | bytes 983072 | tf_op jit(solution)/shard_map/all_to_all | solution.py:243
  200.3 4.1 all-to-all-start.2
  205.3 2.3 reshape_reshape.3
  207.6 20.8 %multiply_reduce_fusion = (f32[4,32]{1,0:T(4,128)S(1)}, f32[4,32,5120]{2,1,0:T(8,128)}) fusion(bf16[4,32,5120]{2,1,0:T(8,128)(2,1)} %reshape_reshape.3, bf16[5120,5120]{1,0:T(8,128)(2,1)} %param.26, bf16[4,32,5120]{2,1,0:T(8,128)(2,1)S(1)} %copy-done), kind=kOutput, calls=%fused_computation.37 | convolution fusion | flops 6714818560 | bytes 57672192 | tf_op jit(solution)/shard_map/sbe,ed->sbd/dot_general | solution.py:48
  228.4 60.0 %fusion.4 = f32[4,32,17408]{2,1,0:T(8,128)} fusion(bf16[5120,17408]{1,0:T(8,128)(2,1)} %param.28, f32[4,32,5120]{2,1,0:T(8,128)} %get-tuple-element.80, f32[5120]{0:T(1024)S(1)} %convert_element_type.61, f32[4,32]{1,0:T(4,128)S(1)} %add_rsqrt_fusion.2), kind=kOutput, calls=%fused_computation.4 | convolution fusion | flops 22818979840 | bytes 189813248 | tf_op jit(solution)/shard_map/sbd,df->sbf/dot_general | solution.py:51
  288.4 1.6 collective-permute-start.24
  290.0 1.4 collective-permute-start.25
  291.5 1.2 collective-permute-start.26
  293.1 60.5 %fusion.13.clone.8 = bf16[4,32,17408]{2,1,0:T(8,128)(2,1)} fusion(bf16[5120,17408]{1,0:T(8,128)(2,1)} %param.29, f32[4,32,17408]{2,1,0:T(8,128)} %fusion.4, f32[4,32,5120]{2,1,0:T(8,128)S(1)} %copy-done.2, f32[5120]{0:T(1024)S(1)} %convert_element_type.61, f32[4,32]{1,0:T(4,128)S(1)} %add_rsqrt_fusion.2), kind=kOutput, calls=%fused_computation.11.clone.clone.clone.clone.clone.clone.clone.1 | convolution fusion | flops 22832349184 | bytes 194269696 | tf_op jit(solution)/shard_map/sbd,df->sbf/dot_general | solution.py:52
  353.6 1.2 collective-permute-start.16
  354.8 71.3 %collective-permute-done.24.refs_4_ = bf16[20,256,128]{2,1,0:T(8,128)(2,1)} collective-permute-done((bf16[20,256,128]{2,1,0:T(8,128)(2,1)}, bf16[20,256,128]{2,1,0:T(8,128)(2,1)}, u32[]{:S(2)}, u32[]{:S(2)}) %collective-permute-start.24) | collective-permute-done | bytes 1310752 | tf_op jit(solution)/shard_map/ppermute | solution.py:221
  426.4 2.8 collective-permute-start.18
  429.5 58.1 %fusion.41 = bf16[4,32,5120]{2,1,0:T(8,128)(2,1)} fusion(f32[4,32,5120]{2,1,0:T(8,128)S(1)} %copy-done.2, bf16[17408,5120]{1,0:T(8,128)(2,1)} %param.30, bf16[4,32,17408]{2,1,0:T(8,128)(2,1)} %fusion.13.clone.8), kind=kOutput, calls=%fused_computation.25 | convolution fusion | flops 22818324480 | bytes 186646528 | tf_op jit(solution)/shard_map/sbf,fd->sbd/dot_general | solution.py:54
  487.6 11.3 %shard_map.180.refs_9_ = bf16[32,256,8,128]{3,2,1,0:T(8,128)(2,1)} custom-call(s32[40]{0:T(128)} %pad_add_fusion.1.meta_ref, bf16[256,256,128]{2,1,0:T(8,128)(2,1)} %bitcast.154, bf16[20,256,128]{2,1,0:T(8,128)(2,1)} %collective-permute-done.21.refs_1_, bf16[20,256,128]{2,1,0:T(8,128)(2,1)} %collective-permute-done.22.refs_2_, ...), custom_call_target="tpu_custom_call", output_to_operand_aliasing={{}: (10, {})} | custom-call | flops 100000000 | bytes 20971520 | tf_op jit(solution)/shard_map/pallas_call | solution.py:102
  498.9 12.3 %shard_map.178 = bf16[32,256,8,128]{3,2,1,0:T(8,128)(2,1)} custom-call(s32[40]{0:T(128)} %pad_add_fusion.1.meta_ref, bf16[8,24,256,128]{3,2,1,0:T(8,128)(2,1)} %all-to-all-done.2.blocks_ref, bf16[4,32,8,128]{3,2,1,0:T(8,128)(2,1)} %bitcast.173, bf16[32,256,8,128]{3,2,1,0:T(8,128)(2,1)} %shard_map.177.partial_ref), custom_call_target="tpu_custom_call", output_to_operand_aliasing={{}: (3, {})} | custom-call | flops 100000000 | bytes 25165824 | tf_op jit(solution)/shard_map/pallas_call | solution.py:124
  512.1 4.0 shard_map.181
  (126 shorter events, 12.3 us)
Async XLA Ops:
  0.7 12.0 %copy-start.19 = (bf16[5120]{0:T(1024)(128)(2,1)S(1)}, bf16[5120]{0:T(1024)(128)(2,1)}, u32[]{:S(2)}) copy-start(bf16[5120]{0:T(1024)(128)(2,1)} %param.20) | copy-start | bytes 30724
  0.7 12.0 %copy-start = (bf16[4,32,5120]{2,1,0:T(8,128)(2,1)S(1)}, bf16[4,32,5120]{2,1,0:T(8,128)(2,1)}, u32[]{:S(2)}) copy-start(bf16[4,32,5120]{2,1,0:T(8,128)(2,1)} %param.17) | copy-start | bytes 3932164
  4.7 52.4 %collective-permute-start = (bf16[8,256,128]{2,1,0:T(8,128)(2,1)}, bf16[8,256,128]{2,1,0:T(8,128)(2,1)}, u32[]{:S(2)}, u32[]{:S(2)}) collective-permute-start(bf16[8,256,128]{2,1,0:T(8,128)(2,1)} %get-tuple-element.71), channel_id=1, source_target_pairs={{0,2},{1,3},{2,0},{3,1},{4,6},{5,7},{6,4},{7,5}} | collective-permute-start | bytes 1572872 | tf_op jit(solution)/shard_map/ppermute | solution.py:221
  8.0 51.5 %collective-permute-start.1 = (bf16[8,256,128]{2,1,0:T(8,128)(2,1)}, bf16[8,256,128]{2,1,0:T(8,128)(2,1)}, u32[]{:S(2)}, u32[]{:S(2)}) collective-permute-start(bf16[8,256,128]{2,1,0:T(8,128)(2,1)} %get-tuple-element.70), channel_id=1, source_target_pairs={{0,4},{1,5},{2,6},{3,7},{4,0},{5,1},{6,2},{7,3}} | collective-permute-start | bytes 1572872 | tf_op jit(solution)/shard_map/ppermute | solution.py:221
  9.5 50.4 %collective-permute-start.2 = (bf16[8,256,128]{2,1,0:T(8,128)(2,1)}, bf16[8,256,128]{2,1,0:T(8,128)(2,1)}, u32[]{:S(2)}, u32[]{:S(2)}) collective-permute-start(bf16[8,256,128]{2,1,0:T(8,128)(2,1)} %get-tuple-element.69), channel_id=1, source_target_pairs={{0,3},{1,2},{2,1},{3,0},{4,7},{5,6},{6,5},{7,4}} | collective-permute-start | bytes 1572872 | tf_op jit(solution)/shard_map/ppermute | solution.py:221
  9.5 50.9 %collective-permute-start.3 = (bf16[8,256,128]{2,1,0:T(8,128)(2,1)}, bf16[8,256,128]{2,1,0:T(8,128)(2,1)}, u32[]{:S(2)}, u32[]{:S(2)}) collective-permute-start(bf16[8,256,128]{2,1,0:T(8,128)(2,1)} %get-tuple-element.68), channel_id=1, source_target_pairs={{0,5},{1,4},{2,7},{3,6},{4,1},{5,0},{6,3},{7,2}} | collective-permute-start | bytes 1572872 | tf_op jit(solution)/shard_map/ppermute | solution.py:221
  9.8 54.5 %collective-permute-start.4 = (bf16[8,256,128]{2,1,0:T(8,128)(2,1)}, bf16[8,256,128]{2,1,0:T(8,128)(2,1)}, u32[]{:S(2)}, u32[]{:S(2)}) collective-permute-start(bf16[8,256,128]{2,1,0:T(8,128)(2,1)} %get-tuple-element.67), channel_id=1, source_target_pairs={{0,6},{1,7},{2,4},{3,5},{4,2},{5,3},{6,0},{7,1}} | collective-permute-start | bytes 1572872 | tf_op jit(solution)/shard_map/ppermute | solution.py:221
  13.1 6.5 %copy-start.22 = (bf16[128]{0:T(256)(128)(2,1)S(1)}, bf16[128]{0:T(256)(128)(2,1)}, u32[]{:S(2)}) copy-start(bf16[128]{0:T(256)(128)(2,1)} %param.25) | copy-start | bytes 772
  13.1 7.1 %copy-start.3 = (bf16[5120,1024]{1,0:T(8,128)(2,1)S(1)}, bf16[5120,1024]{1,0:T(8,128)(2,1)}, u32[]{:S(2)}) copy-start(bf16[5120,1024]{1,0:T(8,128)(2,1)} %param.22) | copy-start | bytes 31457284
  18.9 0.7 copy-start.6
  20.2 1.9 copy-start.21
  20.2 2.0 copy-start.23
  40.4 1.5 copy-start.1
  46.8 1.1 copy-start.5
  48.2 1.8 copy-start.4
  49.9 83.5 %all-to-all-start = ((bf16[8,28,24,128]{3,2,1,0:T(8,128)(2,1)}), bf16[8,28,24,128]{3,2,1,0:T(8,128)(2,1)}, u32[]{:S(2)}, u32[]{:S(2)}) async-start(bf16[8,28,24,128]{3,2,1,0:T(8,128)(2,1)} %slice.29), calls=%async_computation | async-start | bytes 2752512 | tf_op jit(solution)/shard_map/all_to_all | solution.py:238
  53.4 3.7 copy-start.15
  53.4 6.1 %copy-start.14 = (bf16[8,256,128]{2,1,0:T(8,128)(2,1)S(1)}, bf16[8,256,128]{2,1,0:T(8,128)(2,1)}, u32[]{:S(2)}) copy-start(bf16[8,256,128]{2,1,0:T(8,128)(2,1)} %get-tuple-element.66) | copy-start | bytes 1572868
  53.4 7.3 %copy-start.24 = (s32[8]{0:T(128)S(1)}, s32[8]{0:T(128)}, u32[]{:S(2)}) copy-start(s32[8]{0:T(128)} %constant.79.clone) | copy-start | bytes 100
  53.4 42.7 %copy-start.20 = (bf16[5120]{0:T(1024)(128)(2,1)S(1)}, bf16[5120]{0:T(1024)(128)(2,1)}, u32[]{:S(2)}) copy-start(bf16[5120]{0:T(1024)(128)(2,1)} %param.27) | copy-start | bytes 30724
  57.1 25.4 %collective-permute-start.5 = (bf16[8,256,128]{2,1,0:T(8,128)(2,1)S(1)}, bf16[8,256,128]{2,1,0:T(8,128)(2,1)S(1)}, u32[]{:S(2)}, u32[]{:S(2)}) collective-permute-start(bf16[8,256,128]{2,1,0:T(8,128)(2,1)S(1)} %copy-done.15), channel_id=1, source_target_pairs={{0,7},{1,6},{2,5},{3,4},{4,3},{5,2},{6,1},{7,0}} | collective-permute-start | bytes 1572872 | tf_op jit(solution)/shard_map/ppermute | solution.py:221
  59.5 24.0 %collective-permute-start.6 = (bf16[8,256,128]{2,1,0:T(8,128)(2,1)S(1)}, bf16[8,256,128]{2,1,0:T(8,128)(2,1)S(1)}, u32[]{:S(2)}, u32[]{:S(2)}) collective-permute-start(bf16[8,256,128]{2,1,0:T(8,128)(2,1)S(1)} %copy-done.14), channel_id=1, source_target_pairs={{0,1},{1,0},{2,3},{3,2},{4,5},{5,4},{6,7},{7,6}} | collective-permute-start | bytes 1572872 | tf_op jit(solution)/shard_map/ppermute | solution.py:221
  59.9 34.0 %collective-permute-start.7 = (bf16[8,256,128]{2,1,0:T(8,128)(2,1)S(1)}, bf16[8,256,128]{2,1,0:T(8,128)(2,1)S(1)}, u32[]{:S(2)}, u32[]{:S(2)}) collective-permute-start(bf16[8,256,128]{2,1,0:T(8,128)(2,1)S(1)} %get-tuple-element.65), channel_id=1, source_target_pairs={{0,2},{1,3},{2,0},{3,1},{4,6},{5,7},{6,4},{7,5}} | collective-permute-start | bytes 1572872 | tf_op jit(solution)/shard_map/ppermute | solution.py:221
  60.4 33.6 %collective-permute-start.8 = (bf16[8,256,128]{2,1,0:T(8,128)(2,1)S(1)}, bf16[8,256,128]{2,1,0:T(8,128)(2,1)}, u32[]{:S(2)}, u32[]{:S(2)}) collective-permute-start(bf16[8,256,128]{2,1,0:T(8,128)(2,1)S(1)} %get-tuple-element.64), channel_id=1, source_target_pairs={{0,4},{1,5},{2,6},{3,7},{4,0},{5,1},{6,2},{7,3}} | collective-permute-start | bytes 1572872 | tf_op jit(solution)/shard_map/ppermute | solution.py:221
  64.3 58.4 %collective-permute-start.9 = (bf16[8,256,128]{2,1,0:T(8,128)(2,1)}, bf16[8,256,128]{2,1,0:T(8,128)(2,1)}, u32[]{:S(2)}, u32[]{:S(2)}) collective-permute-start(bf16[8,256,128]{2,1,0:T(8,128)(2,1)} %get-tuple-element.63), channel_id=1, source_target_pairs={{0,3},{1,2},{2,1},{3,0},{4,7},{5,6},{6,5},{7,4}} | collective-permute-start | bytes 1572872 | tf_op jit(solution)/shard_map/ppermute | solution.py:221
  82.5 25.3 %copy-start.7 = (bf16[8,256,128]{2,1,0:T(8,128)(2,1)}, bf16[8,256,128]{2,1,0:T(8,128)(2,1)S(1)}, u32[]{:S(2)}) copy-start(bf16[8,256,128]{2,1,0:T(8,128)(2,1)S(1)} %collective-permute-done.5.refs_6_) | copy-start | bytes 1572868
  82.5 41.6 %collective-permute-start.10 = (bf16[8,256,128]{2,1,0:T(8,128)(2,1)}, bf16[8,256,128]{2,1,0:T(8,128)(2,1)}, u32[]{:S(2)}, u32[]{:S(2)}) collective-permute-start(bf16[8,256,128]{2,1,0:T(8,128)(2,1)} %get-tuple-element.62), channel_id=1, source_target_pairs={{0,5},{1,4},{2,7},{3,6},{4,1},{5,0},{6,3},{7,2}} | collective-permute-start | bytes 1572872 | tf_op jit(solution)/shard_map/ppermute | solution.py:221
  83.5 24.3 %copy-start.9 = (bf16[8,256,128]{2,1,0:T(8,128)(2,1)}, bf16[8,256,128]{2,1,0:T(8,128)(2,1)S(1)}, u32[]{:S(2)}) copy-start(bf16[8,256,128]{2,1,0:T(8,128)(2,1)S(1)} %collective-permute-done.6.refs_7_) | copy-start | bytes 1572868
  83.5 41.1 %collective-permute-start.11 = (bf16[8,256,128]{2,1,0:T(8,128)(2,1)}, bf16[8,256,128]{2,1,0:T(8,128)(2,1)}, u32[]{:S(2)}, u32[]{:S(2)}) collective-permute-start(bf16[8,256,128]{2,1,0:T(8,128)(2,1)} %get-tuple-element.61), channel_id=1, source_target_pairs={{0,6},{1,7},{2,4},{3,5},{4,2},{5,3},{6,0},{7,1}} | collective-permute-start | bytes 1572872 | tf_op jit(solution)/shard_map/ppermute | solution.py:221
  93.9 14.0 %copy-start.11 = (bf16[8,256,128]{2,1,0:T(8,128)(2,1)}, bf16[8,256,128]{2,1,0:T(8,128)(2,1)S(1)}, u32[]{:S(2)}) copy-start(bf16[8,256,128]{2,1,0:T(8,128)(2,1)S(1)} %collective-permute-done.7.refs_1_) | copy-start | bytes 1572868
  93.9 33.7 %collective-permute-start.12 = (bf16[8,256,128]{2,1,0:T(8,128)(2,1)}, bf16[8,256,128]{2,1,0:T(8,128)(2,1)}, u32[]{:S(2)}, u32[]{:S(2)}) collective-permute-start(bf16[8,256,128]{2,1,0:T(8,128)(2,1)} %get-tuple-element.60), channel_id=1, source_target_pairs={{0,7},{1,6},{2,5},{3,4},{4,3},{5,2},{6,1},{7,0}} | collective-permute-start | bytes 1572872 | tf_op jit(solution)/shard_map/ppermute | solution.py:221
  94.1 34.0 %collective-permute-start.13 = (bf16[8,256,128]{2,1,0:T(8,128)(2,1)}, bf16[8,256,128]{2,1,0:T(8,128)(2,1)}, u32[]{:S(2)}, u32[]{:S(2)}) collective-permute-start(bf16[8,256,128]{2,1,0:T(8,128)(2,1)} %get-tuple-element.59), channel_id=1, source_target_pairs={{0,1},{1,0},{2,3},{3,2},{4,5},{5,4},{6,7},{7,6}} | collective-permute-start | bytes 1572872 | tf_op jit(solution)/shard_map/ppermute | solution.py:221
  122.6 165.8 %collective-permute-start.14 = (bf16[4,256,128]{2,1,0:T(8,128)(2,1)}, bf16[4,256,128]{2,1,0:T(8,128)(2,1)}, u32[]{:S(2)}, u32[]{:S(2)}) collective-permute-start(bf16[4,256,128]{2,1,0:T(8,128)(2,1)} %get-tuple-element.58), channel_id=1, source_target_pairs={{0,2},{1,3},{2,0},{3,1},{4,6},{5,7},{6,4},{7,5}} | collective-permute-start | bytes 786440 | tf_op jit(solution)/shard_map/ppermute | solution.py:221
  124.1 165.9 %collective-permute-start.15 = (bf16[4,256,128]{2,1,0:T(8,128)(2,1)}, bf16[4,256,128]{2,1,0:T(8,128)(2,1)}, u32[]{:S(2)}, u32[]{:S(2)}) collective-permute-start(bf16[4,256,128]{2,1,0:T(8,128)(2,1)} %get-tuple-element.57), channel_id=1, source_target_pairs={{0,4},{1,5},{2,6},{3,7},{4,0},{5,1},{6,2},{7,3}} | collective-permute-start | bytes 786440 | tf_op jit(solution)/shard_map/ppermute | solution.py:221
  124.6 166.9 %collective-permute-start.21 = (bf16[20,256,128]{2,1,0:T(8,128)(2,1)}, bf16[20,256,128]{2,1,0:T(8,128)(2,1)}, u32[]{:S(2)}, u32[]{:S(2)}) collective-permute-start(bf16[20,256,128]{2,1,0:T(8,128)(2,1)} %get-tuple-element.51), channel_id=1, source_target_pairs={{0,2},{1,3},{2,0},{3,1},{4,6},{5,7},{6,4},{7,5}} | collective-permute-start | bytes 3932168 | tf_op jit(solution)/shard_map/ppermute | solution.py:221
  127.6 165.1 %collective-permute-start.22 = (bf16[20,256,128]{2,1,0:T(8,128)(2,1)}, bf16[20,256,128]{2,1,0:T(8,128)(2,1)}, u32[]{:S(2)}, u32[]{:S(2)}) collective-permute-start(bf16[20,256,128]{2,1,0:T(8,128)(2,1)} %get-tuple-element.50), channel_id=1, source_target_pairs={{0,4},{1,5},{2,6},{3,7},{4,0},{5,1},{6,2},{7,3}} | collective-permute-start | bytes 3932168 | tf_op jit(solution)/shard_map/ppermute | solution.py:221
  128.1 225.5 %collective-permute-start.23 = (bf16[20,256,128]{2,1,0:T(8,128)(2,1)}, bf16[20,256,128]{2,1,0:T(8,128)(2,1)}, u32[]{:S(2)}, u32[]{:S(2)}) collective-permute-start(bf16[20,256,128]{2,1,0:T(8,128)(2,1)} %get-tuple-element.49), channel_id=1, source_target_pairs={{0,3},{1,2},{2,1},{3,0},{4,7},{5,6},{6,5},{7,4}} | collective-permute-start | bytes 3932168 | tf_op jit(solution)/shard_map/ppermute | solution.py:221
  150.9 49.4 %all-to-all-start.1 = ((bf16[8,20,24,128]{3,2,1,0:T(8,128)(2,1)}), bf16[8,20,24,128]{3,2,1,0:T(8,128)(2,1)S(1)}, u32[]{:S(2)}, u32[]{:S(2)}) async-start(bf16[8,20,24,128]{3,2,1,0:T(8,128)(2,1)} %shard_map.175), calls=%async_computation.1 | async-start | bytes 1966080 | tf_op jit(solution)/shard_map/all_to_all | solution.py:243
  153.5 9.6 %copy-start.8 = (bf16[8,256,128]{2,1,0:T(8,128)(2,1)S(1)}, bf16[8,256,128]{2,1,0:T(8,128)(2,1)}, u32[]{:S(2)}) copy-start(bf16[8,256,128]{2,1,0:T(8,128)(2,1)} %copy-done.7) | copy-start | bytes 1572868
  155.5 8.4 %copy-start.10 = (bf16[8,256,128]{2,1,0:T(8,128)(2,1)S(1)}, bf16[8,256,128]{2,1,0:T(8,128)(2,1)}, u32[]{:S(2)}) copy-start(bf16[8,256,128]{2,1,0:T(8,128)(2,1)} %copy-done.9) | copy-start | bytes 1572868
  157.4 7.4 %copy-start.12 = (bf16[8,256,128]{2,1,0:T(8,128)(2,1)S(1)}, bf16[8,256,128]{2,1,0:T(8,128)(2,1)}, u32[]{:S(2)}) copy-start(bf16[8,256,128]{2,1,0:T(8,128)(2,1)} %copy-done.11) | copy-start | bytes 1572868
  186.6 17.8 %copy-start.13 = (bf16[8,20,8,128]{3,2,1,0:T(8,128)(2,1)S(1)}, bf16[8,20,8,128]{3,2,1,0:T(8,128)(2,1)}, u32[]{:S(2)}) copy-start(bf16[8,20,8,128]{3,2,1,0:T(8,128)(2,1)} %shard_map.176) | copy-start | bytes 983044
  200.3 298.7 %all-to-all-start.2 = ((bf16[8,24,256,128]{3,2,1,0:T(8,128)(2,1)}), bf16[8,24,256,128]{3,2,1,0:T(8,128)(2,1)}, u32[]{:S(2)}, u32[]{:S(2)}) async-start(bf16[8,24,256,128]{3,2,1,0:T(8,128)(2,1)} %slice.36), calls=%async_computation.2 | async-start | bytes 25165824 | tf_op jit(solution)/shard_map/all_to_all | solution.py:242
  228.4 64.7 %copy-start.2 = (f32[4,32,5120]{2,1,0:T(8,128)S(1)}, f32[4,32,5120]{2,1,0:T(8,128)}, u32[]{:S(2)}) copy-start(f32[4,32,5120]{2,1,0:T(8,128)} %get-tuple-element.80) | copy-start | bytes 7864324
  288.4 137.6 %collective-permute-start.24 = (bf16[20,256,128]{2,1,0:T(8,128)(2,1)}, bf16[20,256,128]{2,1,0:T(8,128)(2,1)}, u32[]{:S(2)}, u32[]{:S(2)}) collective-permute-start(bf16[20,256,128]{2,1,0:T(8,128)(2,1)} %get-tuple-element.48), channel_id=1, source_target_pairs={{0,5},{1,4},{2,7},{3,6},{4,1},{5,0},{6,3},{7,2}} | collective-permute-start | bytes 3932168 | tf_op jit(solution)/shard_map/ppermute | solution.py:221
  290.0 136.4 %collective-permute-start.25 = (bf16[20,256,128]{2,1,0:T(8,128)(2,1)}, bf16[20,256,128]{2,1,0:T(8,128)(2,1)}, u32[]{:S(2)}, u32[]{:S(2)}) collective-permute-start(bf16[20,256,128]{2,1,0:T(8,128)(2,1)} %get-tuple-element.47), channel_id=1, source_target_pairs={{0,6},{1,7},{2,4},{3,5},{4,2},{5,3},{6,0},{7,1}} | collective-permute-start | bytes 3932168 | tf_op jit(solution)/shard_map/ppermute | solution.py:221
  291.5 137.7 %collective-permute-start.26 = (bf16[20,256,128]{2,1,0:T(8,128)(2,1)}, bf16[20,256,128]{2,1,0:T(8,128)(2,1)}, u32[]{:S(2)}, u32[]{:S(2)}) collective-permute-start(bf16[20,256,128]{2,1,0:T(8,128)(2,1)} %get-tuple-element.46), channel_id=1, source_target_pairs={{0,7},{1,6},{2,5},{3,4},{4,3},{5,2},{6,1},{7,0}} | collective-permute-start | bytes 3932168 | tf_op jit(solution)/shard_map/ppermute | solution.py:221
  292.7 136.6 %collective-permute-start.27 = (bf16[20,256,128]{2,1,0:T(8,128)(2,1)}, bf16[20,256,128]{2,1,0:T(8,128)(2,1)}, u32[]{:S(2)}, u32[]{:S(2)}) collective-permute-start(bf16[20,256,128]{2,1,0:T(8,128)(2,1)} %get-tuple-element.45), channel_id=1, source_target_pairs={{0,1},{1,0},{2,3},{3,2},{4,5},{5,4},{6,7},{7,6}} | collective-permute-start | bytes 3932168 | tf_op jit(solution)/shard_map/ppermute | solution.py:221
  353.6 157.6 %collective-permute-start.16 = (bf16[4,256,128]{2,1,0:T(8,128)(2,1)}, bf16[4,256,128]{2,1,0:T(8,128)(2,1)S(1)}, u32[]{:S(2)}, u32[]{:S(2)}) collective-permute-start(bf16[4,256,128]{2,1,0:T(8,128)(2,1)} %get-tuple-element.56), channel_id=1, source_target_pairs={{0,3},{1,2},{2,1},{3,0},{4,7},{5,6},{6,5},{7,4}} | collective-permute-start | bytes 786440 | tf_op jit(solution)/shard_map/ppermute | solution.py:221
  426.1 85.1 %collective-permute-start.17 = (bf16[4,256,128]{2,1,0:T(8,128)(2,1)}, bf16[4,256,128]{2,1,0:T(8,128)(2,1)S(1)}, u32[]{:S(2)}, u32[]{:S(2)}) collective-permute-start(bf16[4,256,128]{2,1,0:T(8,128)(2,1)} %get-tuple-element.55), channel_id=1, source_target_pairs={{0,5},{1,4},{2,7},{3,6},{4,1},{5,0},{6,3},{7,2}} | collective-permute-start | bytes 786440 | tf_op jit(solution)/shard_map/ppermute | solution.py:221
  426.4 84.8 %collective-permute-start.18 = (bf16[4,256,128]{2,1,0:T(8,128)(2,1)}, bf16[4,256,128]{2,1,0:T(8,128)(2,1)S(1)}, u32[]{:S(2)}, u32[]{:S(2)}) collective-permute-start(bf16[4,256,128]{2,1,0:T(8,128)(2,1)} %get-tuple-element.54), channel_id=1, source_target_pairs={{0,6},{1,7},{2,4},{3,5},{4,2},{5,3},{6,0},{7,1}} | collective-permute-start | bytes 786440 | tf_op jit(solution)/shard_map/ppermute | solution.py:221
  429.2 82.0 %collective-permute-start.19 = (bf16[4,256,128]{2,1,0:T(8,128)(2,1)}, bf16[4,256,128]{2,1,0:T(8,128)(2,1)}, u32[]{:S(2)}, u32[]{:S(2)}) collective-permute-start(bf16[4,256,128]{2,1,0:T(8,128)(2,1)} %get-tuple-element.53), channel_id=1, source_target_pairs={{0,7},{1,6},{2,5},{3,4},{4,3},{5,2},{6,1},{7,0}} | collective-permute-start | bytes 786440 | tf_op jit(solution)/shard_map/ppermute | solution.py:221
  429.3 82.0 %collective-permute-start.20 = (bf16[4,256,128]{2,1,0:T(8,128)(2,1)}, bf16[4,256,128]{2,1,0:T(8,128)(2,1)}, u32[]{:S(2)}, u32[]{:S(2)}) collective-permute-start(bf16[4,256,128]{2,1,0:T(8,128)(2,1)} %get-tuple-element.52), channel_id=1, source_target_pairs={{0,1},{1,0},{2,3},{3,2},{4,5},{5,4},{6,7},{7,6}} | collective-permute-start | bytes 786440 | tf_op jit(solution)/shard_map/ppermute | solution.py:221
  511.2 0.7 copy-start.16
  511.2 0.8 copy-start.17
  511.2 0.8 copy-start.18

commit v5 on v4

--- a/solution.py
+++ b/solution.py
@@ -179,7 +179,7 @@
         out_ref[0, q_idx] = mixed_ref[at:at + step_rows, :].astype(out_ref.dtype)
 
 
-def attend_local(sent, k_blocks, v_blocks, block_ids, first_slots, row_block, n_steps):
+def attend_local(sent, k_blocks, v_blocks, block_ids, first_slots, n_steps):
     n_dev, num_sent, _, head_dim = sent.shape
     step_rows = first_slots.shape[1]
     num_slots = k_blocks.shape[2]
@@ -193,7 +193,7 @@
         grid_spec=pltpu.PrefetchScalarGridSpec(
             num_scalar_prefetch=1,
             grid=(n_dev,),
-            in_specs=[pl.BlockSpec((1, num_sent, step_rows, head_dim), lambda p, meta: (meta[p], 0, row_block, 0)), cache_spec, cache_spec],
+            in_specs=[pl.BlockSpec((1, num_sent, step_rows, head_dim), lambda p, meta: (meta[p], 0, 0, 0)), cache_spec, cache_spec],
             out_specs=pl.BlockSpec((1, num_q, step_rows, head_dim), lambda p, meta: (meta[p], 0, 0, 0)),
             scratch_shapes=[
                 pltpu.VMEM((step_rows * stride + 16, head_dim), jnp.float32),
@@ -202,6 +202,54 @@
         ),
         cost_estimate=pl.CostEstimate(flops=10**9, bytes_accessed=4 * n_dev * step_rows * num_slots * head_dim, transcendentals=0),
     )(jnp.concatenate([block_ids, first_slots.reshape(-1)]).astype(jnp.int32), sent, k_blocks, v_blocks)
+
+
+def attend_near_kernel(n_steps, score_scale, n_dev, first_row, num_rows, meta_ref, sent_ref, *refs):
+    k_srcs, v_srcs = refs[:n_dev], refs[n_dev:2 * n_dev]
+    out_ref, rows_ref, mixed_ref, k_buf, v_buf, copy_sems = refs[2 * n_dev:]
+    near_rows = k_buf.shape[1]
+    block_idx = pl.program_id(0)
+
+    @pl.when(block_idx == 0)
+    def _():
+        own = pl.ds(meta_ref[0] * num_rows + first_row, near_rows)
+        for rel_idx in range(n_dev):
+            for kind, (srcs, buf) in enumerate(((k_srcs, k_buf), (v_srcs, v_buf))):
+                src = srcs[rel_idx] if rel_idx else srcs[0].at[own]
+                pltpu.make_async_copy(src, buf.at[rel_idx], copy_sems.at[kind, rel_idx]).start()
+
+    for kind, (srcs, buf) in enumerate(((k_srcs, k_buf), (v_srcs, v_buf))):
+        pltpu.make_async_copy(srcs[1], buf.at[block_idx], copy_sems.at[kind, block_idx]).wait()
+    block = pl.ds(block_idx, 1)
+    attend_kernel(n_steps, score_scale, meta_ref, sent_ref, k_buf.at[block], v_buf.at[block], out_ref, rows_ref, mixed_ref)
+
+
+def attend_near(sent, k_blocks, v_blocks, block_ids, my_slots, first_row, n_steps):
+    n_dev, num_sent, num_rows, head_dim = sent.shape
+    near_rows, num_slots = k_blocks[1].shape[:2]
+    num_q = num_sent - 2 * n_steps
+    pad_q = num_sent + n_steps
+    stride = num_sent + 1 - num_sent % 2
+    first_slots = jnp.broadcast_to(my_slots, (n_dev, near_rows)).reshape(-1)
+    return pl.pallas_call(
+        functools.partial(attend_near_kernel, n_steps, head_dim ** -0.5, n_dev, first_row, num_rows),
+        out_shape=jax.ShapeDtypeStruct((n_dev, num_q, near_rows, head_dim), sent.dtype),
+        grid_spec=pltpu.PrefetchScalarGridSpec(
+            num_scalar_prefetch=1,
+            grid=(n_dev,),
+            in_specs=[pl.BlockSpec((1, num_sent, near_rows, head_dim), lambda p, meta: (meta[p], 0, first_row // near_rows, 0))]
+            + [pl.BlockSpec(memory_space=pl.ANY)] * (2 * n_dev),
+            out_specs=pl.BlockSpec((1, num_q, near_rows, head_dim), lambda p, meta: (meta[p], 0, 0, 0)),
+            scratch_shapes=[
+                pltpu.VMEM((near_rows * stride + 16, head_dim), jnp.float32),
+                pltpu.VMEM((pad_q * (near_rows + 1) + 8, head_dim), jnp.float32),
+                pltpu.VMEM((n_dev, near_rows, num_slots, head_dim), sent.dtype),
+                pltpu.VMEM((n_dev, near_rows, num_slots, head_dim), sent.dtype),
+                pltpu.SemaphoreType.DMA((2, n_dev)),
+            ],
+        ),
+        cost_estimate=pl.CostEstimate(flops=10**9, bytes_accessed=4 * n_dev * near_rows * num_slots * head_dim, transcendentals=0),
+    )(jnp.concatenate([block_ids, first_slots]).astype(jnp.int32), sent, *k_blocks, *v_blocks)
 
 
 def solution(mesh):
@@ -238,13 +286,11 @@
         got = lax.all_to_all(sent[:, :, :far_rows], 'x', 0, 0, tiled=True)
         peers = jnp.arange(n_dev, dtype=jnp.int32)
         by_peer = (n_dev, num_rows, num_slots, head_dim)
-        mixed = attend_local(got, k_own.reshape(by_peer), v_own.reshape(by_peer), peers, start_pos.reshape(n_dev, num_rows)[:, :far_rows], 0, n_steps)
+        mixed = attend_local(got, k_own.reshape(by_peer), v_own.reshape(by_peer), peers, start_pos.reshape(n_dev, num_rows)[:, :far_rows], n_steps)
         v_got = lax.all_to_all(v_later.reshape(by_peer)[:, :far_rows], 'x', 0, 0, tiled=True)
         back = lax.all_to_all(mixed, 'x', 0, 0, tiled=True)
         head_ids = jnp.bitwise_xor(me, jnp.array((0,) + SWAP_ORDER, dtype=jnp.int32))
-        k_near, v_near_late, _ = lax.optimization_barrier((k_got[0], v_near, mixed))
-        near = [jnp.stack([lax.dynamic_slice_in_dim(own, me * num_rows + far_rows, near_rows)] + blocks) for own, blocks in ((k_later, k_near), (v_later, v_near_late))]
-        mixed_near = attend_local(sent, *near, head_ids, jnp.broadcast_to(my_pos[far_rows:], (n_dev, near_rows)), far_rows // near_rows, n_steps)
+        mixed_near = attend_near(sent, [k_own] + k_got[0], [v_own] + v_near, head_ids, my_pos[far_rows:], far_rows, n_steps)
         attended = jnp.concatenate([back, mixed_near], axis=2)
         attended = attended.reshape(n_dev, n_steps, group, num_rows, head_dim).transpose(1, 3, 0, 2, 4).reshape(n_steps, num_rows, n_dev * group, head_dim)
         out_hidden = finish(hidden_in, attended, w_o, mlp_norm, w_gate, w_up, w_down)

time: 517 us -> 509 us (0.985)
  local copies, waits for them, and re-layouts: 64.2 us -> 40.3 us
  waiting for transfers between devices: 114 us -> 128 us
    ppermute x28, waiting for transfers between devices: 100 us -> 128 us  [swap(): return lax.ppermute(arr, 'x', [(d, d ^ rel_idx) for d in range(n_dev)])]
    unnamed x66 -> x45, local copies, waits for them, and re-layouts: 26.8 us -> 3.61 us
    all_to_all x1, waiting for transfers between devices: 13.7 us -> 0.01 us  [local_run(): back = lax.all_to_all(mixed, 'x', 0, 0, tiled=True)]
    pallas_call x0 -> x1, Pallas kernels: none -> 10.1 us  [attend_near(): pl.pallas_call(functools.partial(attend_near_kernel, n_steps, head_dim **...]
    pallas_call x2 -> x1, Pallas kernels: 27.2 us -> 17.6 us  [attend_local(): pl.pallas_call(functools.partial(attend_kernel, n_steps, head_dim ** (-0....]
  transfers between devices with their start and end apart: 31 -> 31, of which waited for: 5 -> 7; matrix products, arithmetic and copies ran while one was open for 56% -> 46% of each run, Pallas kernels for 12% -> 12%
where the time goes in v5:
time: 509 us; the launch traced here: 508 us
  matrix products  225 us (44%)
  waiting for transfers between devices  128 us (25%)
  Pallas kernels  64.9 us (13%)
  local copies, waits for them, and re-layouts  40.3 us (8%)
  starting transfers between devices  37 us (7%)
  other arithmetic  11.7 us (2%)
    ppermute x28, waiting for transfers between devices, swap(): return lax.ppermute(arr, 'x', [(d, d ^ rel_idx) for d in range(n_dev)])  128 us
    dot_general x1, matrix products, finish(): jnp.einsum('sbd,df->sbf', normed, w_up, preferred_element_type=jnp.float32)  60.4 us
    dot_general x1, matrix products, finish(): jnp.einsum('sbd,df->sbf', normed, w_gate, preferred_element_type=jnp.floa...  60 us
    dot_general x1, matrix products, finish(): jnp.einsum('sbf,fd->sbd', activated, w_down, preferred_element_type=jnp.f...  58.2 us
    ppermute x28, starting transfers between devices, swap(): return lax.ppermute(arr, 'x', [(d, d ^ rel_idx) for d in range(n_dev)])  25.9 us
    pallas_call x4, Pallas kernels, merge_chunk(): pl.pallas_call(functools.partial(merge_chunk_kernel, row_base, n_dev), ou...  24.9 us
    dot_general x1, matrix products, finish(): jnp.einsum('sbe,ed->sbd', flat_attn, w_o, preferred_element_type=jnp.floa...  20.9 us
    dot_general x1, matrix products, project(): jnp.einsum('sbd,de->sbe', normed, w_q, preferred_element_type=jnp.float32)  18.1 us
  transfers between devices with their start and end apart: 31, of which 7 were waited for; matrix products, arithmetic and copies ran while one was open for 46% of the time, Pallas kernels for 12%

profile of v5, /device:TPU:0, one launch (start us, length us, event | category | flops | bytes accessed | tf_op | source)
XLA Modules:
  0.0 507.9 jit_solution(16937782432515158024)
XLA Ops:
  0.7 0.7 convert_element_type.54
  1.3 0.7 convert_element_type.56
  2.0 0.8 dynamic_slice.101
  2.7 1.7 fusion.47
  4.4 0.7 convert_element_type.52
  5.1 6.1 %fusion.58 = bf16[4,32,1024]{2,1,0:T(8,128)(2,1)S(1)} fusion(bf16[5120,1024]{1,0:T(8,128)(2,1)} %param.23, bf16[4,32,5120]{2,1,0:T(8,128)(2,1)} %param.17, f32[5120]{0:T(1024)S(1)} %convert_element_type.52, f32[4,32]{1,0:T(4,128)S(1)} %add_rsqrt_fusion.3), kind=kOutput, calls=%fused_computation.48 | convolution fusion | flops 1344929792 | bytes 12079616 | tf_op jit(solution)/shard_map/sbd,de->sbe/dot_general | solution.py:39
  11.3 0.7 copy-done.6
  12.0 0.7 copy.34
  13.0 1.6 fusion.20
  15.9 0.8 copy.33
  16.6 18.1 %fusion.8 = f32[4,32,5120]{2,1,0:T(8,128)S(1)} fusion(bf16[5120,5120]{1,0:T(8,128)(2,1)} %param.21, bf16[4,32,5120]{2,1,0:T(8,128)(2,1)S(1)} %copy-done, f32[5120]{0:T(1024)S(1)} %convert_element_type.52, f32[4,32]{1,0:T(4,128)S(1)} %add_rsqrt_fusion.3), kind=kOutput, calls=%fused_computation.8 | convolution fusion | flops 6713507840 | bytes 56381952 | tf_op jit(solution)/shard_map/sbd,de->sbe/dot_general | solution.py:37
  35.3 1.0 copy-done.1
  36.3 0.7 fusion.50
  37.2 2.2 fusion.51
  39.3 0.9 subtract_convert_fusion
  40.3 0.7 maximum_bitcast_fusion
  41.6 1.5 slice.29
  43.2 4.3 all-to-all-start
  47.5 3.9 constant_dynamic-slice_fusion.14
  51.3 0.5 collective-permute-start.13
  51.9 2.8 collective-permute-start.12
  54.7 3.9 dynamic-slice_bitcast_fusion
  58.9 1.4 collective-permute-start.3
  60.5 1.4 collective-permute-start.2
  62.0 15.0 %collective-permute-done.12.refs_14_.refs_6_ = bf16[8,256,128]{2,1,0:T(8,128)(2,1)S(1)} collective-permute-done((bf16[8,256,128]{2,1,0:T(8,128)(2,1)}, bf16[8,256,128]{2,1,0:T(8,128)(2,1)S(1)}, u32[]{:S(2)}, u32[]{:S(2)}) %collective-permute-start.12) | collective-permute-done | bytes 524320 | tf_op jit(solution)/shard_map/ppermute | solution.py:269
  77.0 0.6 collective-permute-start.1
  77.6 1.0 collective-permute-start
  78.6 11.1 %collective-permute-done.4.refs_5_ = bf16[8,256,128]{2,1,0:T(8,128)(2,1)} collective-permute-done((bf16[8,256,128]{2,1,0:T(8,128)(2,1)}, bf16[8,256,128]{2,1,0:T(8,128)(2,1)}, u32[]{:S(2)}, u32[]{:S(2)}) %collective-permute-start.4) | collective-permute-done | bytes 524320 | tf_op jit(solution)/shard_map/ppermute | solution.py:269
  89.7 0.6 pad_add_fusion.meta_ref
  90.4 17.6 %shard_map.175 = bf16[8,20,24,128]{3,2,1,0:T(8,128)(2,1)} custom-call(s32[200]{0:T(256)} %pad_add_fusion.meta_ref, bf16[8,28,24,128]{3,2,1,0:T(8,128)(2,1)} %all-to-all-done.sent_ref, bf16[8,32,256,128]{3,2,1,0:T(8,128)(2,1)} %bitcast.117, bf16[8,32,256,128]{3,2,1,0:T(8,128)(2,1)} %bitcast.125), custom_call_target="tpu_custom_call" | custom-call | flops 1000000000 | bytes 25165824 | tf_op jit(solution)/shard_map/pallas_call | solution.py:190
  108.0 2.7 all-to-all-start.1
  110.8 0.6 pad_add_fusion.1.meta_ref
  111.4 2.9 collective-permute-start.11
  114.7 2.0 collective-permute-start.8
  116.7 5.4 %collective-permute-done.5.refs_6_ = bf16[8,256,128]{2,1,0:T(8,128)(2,1)} collective-permute-done((bf16[8,256,128]{2,1,0:T(8,128)(2,1)}, bf16[8,256,128]{2,1,0:T(8,128)(2,1)}, u32[]{:S(2)}, u32[]{:S(2)}) %collective-permute-start.5) | collective-permute-done | bytes 524320 | tf_op jit(solution)/shard_map/ppermute | solution.py:269
  122.1 0.6 collective-permute-start.7
  122.7 0.6 pad_add_fusion.2.meta_ref
  123.3 11.6 %slice.36 = bf16[8,24,256,128]{3,2,1,0:T(8,128)(2,1)} slice(bf16[8,32,256,128]{3,2,1,0:T(8,128)(2,1)} %bitcast.126), slice={[0:8], [0:24], [0:256], [0:128]} | slice | bytes 25165824 | tf_op jit(solution)/shard_map/slice | solution.py:290
  134.9 2.7 constant_dynamic-slice_fusion.7
  137.6 7.3 %constant_dynamic-slice_fusion = (bf16[20,256,128]{2,1,0:T(8,128)(2,1)}, bf16[20,256,128]{2,1,0:T(8,128)(2,1)}, bf16[20,256,128]{2,1,0:T(8,128)(2,1)}, bf16[20,2...) fusion(bf16[256,256,128]{2,1,0:T(8,128)(2,1)} %bitcast.119, ...), kind=kLoop, calls=%fused_computation.67 | loop fusion | bytes 18350108 | tf_op jit(solution)/shard_map/dynamic_slice | solution.py:272
  144.8 4.8 shard_map.179.refs_9_
  149.6 0.9 collective-permute-start.20
  150.5 5.0 collective-permute-done.10.refs_12_.refs_4_
  156.1 11.4 %collective-permute-done.8.refs_10_.refs_2_ = bf16[8,256,128]{2,1,0:T(8,128)(2,1)} collective-permute-done((bf16[8,256,128]{2,1,0:T(8,128)(2,1)}, bf16[8,256,128]{2,1,0:T(8,128)(2,1)}, u32[]{:S(2)}, u32[]{:S(2)}) %collective-permute-start.8) | collective-permute-done | bytes 524320 | tf_op jit(solution)/shard_map/ppermute | solution.py:269
  167.5 2.5 collective-permute-start.25
  170.1 4.8 shard_map.177.partial_ref
  174.8 10.1 %shard_map.176 = bf16[8,20,8,128]{3,2,1,0:T(8,128)(2,1)} custom-call(s32[72]{0:T(128)} %pad_add_fusion.2.meta_ref, bf16[8,28,32,128]{3,2,1,0:T(8,128)(2,1)} %copy-done.4, bf16[256,256,128]{2,1,0:T(8,128)(2,1)} %bitcast.121, bf16[8,256,128]{2,1,0:T(8,128)(2,1)} %collective-permute-done.refs_1_, bf16[8,256,128]{2,1,0:T(8,128)(2,1)} %collective-permute-done.1.refs_2_, ...), custom_call_target="tpu_custom_call" | custom-call | flops 1000000000 | bytes 8388608 | tf_op jit(solution)/shard_map/pallas_call | solution.py:234
  185.0 4.2 all-to-all-start.2
  189.4 0.7 copy.42
  190.1 2.3 reshape_reshape.3
  192.4 20.9 %multiply_reduce_fusion = (f32[4,32]{1,0:T(4,128)S(1)}, f32[4,32,5120]{2,1,0:T(8,128)}) fusion(bf16[4,32,5120]{2,1,0:T(8,128)(2,1)} %reshape_reshape.3, bf16[5120,5120]{1,0:T(8,128)(2,1)} %param.26, bf16[4,32,5120]{2,1,0:T(8,128)(2,1)S(1)} %copy-done), kind=kOutput, calls=%fused_computation.37 | convolution fusion | flops 6714818560 | bytes 57672192 | tf_op jit(solution)/shard_map/sbe,ed->sbd/dot_general | solution.py:48
  213.3 60.0 %fusion.4 = f32[4,32,17408]{2,1,0:T(8,128)} fusion(bf16[5120,17408]{1,0:T(8,128)(2,1)} %param.28, f32[4,32,5120]{2,1,0:T(8,128)} %get-tuple-element.52, f32[5120]{0:T(1024)S(1)} %convert_element_type.61, f32[4,32]{1,0:T(4,128)S(1)} %add_rsqrt_fusion.2), kind=kOutput, calls=%fused_computation.4 | convolution fusion | flops 22818979840 | bytes 189813248 | tf_op jit(solution)/shard_map/sbd,df->sbf/dot_general | solution.py:51
  273.2 1.6 collective-permute-start.24
  274.9 1.5 collective-permute-start.23
  276.3 0.5 collective-permute-start.22
  277.0 60.4 %fusion.13.clone.8 = bf16[4,32,17408]{2,1,0:T(8,128)(2,1)} fusion(bf16[5120,17408]{1,0:T(8,128)(2,1)} %param.29, f32[4,32,17408]{2,1,0:T(8,128)} %fusion.4, f32[4,32,5120]{2,1,0:T(8,128)S(1)} %copy-done.2, f32[5120]{0:T(1024)S(1)} %convert_element_type.61, f32[4,32]{1,0:T(4,128)S(1)} %add_rsqrt_fusion.2), kind=kOutput, calls=%fused_computation.11.clone.clone.clone.clone.clone.clone.clone.1 | convolution fusion | flops 22832349184 | bytes 194269696 | tf_op jit(solution)/shard_map/sbd,df->sbf/dot_general | solution.py:52
  337.5 2.8 collective-permute-start.18
  340.3 51.4 %collective-permute-done.24.refs_4_ = bf16[20,256,128]{2,1,0:T(8,128)(2,1)} collective-permute-done((bf16[20,256,128]{2,1,0:T(8,128)(2,1)}, bf16[20,256,128]{2,1,0:T(8,128)(2,1)}, u32[]{:S(2)}, u32[]{:S(2)}) %collective-permute-start.24) | collective-permute-done | bytes 1310752 | tf_op jit(solution)/shard_map/ppermute | solution.py:269
  392.4 28.1 %collective-permute-done.22.refs_2_ = bf16[20,256,128]{2,1,0:T(8,128)(2,1)} collective-permute-done((bf16[20,256,128]{2,1,0:T(8,128)(2,1)}, bf16[20,256,128]{2,1,0:T(8,128)(2,1)}, u32[]{:S(2)}, u32[]{:S(2)}) %collective-permute-start.22) | collective-permute-done | bytes 1310752 | tf_op jit(solution)/shard_map/ppermute | solution.py:269
  421.2 58.2 %fusion.41 = bf16[4,32,5120]{2,1,0:T(8,128)(2,1)} fusion(f32[4,32,5120]{2,1,0:T(8,128)S(1)} %copy-done.2, bf16[17408,5120]{1,0:T(8,128)(2,1)} %param.30, bf16[4,32,17408]{2,1,0:T(8,128)(2,1)} %fusion.13.clone.8), kind=kOutput, calls=%fused_computation.25 | convolution fusion | flops 22818324480 | bytes 186646528 | tf_op jit(solution)/shard_map/sbf,fd->sbd/dot_general | solution.py:54
  479.4 11.3 %shard_map.180.refs_9_ = bf16[32,256,8,128]{3,2,1,0:T(8,128)(2,1)} custom-call(s32[40]{0:T(128)} %pad_add_fusion.1.meta_ref, bf16[256,256,128]{2,1,0:T(8,128)(2,1)} %bitcast.122, bf16[20,256,128]{2,1,0:T(8,128)(2,1)} %collective-permute-done.21.refs_1_, bf16[20,256,128]{2,1,0:T(8,128)(2,1)} %collective-permute-done.22.refs_2_, ...), custom_call_target="tpu_custom_call", output_to_operand_aliasing={{}: (10, {})} | custom-call | flops 100000000 | bytes 20971520 | tf_op jit(solution)/shard_map/pallas_call | solution.py:102
  490.7 12.3 %shard_map.178 = bf16[32,256,8,128]{3,2,1,0:T(8,128)(2,1)} custom-call(s32[40]{0:T(128)} %pad_add_fusion.1.meta_ref, bf16[8,24,256,128]{3,2,1,0:T(8,128)(2,1)} %all-to-all-done.2.blocks_ref, bf16[4,32,8,128]{3,2,1,0:T(8,128)(2,1)} %bitcast.141, bf16[32,256,8,128]{3,2,1,0:T(8,128)(2,1)} %shard_map.177.partial_ref), custom_call_target="tpu_custom_call", output_to_operand_aliasing={{}: (3, {})} | custom-call | flops 100000000 | bytes 25165824 | tf_op jit(solution)/shard_map/pallas_call | solution.py:124
  503.0 0.6 copy-done.15
  503.8 4.0 shard_map.181
  (103 shorter events, 6.4 us)
Async XLA Ops:
  5.1 7.6 %copy-start = (bf16[4,32,5120]{2,1,0:T(8,128)(2,1)S(1)}, bf16[4,32,5120]{2,1,0:T(8,128)(2,1)}, u32[]{:S(2)}) copy-start(bf16[4,32,5120]{2,1,0:T(8,128)(2,1)} %param.17) | copy-start | bytes 3932164
  5.1 7.9 %copy-start.3 = (bf16[5120,1024]{1,0:T(8,128)(2,1)S(1)}, bf16[5120,1024]{1,0:T(8,128)(2,1)}, u32[]{:S(2)}) copy-start(bf16[5120,1024]{1,0:T(8,128)(2,1)} %param.22) | copy-start | bytes 31457284
  11.3 0.7 copy-start.6
  15.9 18.9 %copy-start.5 = (bf16[4,32,8,128]{3,2,1,0:T(8,128)(2,1)}, bf16[4,32,8,128]{3,2,1,0:T(8,128)(2,1)S(1)}, u32[]{:S(2)}) copy-start(bf16[4,32,8,128]{3,2,1,0:T(8,128)(2,1)S(1)} %pad_maximum_fusion.2.refs_8_) | copy-start | bytes 786436
  34.8 1.5 copy-start.1
  40.3 1.1 copy-start.13
  40.3 1.1 copy-start.14
  41.6 1.6 copy-start.4
  43.2 47.1 %all-to-all-start = ((bf16[8,28,24,128]{3,2,1,0:T(8,128)(2,1)}), bf16[8,28,24,128]{3,2,1,0:T(8,128)(2,1)}, u32[]{:S(2)}, u32[]{:S(2)}) async-start(bf16[8,28,24,128]{3,2,1,0:T(8,128)(2,1)} %slice.29), calls=%async_computation | async-start | bytes 2752512 | tf_op jit(solution)/shard_map/all_to_all | solution.py:286
  51.3 9.2 %collective-permute-start.13 = (bf16[8,256,128]{2,1,0:T(8,128)(2,1)}, bf16[8,256,128]{2,1,0:T(8,128)(2,1)S(1)}, u32[]{:S(2)}, u32[]{:S(2)}) collective-permute-start(bf16[8,256,128]{2,1,0:T(8,128)(2,1)} %get-tuple-element.31), channel_id=1, source_target_pairs={{0,1},{1,0},{2,3},{3,2},{4,5},{5,4},{6,7},{7,6}} | collective-permute-start | bytes 1572872 | tf_op jit(solution)/shard_map/ppermute | solution.py:269
  51.8 8.5 %copy-start.19 = (s32[256]{0:T(256)S(1)}, s32[256]{0:T(256)}, u32[]{:S(2)}) copy-start(s32[256]{0:T(256)} %param.16) | copy-start | bytes 3076
  51.9 25.1 %collective-permute-start.12 = (bf16[8,256,128]{2,1,0:T(8,128)(2,1)}, bf16[8,256,128]{2,1,0:T(8,128)(2,1)S(1)}, u32[]{:S(2)}, u32[]{:S(2)}) collective-permute-start(bf16[8,256,128]{2,1,0:T(8,128)(2,1)} %get-tuple-element.32), channel_id=1, source_target_pairs={{0,7},{1,6},{2,5},{3,4},{4,3},{5,2},{6,1},{7,0}} | collective-permute-start | bytes 1572872 | tf_op jit(solution)/shard_map/ppermute | solution.py:269
  58.5 19.1 %collective-permute-start.6 = (bf16[8,256,128]{2,1,0:T(8,128)(2,1)}, bf16[8,256,128]{2,1,0:T(8,128)(2,1)S(1)}, u32[]{:S(2)}, u32[]{:S(2)}) collective-permute-start(bf16[8,256,128]{2,1,0:T(8,128)(2,1)} %get-tuple-element.38), channel_id=1, source_target_pairs={{0,1},{1,0},{2,3},{3,2},{4,5},{5,4},{6,7},{7,6}} | collective-permute-start | bytes 1572872 | tf_op jit(solution)/shard_map/ppermute | solution.py:269
  58.6 31.2 %collective-permute-start.4 = (bf16[8,256,128]{2,1,0:T(8,128)(2,1)}, bf16[8,256,128]{2,1,0:T(8,128)(2,1)}, u32[]{:S(2)}, u32[]{:S(2)}) collective-permute-start(bf16[8,256,128]{2,1,0:T(8,128)(2,1)} %get-tuple-element.39), channel_id=1, source_target_pairs={{0,6},{1,7},{2,4},{3,5},{4,2},{5,3},{6,0},{7,1}} | collective-permute-start | bytes 1572872 | tf_op jit(solution)/shard_map/ppermute | solution.py:269
  58.9 52.5 %collective-permute-start.3 = (bf16[8,256,128]{2,1,0:T(8,128)(2,1)}, bf16[8,256,128]{2,1,0:T(8,128)(2,1)}, u32[]{:S(2)}, u32[]{:S(2)}) collective-permute-start(bf16[8,256,128]{2,1,0:T(8,128)(2,1)} %get-tuple-element.40), channel_id=1, source_target_pairs={{0,5},{1,4},{2,7},{3,6},{4,1},{5,0},{6,3},{7,2}} | collective-permute-start | bytes 1572872 | tf_op jit(solution)/shard_map/ppermute | solution.py:269
  60.5 47.5 %copy-start.7 = (bf16[8,256,128]{2,1,0:T(8,128)(2,1)}, bf16[8,256,128]{2,1,0:T(8,128)(2,1)S(1)}, u32[]{:S(2)}) copy-start(bf16[8,256,128]{2,1,0:T(8,128)(2,1)S(1)} %collective-permute-done.13.refs_15_.refs_7_) | copy-start | bytes 1572868
  60.5 53.8 %collective-permute-start.2 = (bf16[8,256,128]{2,1,0:T(8,128)(2,1)}, bf16[8,256,128]{2,1,0:T(8,128)(2,1)}, u32[]{:S(2)}, u32[]{:S(2)}) collective-permute-start(bf16[8,256,128]{2,1,0:T(8,128)(2,1)} %get-tuple-element.41), channel_id=1, source_target_pairs={{0,3},{1,2},{2,1},{3,0},{4,7},{5,6},{6,5},{7,4}} | collective-permute-start | bytes 1572872 | tf_op jit(solution)/shard_map/ppermute | solution.py:269
  77.0 31.0 %copy-start.8 = (bf16[8,256,128]{2,1,0:T(8,128)(2,1)}, bf16[8,256,128]{2,1,0:T(8,128)(2,1)S(1)}, u32[]{:S(2)}) copy-start(bf16[8,256,128]{2,1,0:T(8,128)(2,1)S(1)} %collective-permute-done.12.refs_14_.refs_6_) | copy-start | bytes 1572868
  77.0 37.4 %collective-permute-start.1 = (bf16[8,256,128]{2,1,0:T(8,128)(2,1)}, bf16[8,256,128]{2,1,0:T(8,128)(2,1)}, u32[]{:S(2)}, u32[]{:S(2)}) collective-permute-start(bf16[8,256,128]{2,1,0:T(8,128)(2,1)} %get-tuple-element.42), channel_id=1, source_target_pairs={{0,4},{1,5},{2,6},{3,7},{4,0},{5,1},{6,2},{7,3}} | collective-permute-start | bytes 1572872 | tf_op jit(solution)/shard_map/ppermute | solution.py:269
  77.6 30.4 %copy-start.9 = (bf16[8,256,128]{2,1,0:T(8,128)(2,1)}, bf16[8,256,128]{2,1,0:T(8,128)(2,1)S(1)}, u32[]{:S(2)}) copy-start(bf16[8,256,128]{2,1,0:T(8,128)(2,1)S(1)} %collective-permute-done.6.refs_7_) | copy-start | bytes 1572868
  77.6 37.0 %collective-permute-start = (bf16[8,256,128]{2,1,0:T(8,128)(2,1)}, bf16[8,256,128]{2,1,0:T(8,128)(2,1)}, u32[]{:S(2)}, u32[]{:S(2)}) collective-permute-start(bf16[8,256,128]{2,1,0:T(8,128)(2,1)} %get-tuple-element.43), channel_id=1, source_target_pairs={{0,2},{1,3},{2,0},{3,1},{4,6},{5,7},{6,4},{7,5}} | collective-permute-start | bytes 1572872 | tf_op jit(solution)/shard_map/ppermute | solution.py:269
  89.7 32.4 %collective-permute-start.5 = (bf16[8,256,128]{2,1,0:T(8,128)(2,1)}, bf16[8,256,128]{2,1,0:T(8,128)(2,1)}, u32[]{:S(2)}, u32[]{:S(2)}) collective-permute-start(bf16[8,256,128]{2,1,0:T(8,128)(2,1)} %get-tuple-element.44), channel_id=1, source_target_pairs={{0,7},{1,6},{2,5},{3,4},{4,3},{5,2},{6,1},{7,0}} | collective-permute-start | bytes 1572872 | tf_op jit(solution)/shard_map/ppermute | solution.py:269
  90.4 20.3 %copy-start.20 = (s32[8]{0:T(128)S(1)}, s32[8]{0:T(128)}, u32[]{:S(2)}) copy-start(s32[8]{0:T(128)} %constant.78.clone) | copy-start | bytes 100
  90.4 33.0 %copy-start.18 = (bf16[5120]{0:T(1024)(128)(2,1)S(1)}, bf16[5120]{0:T(1024)(128)(2,1)}, u32[]{:S(2)}) copy-start(bf16[5120]{0:T(1024)(128)(2,1)} %param.27) | copy-start | bytes 30724
  108.0 77.0 %all-to-all-start.1 = ((bf16[8,20,24,128]{3,2,1,0:T(8,128)(2,1)}), bf16[8,20,24,128]{3,2,1,0:T(8,128)(2,1)S(1)}, u32[]{:S(2)}, u32[]{:S(2)}) async-start(bf16[8,20,24,128]{3,2,1,0:T(8,128)(2,1)} %shard_map.175), calls=%async_computation.1 | async-start | bytes 1966080 | tf_op jit(solution)/shard_map/all_to_all | solution.py:291
  111.4 38.2 %collective-permute-start.11 = (bf16[8,256,128]{2,1,0:T(8,128)(2,1)}, bf16[8,256,128]{2,1,0:T(8,128)(2,1)S(1)}, u32[]{:S(2)}, u32[]{:S(2)}) collective-permute-start(bf16[8,256,128]{2,1,0:T(8,128)(2,1)} %get-tuple-element.33), channel_id=1, source_target_pairs={{0,6},{1,7},{2,4},{3,5},{4,2},{5,3},{6,0},{7,1}} | collective-permute-start | bytes 1572872 | tf_op jit(solution)/shard_map/ppermute | solution.py:269
  114.3 41.2 %collective-permute-start.10 = (bf16[8,256,128]{2,1,0:T(8,128)(2,1)}, bf16[8,256,128]{2,1,0:T(8,128)(2,1)S(1)}, u32[]{:S(2)}, u32[]{:S(2)}) collective-permute-start(bf16[8,256,128]{2,1,0:T(8,128)(2,1)} %get-tuple-element.34), channel_id=1, source_target_pairs={{0,5},{1,4},{2,7},{3,6},{4,1},{5,0},{6,3},{7,2}} | collective-permute-start | bytes 1572872 | tf_op jit(solution)/shard_map/ppermute | solution.py:269
  114.4 41.4 %collective-permute-start.9 = (bf16[8,256,128]{2,1,0:T(8,128)(2,1)}, bf16[8,256,128]{2,1,0:T(8,128)(2,1)}, u32[]{:S(2)}, u32[]{:S(2)}) collective-permute-start(bf16[8,256,128]{2,1,0:T(8,128)(2,1)} %get-tuple-element.35), channel_id=1, source_target_pairs={{0,3},{1,2},{2,1},{3,0},{4,7},{5,6},{6,5},{7,4}} | collective-permute-start | bytes 1572872 | tf_op jit(solution)/shard_map/ppermute | solution.py:269
  114.7 52.9 %collective-permute-start.8 = (bf16[8,256,128]{2,1,0:T(8,128)(2,1)}, bf16[8,256,128]{2,1,0:T(8,128)(2,1)}, u32[]{:S(2)}, u32[]{:S(2)}) collective-permute-start(bf16[8,256,128]{2,1,0:T(8,128)(2,1)} %get-tuple-element.36), channel_id=1, source_target_pairs={{0,4},{1,5},{2,6},{3,7},{4,0},{5,1},{6,2},{7,3}} | collective-permute-start | bytes 1572872 | tf_op jit(solution)/shard_map/ppermute | solution.py:269
  122.1 45.4 %collective-permute-start.7 = (bf16[8,256,128]{2,1,0:T(8,128)(2,1)}, bf16[8,256,128]{2,1,0:T(8,128)(2,1)}, u32[]{:S(2)}, u32[]{:S(2)}) collective-permute-start(bf16[8,256,128]{2,1,0:T(8,128)(2,1)} %get-tuple-element.37), channel_id=1, source_target_pairs={{0,2},{1,3},{2,0},{3,1},{4,6},{5,7},{6,4},{7,5}} | collective-permute-start | bytes 1572872 | tf_op jit(solution)/shard_map/ppermute | solution.py:269
  149.6 20.4 %copy-start.10 = (bf16[8,256,128]{2,1,0:T(8,128)(2,1)}, bf16[8,256,128]{2,1,0:T(8,128)(2,1)S(1)}, u32[]{:S(2)}) copy-start(bf16[8,256,128]{2,1,0:T(8,128)(2,1)S(1)} %collective-permute-done.11.refs_13_.refs_5_) | copy-start | bytes 1572868
  149.6 123.6 %collective-permute-start.20 = (bf16[4,256,128]{2,1,0:T(8,128)(2,1)}, bf16[4,256,128]{2,1,0:T(8,128)(2,1)}, u32[]{:S(2)}, u32[]{:S(2)}) collective-permute-start(bf16[4,256,128]{2,1,0:T(8,128)(2,1)} %get-tuple-element.24), channel_id=1, source_target_pairs={{0,1},{1,0},{2,3},{3,2},{4,5},{5,4},{6,7},{7,6}} | collective-permute-start | bytes 786440 | tf_op jit(solution)/shard_map/ppermute | solution.py:269
  155.5 14.5 %copy-start.11 = (bf16[8,256,128]{2,1,0:T(8,128)(2,1)}, bf16[8,256,128]{2,1,0:T(8,128)(2,1)S(1)}, u32[]{:S(2)}) copy-start(bf16[8,256,128]{2,1,0:T(8,128)(2,1)S(1)} %collective-permute-done.10.refs_12_.refs_4_) | copy-start | bytes 1572868
  155.5 119.3 %collective-permute-start.19 = (bf16[4,256,128]{2,1,0:T(8,128)(2,1)}, bf16[4,256,128]{2,1,0:T(8,128)(2,1)}, u32[]{:S(2)}, u32[]{:S(2)}) collective-permute-start(bf16[4,256,128]{2,1,0:T(8,128)(2,1)} %get-tuple-element.25), channel_id=1, source_target_pairs={{0,7},{1,6},{2,5},{3,4},{4,3},{5,2},{6,1},{7,0}} | collective-permute-start | bytes 786440 | tf_op jit(solution)/shard_map/ppermute | solution.py:269
  155.7 120.6 %collective-permute-start.27 = (bf16[20,256,128]{2,1,0:T(8,128)(2,1)}, bf16[20,256,128]{2,1,0:T(8,128)(2,1)}, u32[]{:S(2)}, u32[]{:S(2)}) collective-permute-start(bf16[20,256,128]{2,1,0:T(8,128)(2,1)} %get-tuple-element.17), channel_id=1, source_target_pairs={{0,1},{1,0},{2,3},{3,2},{4,5},{5,4},{6,7},{7,6}} | collective-permute-start | bytes 3932168 | tf_op jit(solution)/shard_map/ppermute | solution.py:269
  167.5 109.4 %collective-permute-start.26 = (bf16[20,256,128]{2,1,0:T(8,128)(2,1)}, bf16[20,256,128]{2,1,0:T(8,128)(2,1)}, u32[]{:S(2)}, u32[]{:S(2)}) collective-permute-start(bf16[20,256,128]{2,1,0:T(8,128)(2,1)} %get-tuple-element.18), channel_id=1, source_target_pairs={{0,7},{1,6},{2,5},{3,4},{4,3},{5,2},{6,1},{7,0}} | collective-permute-start | bytes 3932168 | tf_op jit(solution)/shard_map/ppermute | solution.py:269
  167.5 169.9 %collective-permute-start.25 = (bf16[20,256,128]{2,1,0:T(8,128)(2,1)}, bf16[20,256,128]{2,1,0:T(8,128)(2,1)}, u32[]{:S(2)}, u32[]{:S(2)}) collective-permute-start(bf16[20,256,128]{2,1,0:T(8,128)(2,1)} %get-tuple-element.19), channel_id=1, source_target_pairs={{0,6},{1,7},{2,4},{3,5},{4,2},{5,3},{6,0},{7,1}} | collective-permute-start | bytes 3932168 | tf_op jit(solution)/shard_map/ppermute | solution.py:269
  184.9 4.2 copy-start.12
  185.0 305.7 %all-to-all-start.2 = ((bf16[8,24,256,128]{3,2,1,0:T(8,128)(2,1)}), bf16[8,24,256,128]{3,2,1,0:T(8,128)(2,1)}, u32[]{:S(2)}, u32[]{:S(2)}) async-start(bf16[8,24,256,128]{3,2,1,0:T(8,128)(2,1)} %slice.36), calls=%async_computation.2 | async-start | bytes 25165824 | tf_op jit(solution)/shard_map/all_to_all | solution.py:290
  213.3 63.7 %copy-start.2 = (f32[4,32,5120]{2,1,0:T(8,128)S(1)}, f32[4,32,5120]{2,1,0:T(8,128)}, u32[]{:S(2)}) copy-start(f32[4,32,5120]{2,1,0:T(8,128)} %get-tuple-element.52) | copy-start | bytes 7864324
  273.2 118.5 %collective-permute-start.24 = (bf16[20,256,128]{2,1,0:T(8,128)(2,1)}, bf16[20,256,128]{2,1,0:T(8,128)(2,1)}, u32[]{:S(2)}, u32[]{:S(2)}) collective-permute-start(bf16[20,256,128]{2,1,0:T(8,128)(2,1)} %get-tuple-element.20), channel_id=1, source_target_pairs={{0,5},{1,4},{2,7},{3,6},{4,1},{5,0},{6,3},{7,2}} | collective-permute-start | bytes 3932168 | tf_op jit(solution)/shard_map/ppermute | solution.py:269
  274.9 117.2 %collective-permute-start.23 = (bf16[20,256,128]{2,1,0:T(8,128)(2,1)}, bf16[20,256,128]{2,1,0:T(8,128)(2,1)}, u32[]{:S(2)}, u32[]{:S(2)}) collective-permute-start(bf16[20,256,128]{2,1,0:T(8,128)(2,1)} %get-tuple-element.21), channel_id=1, source_target_pairs={{0,3},{1,2},{2,1},{3,0},{4,7},{5,6},{6,5},{7,4}} | collective-permute-start | bytes 3932168 | tf_op jit(solution)/shard_map/ppermute | solution.py:269
  276.3 144.2 %collective-permute-start.22 = (bf16[20,256,128]{2,1,0:T(8,128)(2,1)}, bf16[20,256,128]{2,1,0:T(8,128)(2,1)}, u32[]{:S(2)}, u32[]{:S(2)}) collective-permute-start(bf16[20,256,128]{2,1,0:T(8,128)(2,1)} %get-tuple-element.22), channel_id=1, source_target_pairs={{0,4},{1,5},{2,6},{3,7},{4,0},{5,1},{6,2},{7,3}} | collective-permute-start | bytes 3932168 | tf_op jit(solution)/shard_map/ppermute | solution.py:269
  276.9 144.1 %collective-permute-start.21 = (bf16[20,256,128]{2,1,0:T(8,128)(2,1)}, bf16[20,256,128]{2,1,0:T(8,128)(2,1)}, u32[]{:S(2)}, u32[]{:S(2)}) collective-permute-start(bf16[20,256,128]{2,1,0:T(8,128)(2,1)} %get-tuple-element.23), channel_id=1, source_target_pairs={{0,2},{1,3},{2,0},{3,1},{4,6},{5,7},{6,4},{7,5}} | collective-permute-start | bytes 3932168 | tf_op jit(solution)/shard_map/ppermute | solution.py:269
  337.5 165.5 %collective-permute-start.18 = (bf16[4,256,128]{2,1,0:T(8,128)(2,1)}, bf16[4,256,128]{2,1,0:T(8,128)(2,1)S(1)}, u32[]{:S(2)}, u32[]{:S(2)}) collective-permute-start(bf16[4,256,128]{2,1,0:T(8,128)(2,1)} %get-tuple-element.26), channel_id=1, source_target_pairs={{0,6},{1,7},{2,4},{3,5},{4,2},{5,3},{6,0},{7,1}} | collective-permute-start | bytes 786440 | tf_op jit(solution)/shard_map/ppermute | solution.py:269
  391.7 111.2 %collective-permute-start.17 = (bf16[4,256,128]{2,1,0:T(8,128)(2,1)}, bf16[4,256,128]{2,1,0:T(8,128)(2,1)S(1)}, u32[]{:S(2)}, u32[]{:S(2)}) collective-permute-start(bf16[4,256,128]{2,1,0:T(8,128)(2,1)} %get-tuple-element.27), channel_id=1, source_target_pairs={{0,5},{1,4},{2,7},{3,6},{4,1},{5,0},{6,3},{7,2}} | collective-permute-start | bytes 786440 | tf_op jit(solution)/shard_map/ppermute | solution.py:269
  392.0 110.9 %collective-permute-start.16 = (bf16[4,256,128]{2,1,0:T(8,128)(2,1)}, bf16[4,256,128]{2,1,0:T(8,128)(2,1)S(1)}, u32[]{:S(2)}, u32[]{:S(2)}) collective-permute-start(bf16[4,256,128]{2,1,0:T(8,128)(2,1)} %get-tuple-element.28), channel_id=1, source_target_pairs={{0,3},{1,2},{2,1},{3,0},{4,7},{5,6},{6,5},{7,4}} | collective-permute-start | bytes 786440 | tf_op jit(solution)/shard_map/ppermute | solution.py:269
  420.5 82.4 %collective-permute-start.15 = (bf16[4,256,128]{2,1,0:T(8,128)(2,1)}, bf16[4,256,128]{2,1,0:T(8,128)(2,1)}, u32[]{:S(2)}, u32[]{:S(2)}) collective-permute-start(bf16[4,256,128]{2,1,0:T(8,128)(2,1)} %get-tuple-element.29), channel_id=1, source_target_pairs={{0,4},{1,5},{2,6},{3,7},{4,0},{5,1},{6,2},{7,3}} | collective-permute-start | bytes 786440 | tf_op jit(solution)/shard_map/ppermute | solution.py:269
  421.0 82.0 %collective-permute-start.14 = (bf16[4,256,128]{2,1,0:T(8,128)(2,1)}, bf16[4,256,128]{2,1,0:T(8,128)(2,1)}, u32[]{:S(2)}, u32[]{:S(2)}) collective-permute-start(bf16[4,256,128]{2,1,0:T(8,128)(2,1)} %get-tuple-element.30), channel_id=1, source_target_pairs={{0,2},{1,3},{2,0},{3,1},{4,6},{5,7},{6,4},{7,5}} | collective-permute-start | bytes 786440 | tf_op jit(solution)/shard_map/ppermute | solution.py:269
  503.0 0.7 copy-start.15
  503.0 0.8 copy-start.16
  503.0 0.9 copy-start.17
